TPU v7x, 8 devices: a whole 2x2x1 slice. The times are simulated.
8 devices in a mesh: tp: 4 (over z, y, x), cp: 2 (over core).
Axes of the slice: x: 2, y: 2, z: 1, core: 2. Of those that a mesh axis runs over, the one named last changes fastest.
Arguments:
- x_in: bfloat16 [6, 1536, 2560], P(None, 'cp')
- positions: int32 [1536], P('cp')
- rope_cos: float32 [1536, 256], P('cp')
- rope_sin: float32 [1536, 256], P('cp')
- norm_a: bfloat16 [2560], replicated
- wq_a: bfloat16 [2560, 2048], P(None, 'tp')
- wk_a: bfloat16 [2560, 1024], P(None, 'tp')
- wv_a: bfloat16 [2560, 1024], P(None, 'tp')
- wo_a: bfloat16 [2048, 2560], P('tp')
- norm_b: bfloat16 [2560], replicated
- wq_b: bfloat16 [2560, 2048], P(None, 'tp')
- wk_b: bfloat16 [2560, 1024], P(None, 'tp')
- wv_b: bfloat16 [2560, 1024], P(None, 'tp')
- wo_b: bfloat16 [2048, 2560], P('tp')
- grad_y: bfloat16 [6, 1536, 2560], P(None, 'cp')
Outputs:
- output 1: bfloat16 [6, 1536, 2560], P(None, 'cp')
- output 2: bfloat16 [6, 1536, 2560], P(None, 'cp')
- output 3: bfloat16 [2560], P('cp')
- output 4: bfloat16 [2560, 2048], P('cp', 'tp')
- output 5: bfloat16 [2560, 1024], P('cp', 'tp')
- output 6: bfloat16 [2560, 1024], P('cp', 'tp')
- output 7: bfloat16 [2048, 2560], P(('tp', 'cp'))
- output 8: bfloat16 [2560], P('cp')
- output 9: bfloat16 [2560, 2048], P('cp', 'tp')
- output 10: bfloat16 [2560, 1024], P('cp', 'tp')
- output 11: bfloat16 [2560, 1024], P('cp', 'tp')
- output 12: bfloat16 [2048, 2560], P(('tp', 'cp'))
All inputs are finite; a program needn't handle non-finite values.
Results may differ from a plain program's by a relative error of at most 0.02.
Values are sent between devices in bfloat16 or wider.
A program may use at most 1 GiB of HBM per device.

v0:
```python
import jax
import jax.numpy as jnp
from jax import lax
from jax.sharding import PartitionSpec as P

CHUNK = 8192
NORM_EPS = 1e-5
QK_EPS = 1e-6
TEMP_SCALE = 0.1
NEG_BIG = -1e30


def rms_norm(act, gamma):
    act_wide = act.astype(jnp.float32)
    inv_rms = lax.rsqrt(jnp.mean(act_wide * act_wide, axis=-1, keepdims=True) + NORM_EPS)
    return (act_wide * inv_rms * gamma.astype(jnp.float32)).astype(jnp.bfloat16)


def norm_backward(act, gamma, grad_out):
    act_wide = act.astype(jnp.float32)
    inv_rms = lax.rsqrt(jnp.mean(act_wide * act_wide, axis=-1, keepdims=True) + NORM_EPS)
    x_hat = act_wide * inv_rms
    grad_gain = jnp.sum(grad_out * x_hat, axis=(0, 1))
    grad_hat = grad_out * gamma.astype(jnp.float32)
    grad_act = inv_rms * (grad_hat - x_hat * jnp.mean(grad_hat * x_hat, axis=-1, keepdims=True))
    return grad_act, grad_gain


def rotate(wide, cos_tab, sin_tab):
    half = wide.shape[-1] // 2
    turned = jnp.concatenate([-wide[..., half:], wide[..., :half]], axis=-1)
    return wide * cos_tab[None, :, None, :] + turned * sin_tab[None, :, None, :]


def qk_prep(raw_val, cos_tab, sin_tab):
    wide = rotate(raw_val.astype(jnp.float32), cos_tab, sin_tab)
    return (wide * lax.rsqrt(jnp.mean(wide * wide, axis=-1, keepdims=True) + QK_EPS)).astype(jnp.bfloat16)


def value_a11(positions):
    return jnp.log(((positions + 1) // CHUNK).astype(jnp.float32) + 1.0) * TEMP_SCALE + 1.0


def project(act, weight):
    return jnp.einsum('bsd,dh->bsh', act, weight, preferred_element_type=jnp.float32).astype(jnp.bfloat16)


def project_back(grad_out, weight):
    return jnp.einsum('bsh,dh->bsd', grad_out, weight, preferred_element_type=jnp.float32)


def weight_grad(act, grad_out):
    return jnp.einsum('bsd,bsh->dh', act, grad_out, preferred_element_type=jnp.float32)


def attn_forward(queries, keys, values, allowed, scale):
    scores = jnp.einsum('bqkgd,bskd->bkgqs', queries, keys, preferred_element_type=jnp.float32) * scale
    attn_prob = jax.nn.softmax(jnp.where(allowed, scores, NEG_BIG), axis=-1)
    prob_half = attn_prob.astype(jnp.bfloat16)
    attn_out = jnp.einsum('bkgqs,bskd->bqkgd', prob_half, values, preferred_element_type=jnp.float32)
    return attn_out.astype(jnp.bfloat16), attn_prob, prob_half


def attn_backward(queries, keys, values, attn_prob, prob_half, grad_out, scale):
    grad_value = jnp.einsum('bkgqs,bqkgd->bskd', prob_half, grad_out, preferred_element_type=jnp.float32)
    grad_prob = jnp.einsum('bqkgd,bskd->bkgqs', grad_out, values, preferred_element_type=jnp.float32)
    row_dot = jnp.sum(attn_prob * grad_prob, axis=-1, keepdims=True)
    grad_score = (attn_prob * (grad_prob - row_dot) * scale).astype(jnp.bfloat16)
    grad_query = jnp.einsum('bkgqs,bskd->bqkgd', grad_score, keys, preferred_element_type=jnp.float32)
    grad_key = jnp.einsum('bkgqs,bqkgd->bskd', grad_score, queries, preferred_element_type=jnp.float32)
    return grad_query, grad_key, grad_value


def solution(mesh):
    cp_size = mesh.shape['cp']
    row_spec = P(None, 'cp', None)
    col_spec = P(None, 'tp')
    grid_spec = P('cp', 'tp')
    out_rows = P(('tp', 'cp'), None)
    in_specs = (row_spec, P('cp'), P('cp', None), P('cp', None),
                P(None), col_spec, col_spec, col_spec, P('tp', None),
                P(None), col_spec, col_spec, col_spec, P('tp', None), row_spec)
    out_specs = (row_spec, row_spec,
                 P('cp'), grid_spec, grid_spec, grid_spec, out_rows,
                 P('cp'), grid_spec, grid_spec, grid_spec, out_rows)

    def body(x_in, positions, rope_cos, rope_sin, norm_a, wq_a, wk_a, wv_a, wo_a,
             norm_b, wq_b, wk_b, wv_b, wo_b, grad_y):
        batch, block = x_in.shape[0], x_in.shape[1]
        head_dim = rope_cos.shape[1]
        q_local = wq_a.shape[1] // head_dim
        kv_local = wk_a.shape[1] // head_dim
        q_shape = (batch, block, kv_local, q_local // kv_local, head_dim)
        kv_shape = (batch, block, kv_local, head_dim)
        flat_shape = (batch, block, -1)
        scale = head_dim ** -0.5
        cp_rank = lax.axis_index('cp')
        n_back = min(cp_size - 1, (CHUNK + block - 2) // block)
        window = (n_back + 1) * block
        seq_len = block * cp_size

        def prep(raw_val):
            return qk_prep(raw_val, rope_cos, rope_sin)

        xn_a = rms_norm(x_in, norm_a)
        q_prepped, q_pull = jax.vjp(prep, project(xn_a, wq_a).reshape(batch, block, q_local, head_dim))
        query_a = q_prepped.reshape(q_shape)
        key_a, k_pull = jax.vjp(prep, project(xn_a, wk_a).reshape(kv_shape))
        value_a = project(xn_a, wv_a).reshape(kv_shape)
        key_parts = []
        value_parts = []
        for shift in range(n_back, 0, -1):
            fwd_perm = [(source, source + shift) for source in range(cp_size - shift)]
            key_parts.append(lax.ppermute(key_a, 'cp', fwd_perm))
            value_parts.append(lax.ppermute(value_a, 'cp', fwd_perm))
        key_win = jnp.concatenate(key_parts + [key_a], axis=1)
        value_win = jnp.concatenate(value_parts + [value_a], axis=1)
        offsets = jnp.arange(window) - n_back * block
        key_pos = positions[0] + offsets
        allowed_a = ((key_pos[None, :] <= positions[:, None])
                     & ((key_pos // CHUNK)[None, :] == (positions // CHUNK)[:, None])
                     & (cp_rank * block + offsets >= 0)[None, :])
        out_a, prob_a, half_a = attn_forward(query_a, key_win, value_win, allowed_a, scale)
        out_a = out_a.reshape(flat_shape)
        attn_a = lax.psum(project(out_a, wo_a), 'tp')
        h_mid = (x_in.astype(jnp.float32) + attn_a.astype(jnp.float32)).astype(jnp.bfloat16)

        xn_b = rms_norm(h_mid, norm_b)
        q_temp = value_a11(positions)[None, :, None]
        query_b = (project(xn_b, wq_b).astype(jnp.float32) * q_temp).astype(jnp.bfloat16).reshape(q_shape)
        key_b = project(xn_b, wk_b).reshape(kv_shape)
        value_b = project(xn_b, wv_b).reshape(kv_shape)
        key_all = lax.all_gather(key_b, 'cp', axis=1, tiled=True)
        value_all = lax.all_gather(value_b, 'cp', axis=1, tiled=True)
        allowed_b = jnp.arange(seq_len)[None, :] <= (cp_rank * block + jnp.arange(block))[:, None]
        out_b, prob_b, half_b = attn_forward(query_b, key_all, value_all, allowed_b, scale)
        out_b = out_b.reshape(flat_shape)
        attn_b = lax.psum(project(out_b, wo_b), 'tp')
        out_y = (h_mid.astype(jnp.float32) + attn_b.astype(jnp.float32)).astype(jnp.bfloat16)

        grad_wo_b = weight_grad(out_b, grad_y)
        grad_ob = project_back(grad_y, wo_b).astype(jnp.bfloat16).reshape(q_shape)
        grad_q_b, grad_k_all, grad_v_all = attn_backward(query_b, key_all, value_all, prob_b, half_b, grad_ob, scale)
        grad_k_b = lax.psum_scatter(grad_k_all.astype(jnp.bfloat16), 'cp', scatter_dimension=1, tiled=True).reshape(flat_shape)
        grad_v_b = lax.psum_scatter(grad_v_all.astype(jnp.bfloat16), 'cp', scatter_dimension=1, tiled=True).reshape(flat_shape)
        grad_q_b = (grad_q_b.reshape(flat_shape) * q_temp).astype(jnp.bfloat16)
        grad_wq_b = weight_grad(xn_b, grad_q_b)
        grad_wk_b = weight_grad(xn_b, grad_k_b)
        grad_wv_b = weight_grad(xn_b, grad_v_b)
        grad_xn_b = project_back(grad_q_b, wq_b) + project_back(grad_k_b, wk_b) + project_back(grad_v_b, wv_b)
        grad_xn_b = lax.psum(grad_xn_b.astype(jnp.bfloat16), 'tp')
        grad_h_norm, grad_norm_b = norm_backward(h_mid, norm_b, grad_xn_b.astype(jnp.float32))
        grad_h = (grad_y.astype(jnp.float32) + grad_h_norm).astype(jnp.bfloat16)

        grad_wo_a = weight_grad(out_a, grad_h)
        grad_oa = project_back(grad_h, wo_a).astype(jnp.bfloat16).reshape(q_shape)
        grad_q_a, grad_k_win, grad_v_win = attn_backward(query_a, key_win, value_win, prob_a, half_a, grad_oa, scale)
        grad_k_own = grad_k_win[:, n_back * block:]
        grad_v_own = grad_v_win[:, n_back * block:]
        send_k = grad_k_win[:, :n_back * block].astype(jnp.bfloat16)
        send_v = grad_v_win[:, :n_back * block].astype(jnp.bfloat16)
        for shift in range(1, n_back + 1):
            back_perm = [(source, source - shift) for source in range(shift, cp_size)]
            start_row = (n_back - shift) * block
            grad_k_own = grad_k_own + lax.ppermute(send_k[:, start_row:start_row + block], 'cp', back_perm).astype(jnp.float32)
            grad_v_own = grad_v_own + lax.ppermute(send_v[:, start_row:start_row + block], 'cp', back_perm).astype(jnp.float32)
        grad_q_raw = q_pull(grad_q_a.astype(jnp.bfloat16).reshape(batch, block, q_local, head_dim))[0].reshape(flat_shape)
        grad_k_raw = k_pull(grad_k_own.astype(jnp.bfloat16))[0].reshape(flat_shape)
        grad_v_raw = grad_v_own.astype(jnp.bfloat16).reshape(flat_shape)
        grad_wq_a = weight_grad(xn_a, grad_q_raw)
        grad_wk_a = weight_grad(xn_a, grad_k_raw)
        grad_wv_a = weight_grad(xn_a, grad_v_raw)
        grad_xn_a = project_back(grad_q_raw, wq_a) + project_back(grad_k_raw, wk_a) + project_back(grad_v_raw, wv_a)
        grad_xn_a = lax.psum(grad_xn_a.astype(jnp.bfloat16), 'tp')
        grad_x_norm, grad_norm_a = norm_backward(x_in, norm_a, grad_xn_a.astype(jnp.float32))
        grad_x = (grad_h.astype(jnp.float32) + grad_x_norm).astype(jnp.bfloat16)

        def to_rows(part):
            return lax.psum_scatter(part, 'cp', scatter_dimension=0, tiled=True).astype(jnp.bfloat16)

        return (out_y, grad_x,
                to_rows(grad_norm_a), to_rows(grad_wq_a), to_rows(grad_wk_a), to_rows(grad_wv_a), to_rows(grad_wo_a),
                to_rows(grad_norm_b), to_rows(grad_wq_b), to_rows(grad_wk_b), to_rows(grad_wv_b), to_rows(grad_wo_b))

    return jax.shard_map(body, mesh=mesh, in_specs=in_specs, out_specs=out_specs, check_vma=False)
```

profile of v0, /device:TPU:0, one launch (start us, length us, event | category | flops | bytes accessed | tf_op | source)
XLA Modules:
  0.0 2717.4 jit_solution(7176507450275642252)
XLA Ops:
  7.2 10.1 fusion.31
  17.5 13.8 convolution_convert_fusion.7
  38.5 4.6 multiply_reduce_fusion.1
  47.1 4.4 collective-permute-start.1
  51.5 13.1 convert_bitcast_fusion.1
  67.3 18.9 convolution_convert_fusion.4
  86.2 3.4 convert.12
  92.1 4.7 multiply_reduce_fusion
  99.0 26.0 fusion.38
  125.0 19.2 fusion.19
  144.3 27.0 fusion.85
  171.3 20.0 convolution_convert_fusion.1
  194.0 20.7 convolution_convert_fusion.3
  214.7 384.3 %all-reduce.12.cloned.1.call-done = bf16[6,768,2560]{2,1,0:T(8,128)(2,1)} async-done(((bf16[6,768,2560]{2,1,0:T(8,128)(2,1)}), bf16[6,768,2560]{2,1,0:T(8,128)(2,1)}) %all-reduce.12.cloned.1.call-update) | async-done | bytes 23592976 | tf_op jit(solution)/shard_map/psum | solution.py:125
  599.0 27.6 %fusion.36 = (f32[6,768]{1,0:T(8,128)S(1)}, bf16[6,768,2560]{2,1,0:T(8,128)(2,1)}) fusion(bf16[6,768,2560]{2,1,0:T(8,128)(2,1)} %all-reduce.12.cloned.1.call-done, bf16[6,768,2560]{2,1,0:T(8,128)(2,1)} %param.15), kind=kLoop, calls=%fused_computation.52 | loop fusion | flops 82570752 | bytes 70797312 | tf_op jit(solution)/shard_map/reduce_sum | solution.py:15
  626.7 13.4 convolution_convert_fusion.5
  640.2 15.7 convolution_convert_fusion.6
  656.0 18.2 multiply_convert_fusion
  674.2 24.8 fusion.39
  699.1 19.0 fusion.21
  718.1 46.9 %fusion.12 = (f32[6,2,768]{2,1,0:T(2,128)S(1)}, f32[6,1536,768,2]{2,1,3,0:T(8,128)}) fusion(f32[6,2,768]{2,1,0:T(2,128)S(1)} %fusion.21, f32[6,2,768]{2,1,0:T(2,128)S(1)} %get-tuple-element.36, f32[6,1536,768,2]{2,1,3,0:T(8,128)} %get-tuple-element.37, pred[768,1536]{0,1:T(8,128)(4,1)} %iota_compare_fusion, bf16[6,768,2,256]{1,3,2,0:T(8,128)(2,1)} %bitcast.369, ...), kind=kOutput, calls=%fused_computation.26 | convolution fusion | flops 7332682752 | bytes 123973632 | tf_op jit(solution)/shard_map/bqkgd,bskd->bkgqs/dot_general | solution.py:66
  765.0 46.2 %fusion.40 = bf16[6,2,768,1536]{2,3,1,0:T(8,128)(2,1)} fusion(f32[6,1536,768,2]{2,1,3,0:T(8,128)} %get-tuple-element.39, f32[6,2,768]{2,1,0:T(2,128)S(1)} %get-tuple-element.38, f32[6,2,768]{2,1,0:T(2,128)S(1)} %fusion.21, f32[6,2,768]{2,1,0:T(2,128)S(1)} %get-tuple-element.36, f32[6,1536,768,2]{2,1,3,0:T(8,128)} %get-tuple-element.37, ...), kind=kLoop, calls=%fused_computation.58 | loop fusion | flops 113246208 | bytes 142848000 | tf_op jit(solution)/shard_map/reshape.46
  811.2 16.5 fusion.72
  827.7 27.8 %fusion.73 = bf16[6,1536,1,256]{1,3,0,2:T(8,128)(2,1)} fusion(bf16[6,768,2,256]{1,3,2,0:T(8,128)(2,1)} %bitcast.370, f32[6,2,768]{2,1,0:T(2,128)S(1)} %fusion.21, f32[6,2,768]{2,1,0:T(2,128)S(1)} %get-tuple-element.36, f32[6,1536,768,2]{2,1,3,0:T(8,128)} %get-tuple-element.37, pred[768,1536]{0,1:T(8,128)(4,1)} %iota_compare_fusion), kind=kOutput, calls=%fused_computation.128 | convolution fusion | flops 7320895488 | bytes 67313664 | tf_op jit(solution)/shard_map/bkgqs,bqkgd->bskd/dot_general | solution.py:65
  855.6 19.4 fusion.68
  875.0 6.6 fusion.53
  881.6 20.2 fusion.108
  901.8 20.1 fusion.105
  921.9 40.3 %add_convert_fusion.1 = bf16[6,768,2560]{2,1,0:T(8,128)(2,1)} fusion(f32[6,768,2560]{2,1,0:T(8,128)} %fusion.105, f32[6,768,2560]{2,1,0:T(8,128)} %fusion.108, bf16[6,768,512]{1,2,0:T(8,128)(2,1)} %fusion.53, bf16[2560,512]{1,0:T(8,128)(2,1)S(1)} %copy-done), kind=kOutput, calls=%fused_computation.55 | convolution fusion | flops 12114984960 | bytes 125304832 | tf_op jit(solution)/shard_map/bsh,dh->bsd/dot_general | solution.py:49
  963.0 22.6 convolution_bitcast_fusion.3
  985.7 29.1 %fusion.79 = bf16[6,256,2,768]{3,1,2,0:T(8,128)(2,1)} fusion(bf16[6,1536,256]{2,1,0:T(8,128)(2,1)} %all-gather.5.cloned.1.call-done, f32[6,2,768]{2,1,0:T(2,128)S(1)} %fusion.21, f32[6,2,768]{2,1,0:T(2,128)S(1)} %get-tuple-element.36, f32[6,1536,768,2]{2,1,3,0:T(8,128)} %get-tuple-element.37, pred[768,1536]{0,1:T(8,128)(4,1)S(1)} %copy-done.12), kind=kOutput, calls=%fused_computation.132 | convolution fusion | flops 7320895488 | bytes 67313664 | tf_op jit(solution)/shard_map/bkgqs,bskd->bqkgd/dot_general | solution.py:60
  1014.8 20.4 convolution_bitcast_fusion.1
  1035.3 14.9 convolution_bitcast_fusion.6
  1050.3 15.1 convolution_bitcast_fusion.5
  1065.5 303.7 %all-reduce.14.cloned.1.call-done = bf16[6,768,2560]{2,1,0:T(8,128)(2,1)} async-done(((bf16[6,768,2560]{2,1,0:T(8,128)(2,1)}), bf16[6,768,2560]{2,1,0:T(8,128)(2,1)}) %all-reduce.14.cloned.1.call-update) | async-done | bytes 23592976 | tf_op jit(solution)/shard_map/psum | solution.py:151
  1369.2 27.2 fusion.35
  1396.4 32.8 %fusion.27 = bf16[6,768,2560]{2,1,0:T(8,128)(2,1)} fusion(bf16[6,768,2560]{2,1,0:T(8,128)(2,1)} %all-reduce.14.cloned.1.call-done, bf16[6,768,2560]{2,1,0:T(8,128)(2,1)} %get-tuple-element.23, bf16[6,768,2560]{2,1,0:T(8,128)(2,1)} %param.29, f32[6,768]{1,0:T(8,128)S(1)} %broadcast_multiply_fusion.1, f32[2560]{0:T(1024)S(1)} %copy-done.37, ...), kind=kLoop, calls=%fused_computation.43 | loop fusion | flops 117964800 | bytes 94418944 | tf_op jit(solution)/shard_map/convert_element_type | solution.py:153
  1429.2 19.2 convolution_convert_fusion.2
  1448.4 27.0 fusion.55
  1475.3 4.0 slice.63
  1480.6 48.8 %fusion.8 = (f32[6,2,768]{2,1,0:T(2,128)S(1)}, f32[6,1536,768,2]{2,1,3,0:T(8,128)}) fusion(f32[6,2,768]{2,1,0:T(2,128)S(1)} %copy-done.33, f32[6,2,768]{2,1,0:T(2,128)S(1)} %copy-done.31, f32[6,1536,768,2]{2,1,3,0:T(8,128)} %get-tuple-element.35, pred[768,1536]{0,1:T(8,128)(4,1)S(1)} %copy-done.11, bf16[6,768,2,256]{1,3,2,0:T(8,128)(2,1)} %bitcast.374, ...), kind=kOutput, calls=%fused_computation.20 | convolution fusion | flops 7342119936 | bytes 123973632 | tf_op jit(solution)/shard_map/bqkgd,bskd->bkgqs/dot_general | solution.py:66
  1529.3 45.9 %fusion.41 = bf16[6,2,768,1536]{2,3,1,0:T(8,128)(2,1)} fusion(f32[6,1536,768,2]{2,1,3,0:T(8,128)} %get-tuple-element.41, f32[6,2,768]{2,1,0:T(2,128)S(1)} %get-tuple-element.40, f32[6,2,768]{2,1,0:T(2,128)S(1)} %copy-done.33, f32[6,2,768]{2,1,0:T(2,128)S(1)} %copy-done.31, f32[6,1536,768,2]{2,1,3,0:T(8,128)} %get-tuple-element.35, ...), kind=kLoop, calls=%fused_computation.59 | loop fusion | flops 113246208 | bytes 142848000 | tf_op jit(solution)/shard_map/reshape.71
  1575.3 18.7 convolution_bitcast_fusion
  1597.9 16.9 convolution_bitcast_fusion.7
  1614.9 5.3 fusion.62
  1620.3 4.2 fusion.97
  1628.4 14.1 convolution_bitcast_fusion.8
  1642.6 19.9 convolution_bitcast_fusion.2
  1662.6 21.5 fusion.54
  1684.2 10.7 fusion.60
  1694.9 4.8 fusion.159
  1700.3 8.3 add_convert_fusion.2
  1708.5 21.6 convolution_bitcast_fusion.4
  1730.2 20.0 convolution_convert_fusion
  1750.2 24.8 fusion.94
  1775.0 19.6 fusion.102
  1794.6 41.1 %add_convert_fusion = bf16[6,768,2560]{2,1,0:T(8,128)(2,1)} fusion(f32[6,768,2560]{2,1,0:T(8,128)} %fusion.94, f32[6,768,2560]{2,1,0:T(8,128)} %fusion.102, bf16[2560,256]{1,0:T(8,128)(2,1)} %param.22, bf16[6,768,1,256]{1,3,0,2:T(8,128)(2,1)} %collective-permute-done.3, f32[6,1536,1,256]{1,3,0,2:T(8,128)} %fusion.55), kind=kOutput, calls=%fused_computation.54 | convolution fusion | flops 6078726144 | bytes 126353408 | tf_op jit(solution)/shard_map/bsh,dh->bsd/dot_general | solution.py:49
  1837.6 3.0 convert_element_type.320
  1852.8 3.0 convert_element_type.318
  1858.7 766.8 %all-reduce.16.cloned.1.call-done = (bf16[6,768,2560]{2,1,0:T(8,128)(2,1)}, bf16[6,768,2560]{2,1,0:T(8,128)(2,1)}) async-done(((bf16[6,768,2560]{2,1,0:T(8,128)(2,1)}, bf16[6,768,2560]{2,1,0:T(8,128)(2,1)}), (bf16[6,768,2560]{2,1,0:T(8,128)(2,1)}, bf16[6,768,2560]{2,1,0:T(8,128)(2,1)})) %all-reduce.16.cloned.1.call-update) | async-done | bytes 47185936 | tf_op jit(solution)/shard_map/psum | solution.py:138
  2625.5 23.3 fusion.30
  2648.8 3.4 all-reduce.6
  2653.6 31.3 %fusion.24 = bf16[6,768,2560]{2,1,0:T(8,128)(2,1)} fusion(bf16[6,768,2560]{2,1,0:T(8,128)(2,1)} %get-tuple-element.19, bf16[6,768,2560]{2,1,0:T(8,128)(2,1)} %param.15, bf16[6,768,2560]{2,1,0:T(8,128)(2,1)} %fusion.27, f32[6,768]{1,0:T(8,128)S(1)} %broadcast_multiply_fusion, f32[2560]{0:T(1024)S(1)} %copy-done.35, f32[6,768]{1,0:T(8,128)S(1)} %copy-done.25), kind=kLoop, calls=%fused_computation.40 | loop fusion | flops 117964800 | bytes 94418944 | tf_op jit(solution)/shard_map/convert_element_type | solution.py:176
  2684.9 25.8 fusion.37
  (190 shorter events, 50.1 us)
Async XLA Ops:
  7.2 648.8 %copy-start = (bf16[2560,512]{1,0:T(8,128)(2,1)S(1)}, bf16[2560,512]{1,0:T(8,128)(2,1)}, u32[]{:S(2)}) copy-start(bf16[2560,512]{1,0:T(8,128)(2,1)} %param.25) | copy-start | bytes 7864324
  7.2 10.2 copy-start.43
  7.2 591.8 %all-reduce.12.cloned.1.call-start = ((), (), s32[]{:S(2)}) async-start(), calls=%async_computation.10 | async-start | bytes 47185920 | tf_op jit(solution)/shard_map/psum | solution.py:125
  17.4 49.8 %copy-start.24 = (f32[6,768]{1,0:T(8,128)}, f32[6,768]{1,0:T(8,128)S(1)}, u32[]{:S(2)}) copy-start(f32[6,768]{1,0:T(8,128)S(1)} %add_rsqrt_fusion.1) | copy-start | bytes 55300
  17.4 49.8 %copy-start.34 = (f32[2560]{0:T(1024)}, f32[2560]{0:T(1024)S(1)}, u32[]{:S(2)}) copy-start(f32[2560]{0:T(1024)S(1)} %convert_element_type.248) | copy-start | bytes 30724
  31.2 4.7 copy-start.17
  38.5 8.6 copy-start.3
  38.5 13.0 copy-start.16
  43.1 2.1 copy-start.2
  43.1 4.0 copy-start.28
  43.1 4.0 copy-start.18
  47.1 20.2 copy-start.45
  47.1 51.9 %collective-permute-start.1 = (bf16[6,768,1,256]{1,3,0,2:T(8,128)(2,1)}, bf16[6,768,1,256]{1,3,0,2:T(8,128)(2,1)}, u32[]{:S(2)}, u32[]{:S(2)}) collective-permute-start(bf16[6,768,1,256]{1,3,0,2:T(8,128)(2,1)} %fusion.98), channel_id=1, source_target_pairs={{0,1},{2,3},{4,5},{6,7}} | collective-permute-start | bytes 7077896 | tf_op jit(solution)/shard_map/ppermute | solution.py:114
  64.6 79.7 %collective-permute-start = (bf16[6,768,1,256]{3,1,0,2:T(8,128)(2,1)}, bf16[6,768,1,256]{3,1,0,2:T(8,128)(2,1)}, u32[]{:S(2)}, u32[]{:S(2)}) collective-permute-start(bf16[6,768,1,256]{3,1,0,2:T(8,128)(2,1)} %convert_bitcast_fusion.1), channel_id=1, source_target_pairs={{0,1},{2,3},{4,5},{6,7}} | collective-permute-start | bytes 7077896 | tf_op jit(solution)/shard_map/ppermute | solution.py:115
  86.2 3.5 slice-start.2
  86.2 3.8 slice-start.3
  86.2 4.2 copy-start.39
  90.0 2.1 copy-start.4
  90.0 2.1 copy-start.6
  96.8 28.2 %copy-start.20 = (f32[6,768,2]{1,2,0:T(2,128)}, f32[6,768,2]{1,2,0:T(2,128)S(1)}, u32[]{:S(2)}) copy-start(f32[6,768,2]{1,2,0:T(2,128)S(1)} %fusion.119) | copy-start | bytes 110596
  99.0 26.0 copy-start.10
  125.0 19.3 copy-start.30
  144.3 27.1 copy-start.32
  191.3 482.9 %all-gather.7.cloned.1.call-start = ((), (), s32[]{:S(2)}) async-start(), calls=%async_computation.23 | async-start | bytes 7077888 | tf_op jit(solution)/shard_map/all_gather | solution.py:133
  192.0 464.0 %copy-start.36 = (f32[2560]{0:T(1024)}, f32[2560]{0:T(1024)S(1)}, u32[]{:S(2)}) copy-start(f32[2560]{0:T(1024)S(1)} %convert_element_type.268) | copy-start | bytes 30724
  626.7 29.3 %copy-start.26 = (f32[6,768]{1,0:T(8,128)}, f32[6,768]{1,0:T(8,128)S(1)}, u32[]{:S(2)}) copy-start(f32[6,768]{1,0:T(8,128)S(1)} %add_rsqrt_fusion) | copy-start | bytes 55300
  626.7 13.5 copy-start.40
  640.1 78.0 %all-gather.5.cloned.1.call-start = ((), (), s32[]{:S(2)}) async-start(), calls=%async_computation.22 | async-start | bytes 7077888 | tf_op jit(solution)/shard_map/all_gather | solution.py:134
  640.2 15.8 copy-start.41
  674.2 207.4 %reduce-scatter.11.cloned.1.call-start = ((), (), s32[]{:S(2)}) async-start(), calls=%async_computation.11 | async-start | bytes 7077888 | tf_op jit(solution)/shard_map/reduce_scatter | solution.py:144
  827.7 74.1 %reduce-scatter.13.cloned.1.call-start = ((), (), s32[]{:S(2)}) async-start(), calls=%async_computation.12 | async-start | bytes 7077888 | tf_op jit(solution)/shard_map/reduce_scatter | solution.py:145
  855.6 19.5 copy-start.42
  855.6 513.6 %all-reduce.14.cloned.1.call-start = ((), (), s32[]{:S(2)}) async-start(), calls=%async_computation.13 | async-start | bytes 47185920 | tf_op jit(solution)/shard_map/psum | solution.py:151
  962.3 23.4 copy-start.12
  962.3 875.3 %reduce-scatter.23.cloned.1.call-start = ((), (), s32[]{:S(2)}) async-start(), calls=%async_computation.18 | async-start | bytes 7864320 | tf_op jit(solution)/shard_map/reduce_scatter | solution.py:179
  985.6 854.9 %reduce-scatter.29.cloned.1.call-start = ((), (), s32[]{:S(2)}) async-start(), calls=%async_computation.21 | async-start | bytes 7864320 | tf_op jit(solution)/shard_map/reduce_scatter | solution.py:179
  1014.8 20.5 copy-start.15
  1035.2 808.3 %reduce-scatter.25.cloned.1.call-start = ((), (), s32[]{:S(2)}) async-start(), calls=%async_computation.19 | async-start | bytes 3932160 | tf_op jit(solution)/shard_map/reduce_scatter | solution.py:179
  1050.3 795.8 %reduce-scatter.27.cloned.1.call-start = ((), (), s32[]{:S(2)}) async-start(), calls=%async_computation.20 | async-start | bytes 3932160 | tf_op jit(solution)/shard_map/reduce_scatter | solution.py:179
  1065.4 782.9 %reduce-scatter.19.cloned.1.call-start = ((), (), s32[]{:S(2)}) async-start(), calls=%async_computation.16 | async-start | bytes 3932160 | tf_op jit(solution)/shard_map/reduce_scatter | solution.py:179
  1429.2 19.2 copy-start.11
  1429.2 19.2 copy-start.31
  1429.2 19.2 copy-start.33
  1479.3 118.6 %collective-permute-start.3 = (bf16[6,768,1,256]{1,3,0,2:T(8,128)(2,1)}, bf16[6,768,1,256]{1,3,0,2:T(8,128)(2,1)}, u32[]{:S(2)}, u32[]{:S(2)}) collective-permute-start(bf16[6,768,1,256]{1,3,0,2:T(8,128)(2,1)} %slice.63), channel_id=1, source_target_pairs={{1,0},{3,2},{5,4},{7,6}} | collective-permute-start | bytes 7077896 | tf_op jit(solution)/shard_map/ppermute | solution.py:166
  1529.3 45.9 %copy-start.21 = (f32[6,768,2]{1,2,0:T(2,128)S(1)}, f32[6,768,2]{1,2,0:T(2,128)}, u32[]{:S(2)}) copy-start(f32[6,768,2]{1,2,0:T(2,128)} %copy-done.20) | copy-start | bytes 110596
  1575.3 22.6 copy-start.25
  1575.3 22.6 copy-start.35
  1596.6 18.4 collective-permute-start.2
  1614.8 5.4 copy-start.29
  1614.8 5.5 copy-start.5
  1614.8 5.5 copy-start.19
  1614.9 235.7 %reduce-scatter.17.cloned.1.call-start = ((), (), s32[]{:S(2)}) async-start(), calls=%async_computation.15 | async-start | bytes 3932160 | tf_op jit(solution)/shard_map/reduce_scatter | solution.py:179
  1620.3 4.8 slice-start
  1620.3 4.7 slice-start.1
  1620.3 5.0 copy-start.7
  1642.6 210.2 %reduce-scatter.21.cloned.1.call-start = ((), (), s32[]{:S(2)}) async-start(), calls=%async_computation.17 | async-start | bytes 7864320 | tf_op jit(solution)/shard_map/reduce_scatter | solution.py:179
  1662.5 21.6 copy-start.23
  1662.6 193.2 %reduce-scatter.15.cloned.1.call-start = ((), (), s32[]{:S(2)}) async-start(), calls=%async_computation.14 | async-start | bytes 7864320 | tf_op jit(solution)/shard_map/reduce_scatter | solution.py:179
  1694.9 4.9 copy-start.8
  1694.9 5.3 copy-start.9
  1730.2 895.4 %all-reduce.16.cloned.1.call-start = ((), (), s32[]{:S(2)}) async-start(), calls=%async_computation.24 | async-start | bytes 94371840 | tf_op jit(solution)/shard_map/psum | solution.py:138
  1750.2 24.9 copy-start.14
  2625.5 23.3 copy-start.38
  2684.9 25.8 copy-start.1
  (6 other events, 4.9 us)
Sparse Core Ops, SparseCore 0:
  191.5 407.5 all-reduce.11
  640.2 11.6 all-gather.6
  674.3 11.8 all-gather.4
  827.8 9.8 reduce-scatter.10
  855.7 10.0 reduce-scatter.12
  962.4 406.7 all-reduce.13
  1371.5 10.1 reduce-scatter.22
  1383.9 11.5 reduce-scatter.28
  1397.7 8.9 reduce-scatter.24
  1408.8 8.9 reduce-scatter.26
  1615.0 10.8 reduce-scatter.18
  1642.7 10.9 reduce-scatter.16
  1662.7 14.4 reduce-scatter.20
  1730.3 14.8 reduce-scatter.14
  1835.8 789.6 all-reduce.15
where the time goes:
time: 2730 us; the launch traced here: 2720 us
  waiting for transfers between devices  1460 us (53%)
  matrix products  818 us (30%)
  other arithmetic  396 us (15%)
    psum x1, waiting for transfers between devices, body(): attn_b = lax.psum(project(out_b, wo_b), 'tp')  767 us
    psum x1, waiting for transfers between devices, body(): attn_a = lax.psum(project(out_a, wo_a), 'tp')  384 us
    psum x1, waiting for transfers between devices, body(): grad_xn_b = lax.psum(grad_xn_b.astype(jnp.bfloat16), 'tp')  304 us
    dot_general x8, matrix products, project_back(): jnp.einsum('bsh,dh->bsd', grad_out, weight, preferred_element_type=jnp.fl...  206 us
    dot_general x8, matrix products, weight_grad(): jnp.einsum('bsd,bsh->dh', act, grad_out, preferred_element_type=jnp.float32)  146 us
    dot_general x8, matrix products, project(): jnp.einsum('bsd,dh->bsh', act, weight, preferred_element_type=jnp.float32)  133 us
    dot_general x2, matrix products, attn_backward(): jnp.einsum('bqkgd,bskd->bkgqs', grad_out, values, preferred_element_type=...  95.6 us
    another operation x2, other arithmetic  92.1 us
  transfers between devices with their start and end apart: 19, of which 3 were waited for; matrix products, arithmetic and copies ran while one was open for 31% of the time, Pallas kernels for 0%

commit v1 on v0

v1 whole, which is shorter than its diff:
```python
import functools

import jax
import jax.numpy as jnp
from jax import lax
from jax.experimental import pallas as pl
from jax.experimental.pallas import tpu as pltpu
from jax.sharding import PartitionSpec as P


CHUNK = 8192
NORM_EPS = 1e-5
QK_EPS = 1e-6
TEMP_SCALE = 0.1
CHUNK_BITS = 13
HEAD = 256
TILE = 384
NEG_BIG = -1e30
F32 = jnp.float32
BF16 = jnp.bfloat16


def rms_norm(act, gamma):
    act_wide = act.astype(F32)
    inv_rms = lax.rsqrt(jnp.mean(act_wide * act_wide, axis=-1, keepdims=True) + NORM_EPS)
    return (act_wide * inv_rms * gamma.astype(F32)).astype(BF16)


def norm_backward(act, gamma, grad_out):
    act_wide = act.astype(F32)
    inv_rms = lax.rsqrt(jnp.mean(act_wide * act_wide, axis=-1, keepdims=True) + NORM_EPS)
    x_hat = act_wide * inv_rms
    grad_gain = jnp.sum(grad_out * x_hat, axis=0)
    grad_hat = grad_out * gamma.astype(F32)
    grad_act = inv_rms * (grad_hat - x_hat * jnp.mean(grad_hat * x_hat, axis=-1, keepdims=True))
    return grad_act, grad_gain


def value_a11(positions):
    return jnp.log(((positions + 1) // CHUNK).astype(F32) + 1.0) * TEMP_SCALE + 1.0


def dot_f32(spec, lhs, rhs):
    return jnp.einsum(spec, lhs, rhs, preferred_element_type=F32)


def kdot(lhs, rhs, lhs_dim, rhs_dim):
    return lax.dot_general(lhs, rhs, (((lhs_dim,), (rhs_dim,)), ((), ())), preferred_element_type=F32)


def turn(wide, cos_tab, sin_tab):
    half = HEAD // 2
    turned = jnp.concatenate([-wide[:, half:], wide[:, :half]], axis=1)
    return wide * cos_tab + turned * sin_tab


def prep_kernel(q_ref, kv_ref, cos_ref, sin_ref, q_out, kv_out):
    for src, dst, count in ((q_ref, q_out, 2), (kv_ref, kv_out, 1)):
        for head in range(count):
            cols = pl.ds(head * HEAD, HEAD)
            wide = turn(src[0, :, cols].astype(F32), cos_ref[...], sin_ref[...])
            inv = lax.rsqrt(jnp.mean(wide * wide, axis=-1, keepdims=True) + QK_EPS)
            dst[0, :, cols] = (wide * inv).astype(BF16)
    kv_out[0, :, HEAD:] = kv_ref[0, :, HEAD:]


def prep_back_kernel(q_ref, kv_ref, cos_ref, sin_ref, gq_ref, gkv_ref, q_out, kv_out):
    half = HEAD // 2
    for src, grad, dst, count in ((q_ref, gq_ref, q_out, 2), (kv_ref, gkv_ref, kv_out, 1)):
        for head in range(count):
            cols = pl.ds(head * HEAD, HEAD)
            wide = turn(src[0, :, cols].astype(F32), cos_ref[...], sin_ref[...])
            inv = lax.rsqrt(jnp.mean(wide * wide, axis=-1, keepdims=True) + QK_EPS)
            hat = wide * inv
            up = grad[0, :, cols].astype(F32)
            down = inv * (up - hat * jnp.mean(up * hat, axis=-1, keepdims=True))
            side = down * sin_ref[...]
            back = jnp.concatenate([side[:, half:], -side[:, :half]], axis=1)
            dst[0, :, cols] = (down * cos_ref[...] + back).astype(BF16)
    kv_out[0, :, HEAD:] = gkv_ref[0, :, HEAD:]


def prep_call(kernel, q_val, kv_val, cos_tab, sin_tab, *grads):
    groups, rows, wide = q_val.shape
    big = pl.BlockSpec((1, TILE, wide), lambda g, i: (g, i, 0))
    tab = pl.BlockSpec((TILE, HEAD), lambda g, i: (i, 0))
    return pl.pallas_call(
        kernel,
        grid=(groups, rows // TILE),
        in_specs=[big, big, tab, tab] + [big] * len(grads),
        out_specs=[big, big],
        out_shape=[jax.ShapeDtypeStruct(q_val.shape, BF16)] * 2,
        cost_estimate=pl.CostEstimate(flops=20 * q_val.size, bytes_accessed=10 * q_val.size, transcendentals=0),
    )(q_val, kv_val, cos_tab, sin_tab, *grads)


def tile_mask(meta, tile, keys, local):
    q_at = meta[3 + tile] + lax.broadcasted_iota(jnp.int32, (1, TILE), 1)
    low = jnp.full((1, TILE), meta[6], jnp.int32)
    if local:
        start = lax.shift_left(lax.shift_right_logical(q_at + meta[7], CHUNK_BITS), CHUNK_BITS)
        low = jnp.maximum(low, start - meta[7])
    key = lax.broadcasted_iota(jnp.int32, (keys, 1), 0)
    return (key <= q_at) & (key >= low)


def pick_window(meta, tile, prev_own, cur_own, prev_sh, cur_sh):
    own = meta[tile] == 0
    return jnp.concatenate([jnp.where(own, prev_own[0], prev_sh[0]), jnp.where(own, cur_own[0], cur_sh[0])], axis=0)


def attn_kernel(local, scale, meta, q_ref, prev_own, cur_own, prev_sh, cur_sh, o_ref, stat_ref):
    tile = pl.program_id(1)
    window = pick_window(meta, tile, prev_own, cur_own, prev_sh, cur_sh)
    key = window[:, :HEAD]
    val_t = window[:, HEAD:].T
    allowed = tile_mask(meta, tile, window.shape[0], local)
    for head in range(2):
        query = q_ref[0, :, pl.ds(head * HEAD, HEAD)]
        scores = jnp.where(allowed, kdot(key, query, 1, 1) * scale, NEG_BIG)
        top = jnp.max(scores, axis=0, keepdims=True)
        prob = jnp.exp(scores - top)
        inv = 1.0 / jnp.sum(prob, axis=0, keepdims=True)
        stat_ref[0, pl.ds(head, 1), :] = top
        stat_ref[0, pl.ds(2 + head, 1), :] = inv
        out_t = kdot(val_t, (prob * inv).astype(BF16), 1, 0)
        o_ref[head] = out_t.T.astype(BF16)


def attn_back_kernel(local, scale, meta, q_ref, prev_own, cur_own, prev_sh, cur_sh, stat_ref, g_ref, tau_ref,
                     dq_ref, dprev_own, dcur_own, dprev_sh, dcur_sh, acc):
    tile = pl.program_id(1)

    @pl.when(tile == 0)
    def _():
        acc[...] = jnp.zeros_like(acc)

    window = pick_window(meta, tile, prev_own, cur_own, prev_sh, cur_sh)
    key = window[:, :HEAD]
    val = window[:, HEAD:]
    key_t = key.T
    allowed = tile_mask(meta, tile, window.shape[0], local)
    dkey = None
    for head in range(2):
        query = q_ref[0, :, pl.ds(head * HEAD, HEAD)]
        grad = g_ref[head]
        scores = jnp.where(allowed, kdot(key, query, 1, 1) * scale, NEG_BIG)
        prob = jnp.exp(scores - stat_ref[0, pl.ds(head, 1), :]) * stat_ref[0, pl.ds(2 + head, 1), :]
        dprob = kdot(val, grad, 1, 1)
        row_dot = jnp.sum(prob * dprob, axis=0, keepdims=True)
        dscore = (prob * (dprob - row_dot) * scale).astype(BF16)
        dval_h = kdot(prob.astype(BF16), grad, 1, 0)
        dkey_h = kdot(dscore, query, 1, 0)
        dkey, dval = (dkey_h, dval_h) if dkey is None else (dkey + dkey_h, dval + dval_h)
        dq_t = kdot(key_t, dscore, 1, 0) * tau_ref[...]
        dq_ref[0, :, pl.ds(head * HEAD, HEAD)] = dq_t.T.astype(BF16)
    slot = meta[tile]
    acc[slot, :, :HEAD] += dkey
    acc[slot, :, HEAD:] += dval

    @pl.when(tile == pl.num_programs(1) - 1)
    def _():
        block = acc.shape[1] // 2
        dprev_own[0] = acc[0, :block].astype(BF16)
        dcur_own[0] = acc[0, block:]
        dprev_sh[0] = acc[1, :block].astype(BF16)
        dcur_sh[0] = acc[1, block:]


def attn_specs(block):
    wide = 2 * HEAD
    q_spec = pl.BlockSpec((1, TILE, wide), lambda g, i, meta: (g, i, 0))
    w_spec = pl.BlockSpec((1, block, wide), lambda g, i, meta: (g, 0, 0))
    o_spec = pl.BlockSpec((2, TILE, HEAD), lambda g, i, meta: (0, i, g))
    s_spec = pl.BlockSpec((1, 4, TILE), lambda g, i, meta: (g, 0, i))
    return q_spec, w_spec, o_spec, s_spec


def attn_forward(local, scale, meta, q_val, wins):
    groups, rows, _ = q_val.shape
    block = wins[0].shape[1]
    q_spec, w_spec, o_spec, s_spec = attn_specs(block)
    return pl.pallas_call(
        functools.partial(attn_kernel, local, scale),
        grid_spec=pltpu.PrefetchScalarGridSpec(
            num_scalar_prefetch=1, grid=(groups, rows // TILE),
            in_specs=[q_spec] + [w_spec] * 4, out_specs=[o_spec, s_spec]),
        out_shape=[jax.ShapeDtypeStruct((2, rows, groups * HEAD), BF16), jax.ShapeDtypeStruct((groups, 4, rows), F32)],
        compiler_params=pltpu.CompilerParams(vmem_limit_bytes=56 << 20),
        cost_estimate=pl.CostEstimate(flops=8 * q_val.size * 2 * block, bytes_accessed=12 * q_val.size,
                                      transcendentals=q_val.size * 6),
        name='attn_fwd',
    )(meta, q_val, *wins)


def attn_backward(local, scale, meta, q_val, wins, stats, grad_out, tau):
    groups, rows, wide = q_val.shape
    block = wins[0].shape[1]
    q_spec, w_spec, o_spec, s_spec = attn_specs(block)
    t_spec = pl.BlockSpec((1, TILE), lambda g, i, meta: (0, i))
    half = jax.ShapeDtypeStruct(wins[0].shape, BF16)
    full = jax.ShapeDtypeStruct(wins[0].shape, F32)
    return pl.pallas_call(
        functools.partial(attn_back_kernel, local, scale),
        grid_spec=pltpu.PrefetchScalarGridSpec(
            num_scalar_prefetch=1, grid=(groups, rows // TILE),
            in_specs=[q_spec] + [w_spec] * 4 + [s_spec, o_spec, t_spec],
            out_specs=[q_spec] + [w_spec] * 4,
            scratch_shapes=[pltpu.VMEM((2, 2 * block, wide), F32)]),
        out_shape=[jax.ShapeDtypeStruct(q_val.shape, BF16), half, full, half, full],
        compiler_params=pltpu.CompilerParams(vmem_limit_bytes=60 << 20),
        cost_estimate=pl.CostEstimate(flops=20 * q_val.size * 2 * block, bytes_accessed=20 * q_val.size,
                                      transcendentals=q_val.size * 6),
        name='attn_bwd',
    )(meta, q_val, *wins, stats, grad_out, tau)


def solution(mesh):
    tp_size = mesh.shape['tp']
    row_spec = P(None, 'cp', None)
    col_spec = P(None, 'tp')
    grid_spec = P('cp', 'tp')
    out_rows = P(('tp', 'cp'), None)
    in_specs = (row_spec, P('cp'), P('cp', None), P('cp', None),
                P(None), col_spec, col_spec, col_spec, P('tp', None),
                P(None), col_spec, col_spec, col_spec, P('tp', None), row_spec)
    out_specs = (row_spec, row_spec,
                 P('cp'), grid_spec, grid_spec, grid_spec, out_rows,
                 P('cp'), grid_spec, grid_spec, grid_spec, out_rows)

    def body(x_in, positions, rope_cos, rope_sin, norm_a, wq_a, wk_a, wv_a, wo_a,
             norm_b, wq_b, wk_b, wv_b, wo_b, grad_y):
        batch, block, d_model = x_in.shape
        head_dim = rope_cos.shape[1]
        tp_rank = lax.axis_index('tp')
        cp_rank = lax.axis_index('cp')
        par = tp_rank % 2
        n_rows = batch * block // tp_size
        half = block // 2
        scale = head_dim ** -0.5
        own_at = half * par
        shared_at = block * (1 - par)
        base_shared = half * par

        def my_rows(full):
            return lax.dynamic_slice_in_dim(full.reshape(batch * block, -1), tp_rank * n_rows, n_rows, 0)

        def row_table(tab):
            shared = lax.dynamic_slice_in_dim(tab, base_shared, half, 0)
            long = jnp.concatenate([shared, tab, shared], axis=0)
            return lax.dynamic_slice_in_dim(long, half * (1 - par), n_rows, 0)

        def gather_weight(part):
            over_tp = lax.all_gather(part, 'tp', axis=0, tiled=False)
            return lax.all_gather(over_tp, 'cp', axis=0, tiled=False)

        def gather_qkv(w_q, w_k, w_v):
            return gather_weight(jnp.where(cp_rank == 0, w_q, jnp.concatenate([w_k, w_v], axis=1)))

        def gather_out(w_o):
            part = lax.dynamic_slice_in_dim(w_o, cp_rank * head_dim, head_dim, 0)
            return gather_weight(part).reshape(2, tp_size * head_dim, d_model)

        def swap(val):
            return lax.ppermute(val, 'tp', [(i, i ^ 1) for i in range(tp_size)])

        def kv_windows(key_val):
            own = lax.dynamic_slice_in_dim(key_val, own_at, block, 1)
            shared = lax.dynamic_slice_in_dim(key_val, shared_at, half, 1)
            prev_own = lax.ppermute(own, 'cp', [(0, 1)])
            other = swap(shared)
            sh_blk = lax.dynamic_slice_in_dim(jnp.concatenate([shared, other, shared], axis=1), half * par, block, 1)
            return prev_own, own, lax.ppermute(sh_blk, 'cp', [(0, 1)]), sh_blk

        def kv_windows_back(dprev_own, dcur_own, dprev_sh, dcur_sh):
            sh_blk = dcur_sh + lax.ppermute(dprev_sh, 'cp', [(1, 0)]).astype(F32)
            own = dcur_own + lax.ppermute(dprev_own, 'cp', [(1, 0)]).astype(F32)
            mine = lax.dynamic_slice_in_dim(sh_blk, half * par, half, 1)
            theirs = lax.dynamic_slice_in_dim(sh_blk, half * (1 - par), half, 1)
            mine = (mine + swap(theirs.astype(BF16)).astype(F32)).astype(BF16)
            long = jnp.concatenate([mine, own.astype(BF16), mine], axis=1)
            return lax.dynamic_slice_in_dim(long, half * (1 - par), n_rows, 1)

        def exchange(pick, place, buf):
            for k in range(tp_size):
                peer = tp_rank ^ k
                piece = pick(peer)
                if k:
                    piece = lax.ppermute(piece, 'tp', [(i, i ^ k) for i in range(tp_size)])
                buf = place(buf, piece, peer)
            return buf

        def to_groups(val):
            return exchange(lambda p: lax.dynamic_index_in_dim(val, p, 0, keepdims=False),
                            lambda buf, piece, p: lax.dynamic_update_slice_in_dim(buf, piece, p * n_rows, 0),
                            jnp.zeros((batch * block, val.shape[2]), val.dtype))

        def heads_to_groups(val):
            return exchange(lambda p: lax.dynamic_slice_in_dim(val, p * head_dim, head_dim, 2),
                            lambda buf, piece, p: lax.dynamic_update_slice_in_dim(buf, piece, p * n_rows, 1),
                            jnp.zeros((2, batch * block, head_dim), val.dtype))

        def to_all(rows):
            return lax.all_gather(rows, 'tp', axis=0, tiled=True).reshape(batch, block, d_model)

        def cp_sum(part_of):
            sent = lax.ppermute(part_of(1 - cp_rank), 'cp', [(0, 1), (1, 0)])
            return part_of(cp_rank) + sent

        def cols(val, half_no):
            return lax.dynamic_slice_in_dim(val, half_no * (d_model // 2), d_model // 2, 1)

        def head_rows(val, half_no):
            return lax.dynamic_index_in_dim(val, half_no, 0, keepdims=False)

        w_qkv_a = gather_qkv(wq_a, wk_a, wv_a)
        w_out_a = gather_out(wo_a)
        w_qkv_b = gather_qkv(wq_b, wk_b, wv_b)
        w_out_b = gather_out(wo_b)

        meta = jnp.stack([par, 0 * par, 1 - par,
                          block + half * par, block + half * (1 - par), block + half * par,
                          block * (1 - cp_rank), positions[0] - block]).astype(jnp.int32)
        cos_r = row_table(rope_cos)
        sin_r = row_table(rope_sin)
        q_temp = row_table(value_a11(positions))
        ones = jnp.ones((1, n_rows), F32)

        xn_all = rms_norm(x_in, norm_a).reshape(batch * block, d_model)
        x_rows = my_rows(x_in)
        gy_rows = my_rows(grad_y)
        xn_a = lax.dynamic_slice_in_dim(xn_all, tp_rank * n_rows, n_rows, 0)
        kv_raw = dot_f32('rd,tdh->trh', xn_a, w_qkv_a[1]).astype(BF16)
        q_raw = dot_f32('rd,tdh->trh', xn_a, w_qkv_a[0]).astype(BF16)
        query_a, kv_a = prep_call(prep_kernel, q_raw, kv_raw, cos_r, sin_r)
        wins_a = kv_windows(kv_a)
        out_a, stat_a = attn_forward(True, scale, meta, query_a, wins_a)
        attn_a = dot_f32('crh,chd->rd', out_a, w_out_a).astype(BF16)
        h_rows = (x_rows.astype(F32) + attn_a.astype(F32)).astype(BF16)

        xn_b = rms_norm(h_rows, norm_b)
        kv_b = dot_f32('rd,tdh->trh', xn_b, w_qkv_b[1]).astype(BF16)
        wins_b = kv_windows(kv_b)
        q_b = dot_f32('rd,tdh->trh', xn_b, w_qkv_b[0]).astype(BF16)
        q_b = (q_b.astype(F32) * q_temp[None, :, None]).astype(BF16)
        out_b, stat_b = attn_forward(False, scale, meta, q_b, wins_b)
        attn_b = dot_f32('crh,chd->rd', out_b, w_out_b).astype(BF16)
        y_rows = (h_rows.astype(F32) + attn_b.astype(F32)).astype(BF16)
        out_y = to_all(y_rows)
        gy_rows, _ = lax.optimization_barrier((gy_rows, y_rows))

        grad_ob = dot_f32('rd,chd->crh', gy_rows, w_out_b).astype(BF16)
        grad_q_b, *back_b = attn_backward(False, scale, meta, q_b, wins_b, stat_b, grad_ob, q_temp[None, :])
        out_b_group = heads_to_groups(out_b)
        gy_all = grad_y.reshape(batch * block, d_model)
        grad_wo_b = cp_sum(lambda half_no: dot_f32('rh,rd->hd', head_rows(out_b_group, half_no), gy_all))
        grad_kv_b = kv_windows_back(*back_b)
        parts = []
        for grad_part in (grad_q_b, grad_kv_b):
            part_b = cp_sum(lambda half_no: dot_f32('rd,trh->tdh', cols(xn_b, half_no), grad_part))
            parts.append(lax.psum_scatter(part_b.reshape(-1, 2 * head_dim), 'tp', scatter_dimension=0, tiled=True))
        grad_wq_b, grad_wkv_b = parts
        grad_xn_b = (dot_f32('trh,tdh->rd', grad_q_b, w_qkv_b[0])
                     + dot_f32('trh,tdh->rd', grad_kv_b, w_qkv_b[1])).astype(BF16)
        grad_h_norm, gain_b = norm_backward(h_rows, norm_b, grad_xn_b.astype(F32))
        grad_h = (gy_rows.astype(F32) + grad_h_norm).astype(BF16)

        grad_oa = dot_f32('rd,chd->crh', grad_h, w_out_a).astype(BF16)
        grad_q_a, *back_a = attn_backward(True, scale, meta, query_a, wins_a, stat_a, grad_oa, ones)
        part_o = cp_sum(lambda half_no: dot_f32('rh,rd->hd', head_rows(out_a, half_no), grad_h))
        grad_wo_a = lax.psum_scatter(part_o, 'tp', scatter_dimension=0, tiled=True)
        grad_kv_a = kv_windows_back(*back_a)
        grad_q_raw, grad_kv_raw = prep_call(prep_back_kernel, q_raw, kv_raw, cos_r, sin_r, grad_q_a, grad_kv_a)
        grad_xn_q = dot_f32('trh,tdh->rd', grad_q_raw, w_qkv_a[0])
        grad_xn_a = (grad_xn_q + dot_f32('trh,tdh->rd', grad_kv_raw, w_qkv_a[1])).astype(BF16)
        grad_x_norm, gain_a = norm_backward(x_rows, norm_a, grad_xn_a.astype(F32))
        gx_rows = (grad_h.astype(F32) + grad_x_norm).astype(BF16)
        grad_x = to_all(gx_rows)
        grad_q_group = to_groups(grad_q_raw)
        grad_kv_group = to_groups(grad_kv_raw)
        grad_wq_a = cp_sum(lambda half_no: dot_f32('rd,rh->dh', cols(xn_all, half_no), grad_q_group))
        grad_wkv_a = cp_sum(lambda half_no: dot_f32('rd,rh->dh', cols(xn_all, half_no), grad_kv_group))

        gains = lax.psum(jnp.stack([gain_a, gain_b]), ('tp', 'cp'))
        gains = lax.dynamic_slice_in_dim(gains, cp_rank * (d_model // 2), d_model // 2, 1).astype(BF16)
        grad_wo_b, grad_wo_a, grad_wq_a, grad_wkv_a, grad_wq_b, grad_wkv_b = (
            val.astype(BF16) for val in (grad_wo_b, grad_wo_a, grad_wq_a, grad_wkv_a, grad_wq_b, grad_wkv_b))
        return (out_y, grad_x,
                gains[0], grad_wq_a, grad_wkv_a[:, :head_dim], grad_wkv_a[:, head_dim:], grad_wo_a,
                gains[1], grad_wq_b, grad_wkv_b[:, :head_dim], grad_wkv_b[:, head_dim:], grad_wo_b)

    return jax.shard_map(body, mesh=mesh, in_specs=in_specs, out_specs=out_specs, check_vma=False)
```

time: 2730 us -> 1760 us (0.64)
  waiting for transfers between devices: 1460 us -> 758 us
  matrix products: 818 us -> 374 us
  Pallas kernels: 0 us -> 288 us
  other arithmetic: 396 us -> 135 us
  local copies, waits for them, and re-layouts: 19.2 us -> 121 us
    psum x3 -> x0, waiting for transfers between devices: 1450 us -> none  [the longest x1 767 us: body(): attn_b = lax.psum(project(out_b, wo_b), 'tp')]
    dot_general x36 -> x24, matrix products: 818 us -> 374 us  [dot_f32(): return jnp.einsum(spec, lhs, rhs, preferred_element_type=F32)]
    ppermute x4 -> x27, waiting for transfers between devices: 0.01 us -> 439 us  [the longest x9 225 us: exchange(): piece = lax.ppermute(piece, 'tp', [(i, i ^ k) for i in range(tp_size)])]
    all_gather x2 -> x10, waiting for transfers between devices: 0.04 us -> 319 us  [the longest x4 253 us: gather_weight(): over_tp = lax.all_gather(part, 'tp', axis=0, tiled=False)]
    pallas_call x0 -> x6, Pallas kernels: none -> 288 us  [the longest x2 161 us: attn_backward(): pl.pallas_call(functools.partial(attn_back_kernel, local, scale), grid_sp...]
    reduce_sum x7 -> x1, other arithmetic: 103 us -> 3.89 us  [norm_backward(): jnp.mean(act_wide * act_wide, axis=-1, keepdims=True) + NORM_EPS]
    another operation x2 -> x1, other arithmetic: 92.1 us -> 0.02 us  [body(): gains = lax.psum(jnp.stack([gain_a, gain_b]), ('tp', 'cp'))]
    convert_element_type x19 -> x13, other arithmetic: 135 us -> 61.4 us  [the longest x4 26 us: rms_norm(): return (act_wide * inv_rms * gamma.astype(F32)).astype(BF16)]
  transfers between devices with their start and end apart: 19 -> 40, of which waited for: 3 -> 21; matrix products, arithmetic and copies ran while one was open for 31% -> 29% of each run, Pallas kernels for 0% -> 12%
where the time goes in v1:
time: 1760 us; the launch traced here: 1750 us
  waiting for transfers between devices  758 us (43%)
  matrix products  374 us (21%)
  Pallas kernels  288 us (16%)
  other arithmetic  135 us (8%)
  local copies, waits for them, and re-layouts  121 us (7%)
  starting transfers between devices  33.8 us (2%)
  blocking collectives  23.9 us (1%)
    dot_general x24, matrix products, dot_f32(): return jnp.einsum(spec, lhs, rhs, preferred_element_type=F32)  374 us
    all_gather x4, waiting for transfers between devices, gather_weight(): over_tp = lax.all_gather(part, 'tp', axis=0, tiled=False)  253 us
    ppermute x9, waiting for transfers between devices, exchange(): piece = lax.ppermute(piece, 'tp', [(i, i ^ k) for i in range(tp_size)])  225 us
    ppermute x4, waiting for transfers between devices, swap(): return lax.ppermute(val, 'tp', [(i, i ^ 1) for i in range(tp_size)])  175 us
    pallas_call x2, Pallas kernels, attn_backward(): pl.pallas_call(functools.partial(attn_back_kernel, local, scale), grid_sp...  161 us
    pallas_call x2, Pallas kernels, attn_forward(): pl.pallas_call(functools.partial(attn_kernel, local, scale), grid_spec=pl...  94 us
    all_gather x2, waiting for transfers between devices, to_all(): lax.all_gather(rows, 'tp', axis=0, tiled=True)  65.8 us
    unnamed x76, local copies, waits for them, and re-layouts  39.7 us
  transfers between devices with their start and end apart: 40, of which 21 were waited for; matrix products, arithmetic and copies ran while one was open for 29% of the time, Pallas kernels for 12%

profile of v1, /device:TPU:0, one launch (start us, length us, event | category | flops | bytes accessed | tf_op | source)
XLA Modules:
  0.0 1750.2 jit_solution(2241947230508559526)
XLA Ops:
  18.1 96.3 %all-gather.23.cloned.1.call-done = bf16[10240,512]{1,0:T(8,128)(2,1)} async-done(((bf16[2560,512]{1,0:T(8,128)(2,1)}), bf16[10240,512]{1,0:T(8,128)(2,1)}) %all-gather.23.cloned.1.call-update) | async-done | bytes 10485776 | tf_op jit(solution)/shard_map/all_gather | solution.py:254
  117.4 55.2 %all-gather.27.cloned.1.call-done = bf16[1024,2560]{1,0:T(8,128)(2,1)} async-done(((bf16[256,2560]{1,0:T(8,128)(2,1)}), bf16[1024,2560]{1,0:T(8,128)(2,1)}) %all-gather.27.cloned.1.call-update) | async-done | bytes 5242896 | tf_op jit(solution)/shard_map/all_gather | solution.py:254
  172.6 101.7 %all-gather.31.cloned.1.call-done = bf16[10240,512]{1,0:T(8,128)(2,1)} async-done(((bf16[2560,512]{1,0:T(8,128)(2,1)}), bf16[10240,512]{1,0:T(8,128)(2,1)}) %all-gather.31.cloned.1.call-update) | async-done | bytes 10485776 | tf_op jit(solution)/shard_map/all_gather | solution.py:254
  275.7 13.9 fusion
  291.8 22.1 %fusion.2 = bf16[6,768,2560]{2,1,0:T(8,128)(2,1)} fusion(bf16[6,768,2560]{2,1,0:T(8,128)(2,1)} %param.15, f32[2560]{0:T(1024)S(1)} %convert_element_type.167, f32[6,768]{1,0:T(8,128)S(1)} %add_rsqrt_fusion), kind=kLoop, calls=%fused_computation.4 | loop fusion | flops 47185920 | bytes 47214592 | tf_op jit(solution)/shard_map/convert_element_type | solution.py:26
  313.9 19.2 %fusion.92.kv_ref = bf16[4,1152,512]{2,1,0:T(8,128)(2,1)} fusion(bf16[8,2560,512]{2,1,0:T(8,128)(2,1)} %all-gather.25.cloned.1.call-done, bf16[4608,2560]{1,0:T(8,128)(2,1)} %bitcast.181, s32[]{:T(128)S(6)} %select_n.131), kind=kOutput, calls=%fused_computation.110 | convolution fusion | flops 12081954816 | bytes 31588356 | tf_op jit(solution)/shard_map/rd,tdh->trh/dot_general | solution.py:44
  333.1 18.6 %fusion.95.q_ref = bf16[4,1152,512]{2,1,0:T(8,128)(2,1)} fusion(bf16[8,2560,512]{2,1,0:T(8,128)(2,1)} %all-gather.25.cloned.1.call-done, bf16[4608,2560]{1,0:T(8,128)(2,1)} %bitcast.182, s32[]{:T(128)S(6)} %select_n.131), kind=kOutput, calls=%fused_computation.111 | convolution fusion | flops 12081954816 | bytes 31588356 | tf_op jit(solution)/shard_map/rd,tdh->trh/dot_general | solution.py:44
  351.7 14.4 shard_map.238
  375.9 27.4 %collective-permute-done.1 = bf16[4,384,512]{2,1,0:T(8,128)(2,1)} collective-permute-done((bf16[4,384,512]{2,1,0:T(8,128)(2,1)S(1)}, bf16[4,384,512]{2,1,0:T(8,128)(2,1)}, u32[]{:S(2)}, u32[]{:S(2)}) %collective-permute-start.1) | collective-permute-done | bytes 1572896 | tf_op jit(solution)/shard_map/ppermute | solution.py:265
  403.2 5.6 fusion.108.cur_sh
  414.1 6.1 collective-permute-done.2.prev_sh
  420.2 48.4 %attn_fwd.2 = (bf16[2,1152,1024]{2,1,0:T(8,128)(2,1)}, f32[4,4,1152]{2,1,0:T(4,128)}) custom-call(s32[8]{0:T(128)} %stack.34.meta, bf16[4,1152,512]{2,1,0:T(8,128)(2,1)} %get-tuple-element.31.q_ref, bf16[4,768,512]{2,1,0:T(8,128)(2,1)} %collective-permute-done.prev_own, bf16[4,768,512]{2,1,0:T(8,128)(2,1)} %constant_dynamic-slice_fusion.8.cur_own, ...), custom_call_target="tpu_custom_call" | custom-call | flops 28991029248 | bytes 28311552 | tf_op jit(solution)/shard_map/attn_fwd/pallas_call | solution.py:183
  468.6 17.9 %fusion.27 = (f32[1152]{0:T(1024)S(1)}, bf16[1152,2560]{1,0:T(8,128)(2,1)S(1)}) fusion(bf16[2,1152,1024]{2,1,0:T(8,128)(2,1)} %get-tuple-element.33, bf16[2,1024,2560]{2,1,0:T(8,128)(2,1)} %bitcast.203, bf16[4608,2560]{1,0:T(8,128)(2,1)} %bitcast.172, s32[]{:T(128)S(6)} %select_n.131), kind=kOutput, calls=%fused_computation.43 | convolution fusion | flops 12103187456 | bytes 27005444 | tf_op jit(solution)/shard_map/crh,chd->rd/dot_general | solution.py:44
  492.9 17.1 fusion.74
  520.2 28.8 %collective-permute-done.4 = bf16[4,384,512]{2,1,0:T(8,128)(2,1)} collective-permute-done((bf16[4,384,512]{2,1,0:T(8,128)(2,1)S(1)}, bf16[4,384,512]{2,1,0:T(8,128)(2,1)}, u32[]{:S(2)}, u32[]{:S(2)}) %collective-permute-start.4) | collective-permute-done | bytes 1572896 | tf_op jit(solution)/shard_map/ppermute | solution.py:265
  556.6 5.7 constant_dynamic-slice_fusion.4
  562.3 17.0 fusion.89.q_ref
  579.3 45.6 %attn_fwd.3 = (bf16[2,1152,1024]{2,1,0:T(8,128)(2,1)}, f32[4,4,1152]{2,1,0:T(4,128)}) custom-call(s32[8]{0:T(128)} %stack.34.meta, bf16[4,1152,512]{2,1,0:T(8,128)(2,1)} %fusion.89.q_ref, bf16[4,768,512]{2,1,0:T(8,128)(2,1)} %collective-permute-done.3.prev_own, bf16[4,768,512]{2,1,0:T(8,128)(2,1)} %copy-done.8, ...), custom_call_target="tpu_custom_call" | custom-call | flops 28991029248 | bytes 28311552 | tf_op jit(solution)/shard_map/attn_fwd/pallas_call | solution.py:183
  624.9 19.4 %fusion.28 = bf16[1152,2560]{1,0:T(8,128)(2,1)} fusion(bf16[1152,2560]{1,0:T(8,128)(2,1)} %copy-done.5, bf16[2,1152,1024]{2,1,0:T(8,128)(2,1)} %get-tuple-element.34, bf16[2,1024,2560]{2,1,0:T(8,128)(2,1)} %bitcast.205), kind=kOutput, calls=%fused_computation.44 | convolution fusion | flops 12094341120 | bytes 27000832 | tf_op jit(solution)/shard_map/crh,chd->rd/dot_general | solution.py:44
  644.3 18.4 %fusion.86.g_ref = bf16[2,1152,1024]{2,1,0:T(8,128)(2,1)} fusion(bf16[2,1024,2560]{2,1,0:T(8,128)(2,1)} %bitcast.206, bf16[1152,2560]{1,0:T(8,128)(2,1)} %constant_dynamic-slice_fusion.4), kind=kOutput, calls=%fused_computation.108 | convolution fusion | flops 12081954816 | bytes 21102592 | tf_op jit(solution)/shard_map/rd,chd->crh/dot_general | solution.py:44
  662.7 79.1 %attn_bwd.2 = (bf16[4,1152,512]{2,1,0:T(8,128)(2,1)}, bf16[4,768,512]{2,1,0:T(8,128)(2,1)}, f32[4,768,512]{2,1,0:T(8,128)}, bf16[4,768,512]{2,1,0:T(8,128)(2,1)}, f32[4,768,512]{2,1,0:T(8,128)}) custom-call(s32[8]{0:T(128)} %stack.34.meta, bf16[4,1152,512]{2,1,0:T(8,128)(2,1)} %fusion.89.q_ref, bf16[4,768,512]{2,1,0:T(8,128)(2,1)} %collective-permute-done.3.prev_own, ...), custom_call_target="tpu_custom_call" | custom-call | flops 72477573120 | bytes 47185920 | tf_op jit(solution)/shard_map/attn_bwd/pallas_call | solution.py:203
  741.8 12.2 convolution_bitcast_fusion.7
  754.0 12.4 fusion.118
  770.4 12.4 bitcast_add_fusion.1
  782.8 11.2 copy.75
  797.3 5.3 collective-permute-done.6
  802.6 5.4 convert_add_fusion.3
  814.7 64.2 %collective-permute-done.7 = bf16[4,384,512]{2,1,0:T(8,128)(2,1)S(1)} collective-permute-done((bf16[4,384,512]{2,1,0:T(8,128)(2,1)S(1)}, bf16[4,384,512]{2,1,0:T(8,128)(2,1)S(1)}, u32[]{:S(2)}, u32[]{:S(2)}) %collective-permute-start.7) | collective-permute-done | bytes 1572896 | tf_op jit(solution)/shard_map/ppermute | solution.py:265
  879.5 5.5 fusion.82
  885.1 9.9 convolution_bitcast_fusion.6
  895.0 16.5 collective-permute-done.22
  911.5 13.9 bitcast_add_fusion
  925.4 12.1 copy.78
  937.5 21.2 %convolution_bitcast_fusion.2 = f32[1152,2560]{1,0:T(8,128)} fusion(bf16[4,1152,512]{2,1,0:T(8,128)(2,1)} %copy-done.6, bf16[8,2560,512]{2,1,0:T(8,128)(2,1)} %all-gather.33.cloned.1.call-done), kind=kOutput, calls=%fused_computation.25 | convolution fusion | flops 12079595520 | bytes 27000832 | tf_op jit(solution)/shard_map/trh,tdh->rd/dot_general | solution.py:44
  958.7 22.8 %fusion.26 = (f32[2560]{0:T(1024)}, f32[1152]{0:T(1024)S(1)}, bf16[1152,2560]{1,0:T(8,128)(2,1)}) fusion(bf16[1152,2560]{1,0:T(8,128)(2,1)} %copy-done.5, f32[1152]{0:T(1024)S(1)} %copy-done.18, f32[2560]{0:T(1024)S(1)} %copy-done.16, f32[1152,2560]{1,0:T(8,128)} %convolution_bitcast_fusion.2, bf16[4,1152,512]{2,1,0:T(8,128)(2,1)} %get-tuple-element.37, ...), kind=kOutput, calls=%fused_computation.42 | convolution fusion | flops 12109083648 | bytes 38827008 | tf_op jit(solution)/shard_map/trh,tdh->rd/dot_general | solution.py:44
  981.6 8.7 fusion.19
  990.3 12.4 fusion.127
  1002.7 18.5 %fusion.83.g_ref = bf16[2,1152,1024]{2,1,0:T(8,128)(2,1)} fusion(bf16[2,1024,2560]{2,1,0:T(8,128)(2,1)} %bitcast.204, bf16[1152,2560]{1,0:T(8,128)(2,1)} %copy-done.2), kind=kOutput, calls=%fused_computation.107 | convolution fusion | flops 12081954816 | bytes 21102592 | tf_op jit(solution)/shard_map/rd,chd->crh/dot_general | solution.py:44
  1021.2 12.4 convolution_add_fusion
  1034.3 81.6 %attn_bwd.3 = (bf16[4,1152,512]{2,1,0:T(8,128)(2,1)}, bf16[4,768,512]{2,1,0:T(8,128)(2,1)}, f32[4,768,512]{2,1,0:T(8,128)}, bf16[4,768,512]{2,1,0:T(8,128)(2,1)}, f32[4,768,512]{2,1,0:T(8,128)}) custom-call(s32[8]{0:T(128)} %stack.34.meta, bf16[4,1152,512]{2,1,0:T(8,128)(2,1)} %get-tuple-element.31.q_ref, ...), custom_call_target="tpu_custom_call" | custom-call | flops 72477573120 | bytes 47185920 | tf_op jit(solution)/shard_map/attn_bwd/pallas_call | solution.py:203
  1118.5 5.7 collective-permute-done.9
  1134.8 54.4 %collective-permute-done.10 = bf16[4,384,512]{2,1,0:T(8,128)(2,1)S(1)} collective-permute-done((bf16[4,384,512]{2,1,0:T(8,128)(2,1)S(1)}, bf16[4,384,512]{2,1,0:T(8,128)(2,1)S(1)}, u32[]{:S(2)}, u32[]{:S(2)}) %collective-permute-start.10) | collective-permute-done | bytes 1572896 | tf_op jit(solution)/shard_map/ppermute | solution.py:265
  1189.7 6.7 fusion.80.gkv_ref
  1196.4 18.7 %shard_map.239 = (bf16[4,1152,512]{2,1,0:T(8,128)(2,1)}, bf16[4,1152,512]{2,1,0:T(8,128)(2,1)}) custom-call(bf16[4,1152,512]{2,1,0:T(8,128)(2,1)} %fusion.95.q_ref, bf16[4,1152,512]{2,1,0:T(8,128)(2,1)} %fusion.92.kv_ref, f32[1152,256]{1,0:T(8,128)} %get-tuple-element.75.cos_ref, f32[1152,256]{1,0:T(8,128)} %get-tuple-element.74.sin_ref, ...), custom_call_target="tpu_custom_call" | custom-call | flops 47185920 | bytes 23592960 | tf_op jit(solution)/shard_map/pallas_call | solution.py:87
  1215.1 19.3 %convolution_bitcast_fusion.1 = f32[1152,2560]{1,0:T(8,128)} fusion(bf16[4,1152,512]{2,1,0:T(8,128)(2,1)} %get-tuple-element.48, bf16[8,2560,512]{2,1,0:T(8,128)(2,1)} %all-gather.25.cloned.1.call-done), kind=kOutput, calls=%fused_computation.24 | convolution fusion | flops 12079595520 | bytes 27000832 | tf_op jit(solution)/shard_map/trh,tdh->rd/dot_general | solution.py:44
  1234.4 22.8 %fusion.21 = (f32[2560]{0:T(1024)S(1)}, f32[1152]{0:T(1024)S(1)}, bf16[1152,2560]{1,0:T(8,128)(2,1)}) fusion(f32[1152]{0:T(1024)S(1)} %add_rsqrt_fusion.1, bf16[4608,2560]{1,0:T(8,128)(2,1)} %bitcast.174, s32[]{:T(128)S(6)} %select_n.131, f32[2560]{0:T(1024)S(1)} %copy-done.14, f32[1152,2560]{1,0:T(8,128)} %convolution_bitcast_fusion.1, ...), kind=kOutput, calls=%fused_computation.37 | convolution fusion | flops 12109083648 | bytes 38827012 | tf_op jit(solution)/shard_map/trh,tdh->rd/dot_general | solution.py:44
  1257.1 11.6 fusion.16
  1279.5 50.9 %collective-permute-done.23 = bf16[2,1152,256]{2,1,0:T(8,128)(2,1)} collective-permute-done((bf16[2,1152,256]{2,1,0:T(8,128)(2,1)}, bf16[2,1152,256]{2,1,0:T(8,128)(2,1)}, u32[]{:S(2)}, u32[]{:S(2)}) %collective-permute-start.23) | collective-permute-done | bytes 1179680 | tf_op jit(solution)/shard_map/ppermute | solution.py:289
  1334.0 44.4 %collective-permute-done.25 = bf16[2,1152,256]{2,1,0:T(8,128)(2,1)S(1)} collective-permute-done((bf16[2,1152,256]{2,1,0:T(8,128)(2,1)}, bf16[2,1152,256]{2,1,0:T(8,128)(2,1)S(1)}, u32[]{:S(2)}, u32[]{:S(2)}) %collective-permute-start.25) | collective-permute-done | bytes 1179680 | tf_op jit(solution)/shard_map/ppermute | solution.py:289
  1379.5 13.6 fusion.124
  1398.3 13.4 fusion.98
  1430.3 6.9 collective-permute-done.16
  1439.8 14.3 collective-permute-done.17
  1455.2 28.4 %collective-permute-done.18 = bf16[1152,512]{1,0:T(8,128)(2,1)S(1)} collective-permute-done((bf16[1152,512]{1,0:T(8,128)(2,1)}, bf16[1152,512]{1,0:T(8,128)(2,1)S(1)}, u32[]{:S(2)}, u32[]{:S(2)}) %collective-permute-start.18) | collective-permute-done | bytes 1179680 | tf_op jit(solution)/shard_map/ppermute | solution.py:289
  1484.8 9.6 fusion.37
  1494.4 38.7 %collective-permute-done.12 = bf16[1152,512]{1,0:T(8,128)(2,1)S(1)} collective-permute-done((bf16[1152,512]{1,0:T(8,128)(2,1)}, bf16[1152,512]{1,0:T(8,128)(2,1)S(1)}, u32[]{:S(2)}, u32[]{:S(2)}) %collective-permute-start.12) | collective-permute-done | bytes 1179680 | tf_op jit(solution)/shard_map/ppermute | solution.py:289
  1535.4 41.7 %collective-permute-done.14 = bf16[1152,512]{1,0:T(8,128)(2,1)S(1)} collective-permute-done((bf16[1152,512]{1,0:T(8,128)(2,1)}, bf16[1152,512]{1,0:T(8,128)(2,1)S(1)}, u32[]{:S(2)}, u32[]{:S(2)}) %collective-permute-start.14) | collective-permute-done | bytes 1179680 | tf_op jit(solution)/shard_map/ppermute | solution.py:289
  1578.2 9.6 fusion.39
  1587.8 23.9 %psum.7 = bf16[2,2560]{1,0:T(2,128)(2,1)S(1)} all-reduce(f32[2,2560]{1,0:T(2,128)S(1)} %pad_maximum_fusion), channel_id=1, replica_groups=mesh['tp'=4,'cp'=2] {'tp','cp'}, use_global_device_ids=true, to_apply=%region_7.8 | all-reduce | flops 5120 | bytes 30720 | tf_op jit(solution)/shard_map/psum | solution.py:384
  1612.3 10.9 fusion.109
  1624.4 11.9 fusion.112
  1645.3 65.8 %all-gather.21.cloned.1.call-done = bf16[4608,2560]{1,0:T(8,128)(2,1)} async-done(((bf16[1152,2560]{1,0:T(8,128)(2,1)}), bf16[4608,2560]{1,0:T(8,128)(2,1)}) %all-gather.21.cloned.1.call-update) | async-done | bytes 23592976 | tf_op jit(solution)/shard_map/all_gather | solution.py:304
  1711.1 20.8 %copy.111 = bf16[6,768,2560]{2,1,0:T(8,128)(2,1)} copy(bf16[6,768,2560]{2,1,0:T(8,128)(2,1)} %bitcast.189) | data formatting | bytes 47185920
  1734.4 8.7 copy.112
  (215 shorter events, 145.4 us)
Async XLA Ops:
  7.2 107.2 %all-gather.23.cloned.1.call-start = ((), (), s32[]{:S(2)}) async-start(), calls=%async_computation.8 | async-start | bytes 13107200 | tf_op jit(solution)/shard_map/all_gather | solution.py:254
  12.1 160.4 %all-gather.27.cloned.1.call-start = ((), (), s32[]{:S(2)}) async-start(), calls=%async_computation.10 | async-start | bytes 6553600 | tf_op jit(solution)/shard_map/all_gather | solution.py:254
  13.3 261.0 %all-gather.31.cloned.1.call-start = ((), (), s32[]{:S(2)}) async-start(), calls=%async_computation.12 | async-start | bytes 13107200 | tf_op jit(solution)/shard_map/all_gather | solution.py:254
  18.1 295.8 %all-gather.25.cloned.1.call-start = ((), (), s32[]{:S(2)}) async-start(), calls=%async_computation.9 | async-start | bytes 31457280 | tf_op jit(solution)/shard_map/all_gather | solution.py:255
  114.4 299.6 %all-gather.35.cloned.1.call-start = ((), (), s32[]{:S(2)}) async-start(), calls=%async_computation.14 | async-start | bytes 6553600 | tf_op jit(solution)/shard_map/all_gather | solution.py:254
  117.3 351.3 %all-gather.29.cloned.1.call-start = ((), (), s32[]{:S(2)}) async-start(), calls=%async_computation.11 | async-start | bytes 15728640 | tf_op jit(solution)/shard_map/all_gather | solution.py:255
  172.6 320.3 %all-gather.33.cloned.1.call-start = ((), (), s32[]{:S(2)}) async-start(), calls=%async_computation.13 | async-start | bytes 31457280 | tf_op jit(solution)/shard_map/all_gather | solution.py:255
  274.3 350.6 %all-gather.37.cloned.1.call-start = ((), (), s32[]{:S(2)}) async-start(), calls=%async_computation.15 | async-start | bytes 15728640 | tf_op jit(solution)/shard_map/all_gather | solution.py:255
  275.0 16.8 copy-start.13
  367.7 35.6 %collective-permute-start.1 = (bf16[4,384,512]{2,1,0:T(8,128)(2,1)S(1)}, bf16[4,384,512]{2,1,0:T(8,128)(2,1)}, u32[]{:S(2)}, u32[]{:S(2)}) collective-permute-start(bf16[4,384,512]{2,1,0:T(8,128)(2,1)S(1)} %constant_dynamic-slice_fusion.7), channel_id=1, source_target_pairs={{0,2},{2,0},{4,6},{6,4},{1,3},{3,1},{5,7},{7,5}} | collective-permute-start | bytes 4718600 | tf_op jit(solution)/shard_map/ppermute | solution.py:265
  372.6 39.6 %copy-start.22 = (s32[768]{0:T(1024)S(1)}, s32[768]{0:T(1024)}, u32[]{:S(2)}) copy-start(s32[768]{0:T(1024)} %param.16) | copy-start | bytes 9220
  372.6 40.1 %copy-start.21 = (bf16[2560]{0:T(1024)(128)(2,1)S(1)}, bf16[2560]{0:T(1024)(128)(2,1)}, u32[]{:S(2)}) copy-start(bf16[2560]{0:T(1024)(128)(2,1)} %param.24) | copy-start | bytes 15364
  372.6 41.5 %collective-permute-start = (bf16[4,768,512]{2,1,0:T(8,128)(2,1)}, bf16[4,768,512]{2,1,0:T(8,128)(2,1)}, u32[]{:S(2)}, u32[]{:S(2)}) collective-permute-start(bf16[4,768,512]{2,1,0:T(8,128)(2,1)} %constant_dynamic-slice_fusion.8.cur_own), channel_id=1, source_target_pairs={{0,1},{2,3},{4,5},{6,7}} | collective-permute-start | bytes 9437192 | tf_op jit(solution)/shard_map/ppermute | solution.py:270
  408.8 11.4 collective-permute-start.2
  412.7 73.9 %copy-start.15 = (f32[2560]{0:T(1024)}, f32[2560]{0:T(1024)S(1)}, u32[]{:S(2)}) copy-start(f32[2560]{0:T(1024)S(1)} %convert_element_type.177) | copy-start | bytes 30724
  414.1 1222.3 %reduce-scatter.6.cloned.1.call-start = ((), (), s32[]{:S(2)}) async-start(), calls=%async_computation.6 | async-start | bytes 13107200 | tf_op jit(solution)/shard_map/reduce_scatter | solution.py:361
  512.2 36.8 %collective-permute-start.4 = (bf16[4,384,512]{2,1,0:T(8,128)(2,1)S(1)}, bf16[4,384,512]{2,1,0:T(8,128)(2,1)}, u32[]{:S(2)}, u32[]{:S(2)}) collective-permute-start(bf16[4,384,512]{2,1,0:T(8,128)(2,1)S(1)} %dynamic-slice_bitcast_fusion.1), channel_id=1, source_target_pairs={{0,2},{2,0},{4,6},{6,4},{1,3},{3,1},{5,7},{7,5}} | collective-permute-start | bytes 4718600 | tf_op jit(solution)/shard_map/ppermute | solution.py:265
  516.5 45.8 %copy-start.8 = (bf16[4,768,512]{2,1,0:T(8,128)(2,1)}, bf16[4,768,512]{2,1,0:T(8,128)(2,1)S(1)}, u32[]{:S(2)}) copy-start(bf16[4,768,512]{2,1,0:T(8,128)(2,1)S(1)} %dynamic-slice_bitcast_fusion.cur_own) | copy-start | bytes 9437188
  516.5 62.8 %collective-permute-start.3 = (bf16[4,768,512]{2,1,0:T(8,128)(2,1)S(1)}, bf16[4,768,512]{2,1,0:T(8,128)(2,1)}, u32[]{:S(2)}, u32[]{:S(2)}) collective-permute-start(bf16[4,768,512]{2,1,0:T(8,128)(2,1)S(1)} %dynamic-slice_bitcast_fusion.cur_own), channel_id=1, source_target_pairs={{0,1},{2,3},{4,5},{6,7}} | collective-permute-start | bytes 9437192 | tf_op jit(solution)/shard_map/ppermute | solution.py:270
  549.0 13.3 slice-start.8
  553.5 25.8 %collective-permute-start.5 = (bf16[4,768,512]{2,1,0:T(8,128)(2,1)S(1)}, bf16[4,768,512]{2,1,0:T(8,128)(2,1)}, u32[]{:S(2)}, u32[]{:S(2)}) collective-permute-start(bf16[4,768,512]{2,1,0:T(8,128)(2,1)S(1)} %fusion.106.cur_sh), channel_id=1, source_target_pairs={{0,1},{2,3},{4,5},{6,7}} | collective-permute-start | bytes 9437192 | tf_op jit(solution)/shard_map/ppermute | solution.py:273
  753.9 16.5 collective-permute-start.21
  794.1 845.2 %all-gather.19.cloned.1.call-start = ((), (), s32[]{:S(2)}) async-start(), calls=%async_computation.3 | async-start | bytes 29491200 | tf_op jit(solution)/shard_map/all_gather | solution.py:304
  794.6 844.6 %reduce-scatter.8.cloned.1.call-start = ((), (), s32[]{:S(2)}) async-start(), calls=%async_computation.7 | async-start | bytes 13107200 | tf_op jit(solution)/shard_map/reduce_scatter | solution.py:361
  794.7 7.9 collective-permute-start.6
  796.0 13.6 collective-permute-start.8
  808.2 70.8 %collective-permute-start.7 = (bf16[4,384,512]{2,1,0:T(8,128)(2,1)S(1)}, bf16[4,384,512]{2,1,0:T(8,128)(2,1)S(1)}, u32[]{:S(2)}, u32[]{:S(2)}) collective-permute-start(bf16[4,384,512]{2,1,0:T(8,128)(2,1)S(1)} %dynamic-slice_convert_fusion.1), channel_id=1, source_target_pairs={{0,2},{2,0},{4,6},{6,4},{1,3},{3,1},{5,7},{7,5}} | collective-permute-start | bytes 4718600 | tf_op jit(solution)/shard_map/ppermute | solution.py:265
  885.0 9.9 copy-start.6
  895.0 16.5 collective-permute-start.22
  937.5 21.3 %copy-start.16 = (f32[2560]{0:T(1024)S(1)}, f32[2560]{0:T(1024)}, u32[]{:S(2)}) copy-start(f32[2560]{0:T(1024)} %copy-done.15) | copy-start | bytes 30724
  937.5 21.2 %copy-start.18 = (f32[1152]{0:T(1024)S(1)}, f32[1152]{0:T(1024)}, u32[]{:S(2)}) copy-start(f32[1152]{0:T(1024)} %copy-done.17) | copy-start | bytes 13828
  937.5 703.7 %reduce-scatter.4.cloned.1.call-start = ((), (), s32[]{:S(2)}) async-start(), calls=%async_computation.5 | async-start | bytes 13107200 | tf_op jit(solution)/shard_map/reduce_scatter | solution.py:371
  990.2 12.5 copy-start.2
  990.3 31.0 %slice-start.12 = ((s8[4718592]{0:T(1024)(128)(4,1)}), s8[524288]{0:T(1024)(128)(4,1)S(1)}, s32[]{:S(2)}) async-start(s8[4718592]{0:T(1024)(128)(4,1)} %bitcast.201), calls=%async_computation.28 | async-start | bytes 1048576
  1002.7 18.5 %collective-permute-start.20 = (f32[1024,2560]{1,0:T(8,128)}, f32[1024,2560]{1,0:T(8,128)}, u32[]{:S(2)}, u32[]{:S(2)}) collective-permute-start(f32[1024,2560]{1,0:T(8,128)} %fusion.127), channel_id=1, source_target_pairs={{0,1},{1,0},{2,3},{3,2},{4,5},{5,4},{6,7},{7,6}} | collective-permute-start | bytes 31457288 | tf_op jit(solution)/shard_map/ppermute | solution.py:307
  1002.7 18.5 %copy-start.3 = (bf16[1152,2560]{1,0:T(8,128)(2,1)S(1)}, bf16[1152,2560]{1,0:T(8,128)(2,1)}, u32[]{:S(2)}) copy-start(bf16[1152,2560]{1,0:T(8,128)(2,1)} %copy-done.2) | copy-start | bytes 17694724
  1002.7 18.5 %slice-start.13 = ((s8[4718592]{0:T(1024)(128)(4,1)}), s8[4194304]{0:T(1024)(128)(4,1)S(1)}, s32[]{:S(2)}) async-start(s8[4718592]{0:T(1024)(128)(4,1)} %bitcast.201), calls=%async_computation.29 | async-start | bytes 8388608
  1033.7 677.4 %all-gather.21.cloned.1.call-start = ((), (), s32[]{:S(2)}) async-start(), calls=%async_computation.4 | async-start | bytes 29491200 | tf_op jit(solution)/shard_map/all_gather | solution.py:304
  1115.9 8.3 collective-permute-start.9
  1117.2 16.4 collective-permute-start.11
  1124.2 9.4 slice-start.6
  1124.2 9.4 slice-start.7
  1128.7 60.5 %collective-permute-start.10 = (bf16[4,384,512]{2,1,0:T(8,128)(2,1)S(1)}, bf16[4,384,512]{2,1,0:T(8,128)(2,1)S(1)}, u32[]{:S(2)}, u32[]{:S(2)}) collective-permute-start(bf16[4,384,512]{2,1,0:T(8,128)(2,1)S(1)} %dynamic-slice_convert_fusion), channel_id=1, source_target_pairs={{0,2},{2,0},{4,6},{6,4},{1,3},{3,1},{5,7},{7,5}} | collective-permute-start | bytes 4718600 | tf_op jit(solution)/shard_map/ppermute | solution.py:265
  1215.1 19.3 %copy-start.14 = (f32[2560]{0:T(1024)S(1)}, f32[2560]{0:T(1024)}, u32[]{:S(2)}) copy-start(f32[2560]{0:T(1024)} %copy-done.13) | copy-start | bytes 30724
  1276.1 54.4 %collective-permute-start.23 = (bf16[2,1152,256]{2,1,0:T(8,128)(2,1)}, bf16[2,1152,256]{2,1,0:T(8,128)(2,1)}, u32[]{:S(2)}, u32[]{:S(2)}) collective-permute-start(bf16[2,1152,256]{2,1,0:T(8,128)(2,1)} %get-tuple-element.58), channel_id=1, source_target_pairs={{0,2},{2,0},{4,6},{6,4},{1,3},{3,1},{5,7},{7,5}} | collective-permute-start | bytes 3538952 | tf_op jit(solution)/shard_map/ppermute | solution.py:289
  1276.6 56.3 %collective-permute-start.24 = (bf16[2,1152,256]{2,1,0:T(8,128)(2,1)}, bf16[2,1152,256]{2,1,0:T(8,128)(2,1)S(1)}, u32[]{:S(2)}, u32[]{:S(2)}) collective-permute-start(bf16[2,1152,256]{2,1,0:T(8,128)(2,1)} %get-tuple-element.57), channel_id=1, source_target_pairs={{0,4},{2,6},{4,0},{6,2},{1,5},{3,7},{5,1},{7,3}} | collective-permute-start | bytes 3538952 | tf_op jit(solution)/shard_map/ppermute | solution.py:289
  1278.2 100.2 %collective-permute-start.25 = (bf16[2,1152,256]{2,1,0:T(8,128)(2,1)}, bf16[2,1152,256]{2,1,0:T(8,128)(2,1)S(1)}, u32[]{:S(2)}, u32[]{:S(2)}) collective-permute-start(bf16[2,1152,256]{2,1,0:T(8,128)(2,1)} %get-tuple-element.56), channel_id=1, source_target_pairs={{0,6},{2,4},{4,2},{6,0},{1,7},{3,5},{5,3},{7,1}} | collective-permute-start | bytes 3538952 | tf_op jit(solution)/shard_map/ppermute | solution.py:289
  1393.2 5.1 collective-permute-start.26
  1396.8 14.9 copy-start.19
  1396.8 40.3 %collective-permute-start.16 = (bf16[1152,512]{1,0:T(8,128)(2,1)S(1)}, bf16[1152,512]{1,0:T(8,128)(2,1)S(1)}, u32[]{:S(2)}, u32[]{:S(2)}) collective-permute-start(bf16[1152,512]{1,0:T(8,128)(2,1)S(1)} %get-tuple-element.62), channel_id=1, source_target_pairs={{0,2},{2,0},{4,6},{6,4},{1,3},{3,1},{5,7},{7,5}} | collective-permute-start | bytes 3538952 | tf_op jit(solution)/shard_map/ppermute | solution.py:289
  1398.3 86.4 %slice-start = ((s8[23592960]{0:T(1024)(128)(4,1)}), s8[2621440]{0:T(1024)(128)(4,1)S(1)}, s32[]{:S(2)}) async-start(s8[23592960]{0:T(1024)(128)(4,1)} %bitcast.185), calls=%async_computation.16 | async-start | bytes 5242880
  1398.3 86.4 %slice-start.1 = ((s8[23592960]{0:T(1024)(128)(4,1)}), s8[4194304]{0:T(1024)(128)(4,1)S(1)}, s32[]{:S(2)}) async-start(s8[23592960]{0:T(1024)(128)(4,1)} %bitcast.185), calls=%async_computation.17 | async-start | bytes 8388608
  1398.3 86.4 %slice-start.2 = ((s8[23592960]{0:T(1024)(128)(4,1)}), s8[4194304]{0:T(1024)(128)(4,1)S(1)}, s32[]{:S(2)}) async-start(s8[23592960]{0:T(1024)(128)(4,1)} %bitcast.185), calls=%async_computation.18 | async-start | bytes 8388608
  1398.3 86.4 %slice-start.3 = ((s8[23592960]{0:T(1024)(128)(4,1)}), s8[4194304]{0:T(1024)(128)(4,1)S(1)}, s32[]{:S(2)}) async-start(s8[23592960]{0:T(1024)(128)(4,1)} %bitcast.185), calls=%async_computation.19 | async-start | bytes 8388608
  1411.7 42.4 %collective-permute-start.17 = (bf16[1152,512]{1,0:T(8,128)(2,1)}, bf16[1152,512]{1,0:T(8,128)(2,1)S(1)}, u32[]{:S(2)}, u32[]{:S(2)}) collective-permute-start(bf16[1152,512]{1,0:T(8,128)(2,1)} %get-tuple-element.61), channel_id=1, source_target_pairs={{0,4},{2,6},{4,0},{6,2},{1,5},{3,7},{5,1},{7,3}} | collective-permute-start | bytes 3538952 | tf_op jit(solution)/shard_map/ppermute | solution.py:289
  1412.2 71.4 %collective-permute-start.18 = (bf16[1152,512]{1,0:T(8,128)(2,1)}, bf16[1152,512]{1,0:T(8,128)(2,1)S(1)}, u32[]{:S(2)}, u32[]{:S(2)}) collective-permute-start(bf16[1152,512]{1,0:T(8,128)(2,1)} %get-tuple-element.60), channel_id=1, source_target_pairs={{0,6},{2,4},{4,2},{6,0},{1,7},{3,5},{5,3},{7,1}} | collective-permute-start | bytes 3538952 | tf_op jit(solution)/shard_map/ppermute | solution.py:289
  1417.6 115.5 %collective-permute-start.12 = (bf16[1152,512]{1,0:T(8,128)(2,1)}, bf16[1152,512]{1,0:T(8,128)(2,1)S(1)}, u32[]{:S(2)}, u32[]{:S(2)}) collective-permute-start(bf16[1152,512]{1,0:T(8,128)(2,1)} %get-tuple-element.65), channel_id=1, source_target_pairs={{0,2},{2,0},{4,6},{6,4},{1,3},{3,1},{5,7},{7,5}} | collective-permute-start | bytes 3538952 | tf_op jit(solution)/shard_map/ppermute | solution.py:289
  1419.0 115.2 %collective-permute-start.13 = (bf16[1152,512]{1,0:T(8,128)(2,1)}, bf16[1152,512]{1,0:T(8,128)(2,1)S(1)}, u32[]{:S(2)}, u32[]{:S(2)}) collective-permute-start(bf16[1152,512]{1,0:T(8,128)(2,1)} %get-tuple-element.64), channel_id=1, source_target_pairs={{0,4},{2,6},{4,0},{6,2},{1,5},{3,7},{5,1},{7,3}} | collective-permute-start | bytes 3538952 | tf_op jit(solution)/shard_map/ppermute | solution.py:289
  1419.5 65.2 %slice-start.4 = ((s8[23592960]{0:T(1024)(128)(4,1)}), s8[4194304]{0:T(1024)(128)(4,1)S(1)}, s32[]{:S(2)}) async-start(s8[23592960]{0:T(1024)(128)(4,1)} %bitcast.185), calls=%async_computation.20 | async-start | bytes 8388608
  1424.9 59.9 %slice-start.5 = ((s8[23592960]{0:T(1024)(128)(4,1)}), s8[4194304]{0:T(1024)(128)(4,1)S(1)}, s32[]{:S(2)}) async-start(s8[23592960]{0:T(1024)(128)(4,1)} %bitcast.185), calls=%async_computation.21 | async-start | bytes 8388608
  1437.1 140.0 %collective-permute-start.14 = (bf16[1152,512]{1,0:T(8,128)(2,1)}, bf16[1152,512]{1,0:T(8,128)(2,1)S(1)}, u32[]{:S(2)}, u32[]{:S(2)}) collective-permute-start(bf16[1152,512]{1,0:T(8,128)(2,1)} %get-tuple-element.63), channel_id=1, source_target_pairs={{0,6},{2,4},{4,2},{6,0},{1,7},{3,5},{5,3},{7,1}} | collective-permute-start | bytes 3538952 | tf_op jit(solution)/shard_map/ppermute | solution.py:289
  1494.4 117.9 %collective-permute-start.19 = (f32[1280,512]{1,0:T(8,128)}, f32[1280,512]{1,0:T(8,128)}, u32[]{:S(2)}, u32[]{:S(2)}) collective-permute-start(f32[1280,512]{1,0:T(8,128)} %fusion.37), channel_id=1, source_target_pairs={{0,1},{1,0},{2,3},{3,2},{4,5},{5,4},{6,7},{7,6}} | collective-permute-start | bytes 7864328 | tf_op jit(solution)/shard_map/ppermute | solution.py:307
  1587.8 36.7 %collective-permute-start.15 = (f32[1280,512]{1,0:T(8,128)}, f32[1280,512]{1,0:T(8,128)}, u32[]{:S(2)}, u32[]{:S(2)}) collective-permute-start(f32[1280,512]{1,0:T(8,128)} %fusion.39), channel_id=1, source_target_pairs={{0,1},{1,0},{2,3},{3,2},{4,5},{5,4},{6,7},{7,6}} | collective-permute-start | bytes 7864328 | tf_op jit(solution)/shard_map/ppermute | solution.py:307
  1711.1 23.3 %copy-start.4 = (bf16[4608,2560]{1,0:T(8,128)(2,1)S(1)}, bf16[4608,2560]{1,0:T(8,128)(2,1)}, u32[]{:S(2)}) copy-start(bf16[4608,2560]{1,0:T(8,128)(2,1)} %all-gather.21.cloned.1.call-done) | copy-start | bytes 70778880
  (13 other events, 55.7 us)
Sparse Core Ops, SparseCore 0:
  12.2 102.1 all-gather.22
  116.8 55.7 all-gather.26
  174.9 99.3 all-gather.30
  275.7 32.8 all-gather.24
  310.8 56.9 all-gather.34
  369.1 19.8 all-gather.28
  390.5 38.3 all-gather.32
  430.5 21.2 all-gather.36
  794.2 131.4 reduce-scatter.5
  927.4 213.7 all-gather.18
  1144.2 117.8 reduce-scatter.7
  1265.0 160.3 reduce-scatter.3
  1427.7 283.2 all-gather.20

commit v2 on v1

v2 whole, which is shorter than its diff:
```python
import functools

import jax
import jax.numpy as jnp
from jax import lax
from jax.experimental import pallas as pl
from jax.experimental.pallas import tpu as pltpu
from jax.experimental.layout import Layout, with_layout_constraint
from jax.sharding import PartitionSpec as P


CHUNK = 8192
NORM_EPS = 1e-5
QK_EPS = 1e-6
TEMP_SCALE = 0.1
CHUNK_BITS = 13
HEAD = 256
TILE = 384
NEG_BIG = -1e30
F32 = jnp.float32
BF16 = jnp.bfloat16


def rms_norm(act, gamma):
    act_wide = act.astype(F32)
    inv_rms = lax.rsqrt(jnp.mean(act_wide * act_wide, axis=-1, keepdims=True) + NORM_EPS)
    return (act_wide * inv_rms * gamma.astype(F32)).astype(BF16)


def norm_backward(act, gamma, grad_out):
    act_wide = act.astype(F32)
    inv_rms = lax.rsqrt(jnp.mean(act_wide * act_wide, axis=-1, keepdims=True) + NORM_EPS)
    x_hat = act_wide * inv_rms
    grad_gain = jnp.sum(grad_out * x_hat, axis=0)
    grad_hat = grad_out * gamma.astype(F32)
    grad_act = inv_rms * (grad_hat - x_hat * jnp.mean(grad_hat * x_hat, axis=-1, keepdims=True))
    return grad_act, grad_gain


def value_a11(positions):
    return jnp.log(((positions + 1) // CHUNK).astype(F32) + 1.0) * TEMP_SCALE + 1.0


def dot_f32(spec, lhs, rhs):
    return jnp.einsum(spec, lhs, rhs, preferred_element_type=F32)


def kdot(lhs, rhs, lhs_dim, rhs_dim):
    return lax.dot_general(lhs, rhs, (((lhs_dim,), (rhs_dim,)), ((), ())), preferred_element_type=F32)


def turn(wide, cos_tab, sin_tab):
    half = HEAD // 2
    turned = jnp.concatenate([-wide[:, half:], wide[:, :half]], axis=1)
    return wide * cos_tab + turned * sin_tab


def prep_kernel(heads, src, cos_ref, sin_ref, dst):
    for head in range(heads):
        cols = pl.ds(head * HEAD, HEAD)
        wide = turn(src[0, :, cols].astype(F32), cos_ref[...], sin_ref[...])
        inv = lax.rsqrt(jnp.mean(wide * wide, axis=-1, keepdims=True) + QK_EPS)
        dst[0, :, cols] = (wide * inv).astype(BF16)
    if heads == 1:
        dst[0, :, HEAD:] = src[0, :, HEAD:]


def prep_back_kernel(heads, src, cos_ref, sin_ref, grad, dst):
    half = HEAD // 2
    for head in range(heads):
        cols = pl.ds(head * HEAD, HEAD)
        wide = turn(src[0, :, cols].astype(F32), cos_ref[...], sin_ref[...])
        inv = lax.rsqrt(jnp.mean(wide * wide, axis=-1, keepdims=True) + QK_EPS)
        hat = wide * inv
        up = grad[0, :, cols].astype(F32)
        down = inv * (up - hat * jnp.mean(up * hat, axis=-1, keepdims=True))
        side = down * sin_ref[...]
        back = jnp.concatenate([side[:, half:], -side[:, :half]], axis=1)
        dst[0, :, cols] = (down * cos_ref[...] + back).astype(BF16)
    if heads == 1:
        dst[0, :, HEAD:] = grad[0, :, HEAD:]


def prep_call(kernel, heads, val, cos_tab, sin_tab, *grads):
    groups, rows, wide = val.shape
    big = pl.BlockSpec((1, TILE, wide), lambda i, g: (g, i, 0))
    tab = pl.BlockSpec((TILE, HEAD), lambda i, g: (i, 0))
    return pl.pallas_call(
        functools.partial(kernel, heads),
        grid=(rows // TILE, groups),
        in_specs=[big, tab, tab] + [big] * len(grads),
        out_specs=big,
        out_shape=jax.ShapeDtypeStruct(val.shape, BF16),
        cost_estimate=pl.CostEstimate(flops=1000 * val.size, bytes_accessed=6 * val.size, transcendentals=0),
    )(val, cos_tab, sin_tab, *grads)


def tile_mask(meta, keys, local):
    q_at = meta[1] + pl.program_id(1) * TILE + lax.broadcasted_iota(jnp.int32, (1, TILE), 1)
    low = jnp.full((1, TILE), meta[2], jnp.int32)
    if local:
        start = lax.shift_left(lax.shift_right_logical(q_at + meta[3], CHUNK_BITS), CHUNK_BITS)
        low = jnp.maximum(low, start - meta[3])
    key = lax.broadcasted_iota(jnp.int32, (keys, 1), 0)
    return (key <= q_at) & (key >= low)


def attn_kernel(local, scale, meta, q_ref, prev, cur, *rest):
    o_ref, stat_ref = rest[-2:]
    window = jnp.concatenate([prev[0], cur[0]], axis=0)
    key = window[:, :HEAD]
    val_t = window[:, HEAD:].T
    allowed = tile_mask(meta, window.shape[0], local)
    for head in range(2):
        query = q_ref[0, :, pl.ds(head * HEAD, HEAD)]
        scores = jnp.where(allowed, kdot(key, query, 1, 1) * scale, NEG_BIG)
        top = jnp.max(scores, axis=0, keepdims=True)
        prob = jnp.exp(scores - top)
        inv = 1.0 / jnp.sum(prob, axis=0, keepdims=True)
        stat_ref[0, pl.ds(head, 1), :] = top
        stat_ref[0, pl.ds(2 + head, 1), :] = inv
        out_t = kdot(val_t, (prob * inv).astype(BF16), 1, 0)
        o_ref[head] = out_t.T.astype(BF16)


def attn_back_kernel(local, scale, meta, q_ref, prev, cur, stat_ref, g_ref, tau_ref, *rest):
    dq_ref, dprev, dcur, acc = rest[-4:]
    tile = pl.program_id(1)

    @pl.when(tile == 0)
    def _():
        acc[...] = jnp.zeros_like(acc)

    window = jnp.concatenate([prev[0], cur[0]], axis=0)
    key = window[:, :HEAD]
    val = window[:, HEAD:]
    key_t = key.T
    allowed = tile_mask(meta, window.shape[0], local)
    dkey = None
    for head in range(2):
        query = q_ref[0, :, pl.ds(head * HEAD, HEAD)]
        grad = g_ref[head]
        scores = jnp.where(allowed, kdot(key, query, 1, 1) * scale, NEG_BIG)
        prob = jnp.exp(scores - stat_ref[0, pl.ds(head, 1), :]) * stat_ref[0, pl.ds(2 + head, 1), :]
        dprob = kdot(val, grad, 1, 1)
        row_dot = jnp.sum(prob * dprob, axis=0, keepdims=True)
        dscore = (prob * (dprob - row_dot) * scale).astype(BF16)
        dval_h = kdot(prob.astype(BF16), grad, 1, 0)
        dkey_h = kdot(dscore, query, 1, 0)
        dkey, dval = (dkey_h, dval_h) if dkey is None else (dkey + dkey_h, dval + dval_h)
        dq_t = kdot(key_t, dscore, 1, 0) * tau_ref[...]
        dq_ref[0, :, pl.ds(head * HEAD, HEAD)] = dq_t.T.astype(BF16)
    acc[:, :HEAD] += dkey
    acc[:, HEAD:] += dval

    @pl.when(tile == pl.num_programs(1) - 1)
    def _():
        block = acc.shape[0] // 2
        dprev[0] = acc[:block].astype(BF16)
        dcur[0] = acc[block:]


def attn_specs(block):
    wide = 2 * HEAD
    q_spec = pl.BlockSpec((1, TILE, wide), lambda g, i, meta: (g, meta[0] + i, 0))
    w_spec = pl.BlockSpec((1, block, wide), lambda g, i, meta: (g, 0, 0))
    o_spec = pl.BlockSpec((2, TILE, HEAD), lambda g, i, meta: (0, meta[0] + i, g))
    s_spec = pl.BlockSpec((1, 4, TILE), lambda g, i, meta: (g, 0, i))
    t_spec = pl.BlockSpec((1, TILE), lambda g, i, meta: (0, meta[0] + i))
    return q_spec, w_spec, o_spec, s_spec, t_spec


def attn_forward(local, scale, meta, tiles, q_val, window, into=()):
    groups, rows, wide = q_val.shape
    block = window[0].shape[1]
    q_spec, w_spec, o_spec, s_spec, _ = attn_specs(block)
    work = groups * tiles * TILE * wide
    return pl.pallas_call(
        functools.partial(attn_kernel, local, scale),
        grid_spec=pltpu.PrefetchScalarGridSpec(
            num_scalar_prefetch=1, grid=(groups, tiles),
            in_specs=[q_spec, w_spec, w_spec] + [pl.BlockSpec(memory_space=pl.ANY)] * len(into),
            out_specs=[o_spec, s_spec]),
        out_shape=[jax.ShapeDtypeStruct((2, rows, groups * HEAD), BF16),
                   jax.ShapeDtypeStruct((groups, 4, tiles * TILE), F32)],
        input_output_aliases={4: 0} if into else {},
        compiler_params=pltpu.CompilerParams(vmem_limit_bytes=56 << 20),
        cost_estimate=pl.CostEstimate(flops=8 * work * 2 * block, bytes_accessed=12 * work, transcendentals=work * 6),
        name='attn_fwd',
    )(meta, q_val, *window, *into)


def attn_backward(local, scale, meta, tiles, q_val, window, stats, grad_out, tau, into=()):
    groups, _, wide = q_val.shape
    block = window[0].shape[1]
    q_spec, w_spec, o_spec, s_spec, t_spec = attn_specs(block)
    work = groups * tiles * TILE * wide
    return pl.pallas_call(
        functools.partial(attn_back_kernel, local, scale),
        grid_spec=pltpu.PrefetchScalarGridSpec(
            num_scalar_prefetch=1, grid=(groups, tiles),
            in_specs=[q_spec, w_spec, w_spec, s_spec, o_spec, t_spec] + [pl.BlockSpec(memory_space=pl.ANY)] * len(into),
            out_specs=[q_spec, w_spec, w_spec],
            scratch_shapes=[pltpu.VMEM((2 * block, wide), F32)]),
        out_shape=[jax.ShapeDtypeStruct(q_val.shape, BF16), jax.ShapeDtypeStruct(window[0].shape, BF16),
                   jax.ShapeDtypeStruct(window[0].shape, F32)],
        input_output_aliases={7: 0} if into else {},
        compiler_params=pltpu.CompilerParams(vmem_limit_bytes=60 << 20),
        cost_estimate=pl.CostEstimate(flops=20 * work * 2 * block, bytes_accessed=20 * work, transcendentals=work * 6),
        name='attn_bwd',
    )(meta, q_val, *window, stats, grad_out, tau, *into)


def solution(mesh):
    tp_size = mesh.shape['tp']
    row_spec = P(None, 'cp', None)
    col_spec = P(None, 'tp')
    grid_spec = P('cp', 'tp')
    out_rows = P(('tp', 'cp'), None)
    in_specs = (row_spec, P('cp'), P('cp', None), P('cp', None),
                P(None), col_spec, col_spec, col_spec, P('tp', None),
                P(None), col_spec, col_spec, col_spec, P('tp', None), row_spec)
    out_specs = (row_spec, row_spec,
                 P('cp'), grid_spec, grid_spec, grid_spec, out_rows,
                 P('cp'), grid_spec, grid_spec, grid_spec, out_rows)

    def body(x_in, positions, rope_cos, rope_sin, norm_a, wq_a, wk_a, wv_a, wo_a,
             norm_b, wq_b, wk_b, wv_b, wo_b, grad_y):
        batch, block, d_model = x_in.shape
        head_dim = rope_cos.shape[1]
        tp_rank = lax.axis_index('tp')
        cp_rank = lax.axis_index('cp')
        par = tp_rank % 2
        n_rows = batch * block // tp_size
        half = block // 2
        scale = head_dim ** -0.5
        own_at = half * par
        shared_at = block * (1 - par)
        base_shared = half * par

        def my_rows(full):
            return lax.dynamic_slice_in_dim(full.reshape(batch * block, -1), tp_rank * n_rows, n_rows, 0)

        def row_table(tab):
            shared = lax.dynamic_slice_in_dim(tab, base_shared, half, 0)
            long = jnp.concatenate([shared, tab, shared], axis=0)
            return lax.dynamic_slice_in_dim(long, half * (1 - par), n_rows, 0)

        def gather_weight(part):
            over_tp = lax.all_gather(part, 'tp', axis=0, tiled=False)
            return lax.all_gather(over_tp, 'cp', axis=0, tiled=False)

        def gather_qkv(w_q, w_k, w_v):
            return gather_weight(jnp.where(cp_rank == 0, w_q, jnp.concatenate([w_k, w_v], axis=1)))

        def gather_out(w_o):
            part = lax.dynamic_slice_in_dim(w_o, cp_rank * head_dim, head_dim, 0)
            return gather_weight(part).reshape(2, tp_size * head_dim, d_model)

        def swap(val):
            return lax.ppermute(val, 'tp', [(i, i ^ 1) for i in range(tp_size)])

        def attention(local, key_val, make_query):
            own = lax.dynamic_slice_in_dim(key_val, own_at, block, 1)
            shared = lax.dynamic_slice_in_dim(key_val, shared_at, half, 1)
            other = swap(shared)
            win_own = (lax.ppermute(own, 'cp', [(0, 1)]), own)
            query = make_query()
            out, stat_own = attn_forward(local, scale, meta_own, 2, query, win_own)
            sh_blk = lax.dynamic_slice_in_dim(jnp.concatenate([shared, other, shared], axis=1), half * par, block, 1)
            win_sh = (lax.ppermute(sh_blk, 'cp', [(0, 1)]), sh_blk)
            out, stat_sh = attn_forward(local, scale, meta_sh, 1, query, win_sh, (out,))
            return out, (query, win_own, win_sh, stat_own, stat_sh)

        def attention_back(local, saved, grad_out, tau):
            query, win_own, win_sh, stat_own, stat_sh = saved
            grad_q, dprev, dcur = attn_backward(local, scale, meta_sh, 1, query, win_sh, stat_sh, grad_out, tau)
            sh_blk = dcur + lax.ppermute(dprev, 'cp', [(1, 0)]).astype(F32)
            mine = lax.dynamic_slice_in_dim(sh_blk, half * par, half, 1)
            theirs = lax.dynamic_slice_in_dim(sh_blk, half * (1 - par), half, 1).astype(BF16)
            theirs = swap(theirs)
            grad_q, dprev, dcur = attn_backward(local, scale, meta_own, 2, query, win_own, stat_own, grad_out, tau,
                                                (grad_q,))
            mine = (mine + theirs.astype(F32)).astype(BF16)
            own = (dcur + lax.ppermute(dprev, 'cp', [(1, 0)]).astype(F32)).astype(BF16)
            long = jnp.concatenate([mine, own, mine], axis=1)
            return grad_q, lax.dynamic_slice_in_dim(long, half * (1 - par), n_rows, 1)

        def exchange(pick, place, buf):
            for k in range(tp_size):
                peer = tp_rank ^ k
                piece = pick(peer)
                if k:
                    piece = lax.ppermute(piece, 'tp', [(i, i ^ k) for i in range(tp_size)])
                buf = place(buf, piece, peer)
            return buf

        def to_groups(val):
            return exchange(lambda p: lax.dynamic_index_in_dim(val, p, 0, keepdims=False),
                            lambda buf, piece, p: lax.dynamic_update_slice_in_dim(buf, piece, p * n_rows, 0),
                            jnp.zeros((batch * block, val.shape[2]), val.dtype))

        def heads_to_groups(val):
            return exchange(lambda p: lax.dynamic_slice_in_dim(val, p * head_dim, head_dim, 2),
                            lambda buf, piece, p: lax.dynamic_update_slice_in_dim(buf, piece, p * n_rows, 1),
                            jnp.zeros((2, batch * block, head_dim), val.dtype))

        def to_all(rows):
            own = lax.dynamic_slice_in_dim(rows, own_at, block, 0)
            shared = lax.dynamic_slice_in_dim(rows, shared_at, half, 0)
            shared = lax.all_gather(shared, 'tp', axis=0, tiled=True)
            own = lax.all_gather(own, 'tp', axis=0, tiled=True)
            pieces = []
            for chip in range(tp_size):
                pair = [own[block * chip:block * (chip + 1)], shared[half * chip:half * (chip + 1)]]
                pieces += pair[::-1] if chip % 2 else pair
            return jnp.concatenate(pieces, axis=0).reshape(batch, block, d_model)

        def cp_sum(part_of):
            sent = lax.ppermute(part_of(1 - cp_rank), 'cp', [(0, 1), (1, 0)])
            return part_of(cp_rank) + sent

        def cols(val, half_no):
            return lax.dynamic_slice_in_dim(val, half_no * (d_model // 2), d_model // 2, 1)

        def head_rows(val, half_no):
            return lax.dynamic_index_in_dim(val, half_no, 0, keepdims=False)

        w_qkv_a = gather_qkv(wq_a, wk_a, wv_a)
        w_out_a = gather_out(wo_a)
        w_qkv_b = gather_qkv(wq_b, wk_b, wv_b)
        w_out_b = gather_out(wo_b)

        key_at = [block * (1 - cp_rank), positions[0] - block]
        meta_own = jnp.stack([par, block + 0 * par] + key_at).astype(jnp.int32)
        meta_sh = jnp.stack([2 * (1 - par), block + half * par] + key_at).astype(jnp.int32)
        cos_r = row_table(rope_cos)
        sin_r = row_table(rope_sin)
        q_temp = row_table(value_a11(positions))
        ones = jnp.ones((1, n_rows), F32)

        xn_all = rms_norm(x_in, norm_a).reshape(batch * block, d_model)
        xn_a = lax.dynamic_slice_in_dim(xn_all, tp_rank * n_rows, n_rows, 0)
        x_rows = my_rows(x_in)
        gy_rows = my_rows(grad_y)
        kv_raw = dot_f32('rd,tdh->trh', xn_a, w_qkv_a[1]).astype(BF16)
        kv_a = prep_call(prep_kernel, 1, kv_raw, cos_r, sin_r)

        def query_a():
            raw = dot_f32('rd,tdh->trh', xn_a, w_qkv_a[0]).astype(BF16)
            q_raws.append(raw)
            return prep_call(prep_kernel, 2, raw, cos_r, sin_r)

        q_raws = []
        out_a, saved_a = attention(True, kv_a, query_a)
        q_raw = q_raws[0]
        attn_a = dot_f32('crh,chd->rd', out_a, w_out_a).astype(BF16)
        h_rows = (x_rows.astype(F32) + attn_a.astype(F32)).astype(BF16)

        xn_b = rms_norm(h_rows, norm_b)
        kv_b = dot_f32('rd,tdh->trh', xn_b, w_qkv_b[1]).astype(BF16)

        def query_b():
            raw = dot_f32('rd,tdh->trh', xn_b, w_qkv_b[0]).astype(BF16)
            return (raw.astype(F32) * q_temp[None, :, None]).astype(BF16)

        out_b, saved_b = attention(False, kv_b, query_b)
        attn_b = dot_f32('crh,chd->rd', out_b, w_out_b).astype(BF16)
        y_rows = (h_rows.astype(F32) + attn_b.astype(F32)).astype(BF16)
        out_y = to_all(y_rows)
        gy_rows, _ = lax.optimization_barrier((gy_rows, y_rows))

        grad_ob = dot_f32('rd,chd->crh', gy_rows, w_out_b).astype(BF16)
        grad_q_b, grad_kv_b = attention_back(False, saved_b, grad_ob, q_temp[None, :])
        out_b_group = heads_to_groups(out_b)
        gy_all = grad_y.reshape(batch * block, d_model)
        grad_wo_b = cp_sum(lambda half_no: dot_f32('rh,rd->hd', head_rows(out_b_group, half_no), gy_all))
        parts = []
        for grad_part in (grad_q_b, grad_kv_b):
            part_b = cp_sum(lambda half_no: dot_f32('rd,trh->thd', cols(xn_b, half_no), grad_part))
            part_b = with_layout_constraint(part_b.reshape(-1, d_model // 2), Layout((0, 1)))
            part_b = lax.psum_scatter(part_b, 'tp', scatter_dimension=0, tiled=True)
            part_b = with_layout_constraint(part_b, Layout((0, 1)))
            parts.append(part_b.T)
        grad_wq_b, grad_wkv_b = parts
        grad_xn_b = (dot_f32('trh,tdh->rd', grad_q_b, w_qkv_b[0])
                     + dot_f32('trh,tdh->rd', grad_kv_b, w_qkv_b[1])).astype(BF16)
        grad_h_norm, gain_b = norm_backward(h_rows, norm_b, grad_xn_b.astype(F32))
        grad_h = (gy_rows.astype(F32) + grad_h_norm).astype(BF16)

        grad_oa = dot_f32('rd,chd->crh', grad_h, w_out_a).astype(BF16)
        grad_q_a, grad_kv_a = attention_back(True, saved_a, grad_oa, ones)
        part_o = cp_sum(lambda half_no: dot_f32('rh,rd->hd', head_rows(out_a, half_no), grad_h))
        grad_wo_a = lax.psum_scatter(part_o, 'tp', scatter_dimension=0, tiled=True)
        grad_q_raw = prep_call(prep_back_kernel, 2, q_raw, cos_r, sin_r, grad_q_a)
        grad_kv_raw = prep_call(prep_back_kernel, 1, kv_raw, cos_r, sin_r, grad_kv_a)
        grad_xn_q = dot_f32('trh,tdh->rd', grad_q_raw, w_qkv_a[0])
        grad_xn_a = (grad_xn_q + dot_f32('trh,tdh->rd', grad_kv_raw, w_qkv_a[1])).astype(BF16)
        grad_x_norm, gain_a = norm_backward(x_rows, norm_a, grad_xn_a.astype(F32))
        gx_rows = (grad_h.astype(F32) + grad_x_norm).astype(BF16)
        grad_x = to_all(gx_rows)
        grad_q_group = to_groups(grad_q_raw)
        grad_kv_group = to_groups(grad_kv_raw)
        grad_wq_a = cp_sum(lambda half_no: dot_f32('rd,rh->dh', cols(xn_all, half_no), grad_q_group))
        grad_wkv_a = cp_sum(lambda half_no: dot_f32('rd,rh->dh', cols(xn_all, half_no), grad_kv_group))

        gains = lax.psum(jnp.stack([gain_a, gain_b]), ('tp', 'cp'))
        gains = lax.dynamic_slice_in_dim(gains, cp_rank * (d_model // 2), d_model // 2, 1).astype(BF16)
        grad_wo_b, grad_wo_a, grad_wq_a, grad_wkv_a, grad_wq_b, grad_wkv_b = (
            val.astype(BF16) for val in (grad_wo_b, grad_wo_a, grad_wq_a, grad_wkv_a, grad_wq_b, grad_wkv_b))
        return (out_y, grad_x,
                gains[0], grad_wq_a, grad_wkv_a[:, :head_dim], grad_wkv_a[:, head_dim:], grad_wo_a,
                gains[1], grad_wq_b, grad_wkv_b[:, :head_dim], grad_wkv_b[:, head_dim:], grad_wo_b)

    return jax.shard_map(body, mesh=mesh, in_specs=in_specs, out_specs=out_specs, check_vma=False)
```

time: 1760 us -> 1720 us (0.977)
  waiting for transfers between devices: 758 us -> 698 us
    ppermute x4, waiting for transfers between devices: 175 us -> 93.7 us  [swap(): return lax.ppermute(val, 'tp', [(i, i ^ 1) for i in range(tp_size)])]
    reduce_scatter x1, waiting for transfers between devices: 0.02 us -> 69.6 us  [body(): grad_wo_a = lax.psum_scatter(part_o, 'tp', scatter_dimension=0, tiled=True)]
    all_gather x2 -> x4, waiting for transfers between devices: 65.8 us -> 0.01 us  [the longest x2 0.01 us: to_all(): own = lax.all_gather(own, 'tp', axis=0, tiled=True)]
    all_gather x4, waiting for transfers between devices: 253 us -> 286 us  [gather_weight(): over_tp = lax.all_gather(part, 'tp', axis=0, tiled=False)]
    add x2 -> x0, local copies, waits for them, and re-layouts: 23.3 us -> none  [cp_sum(): return part_of(cp_rank) + sent]
    unnamed x76 -> x83, local copies, waits for them, and re-layouts: 39.7 us -> 60.6 us
    pallas_call x2 -> x4, Pallas kernels: 33.1 us -> 47.3 us  [prep_call(): pl.pallas_call(functools.partial(kernel, heads), grid=(rows // TILE, grou...]
    pallas_call x2 -> x4, Pallas kernels: 94 us -> 98 us  [attn_forward(): pl.pallas_call(functools.partial(attn_kernel, local, scale), grid_spec=pl...]
  transfers between devices with their start and end apart: 40 -> 42, of which waited for: 21 -> 16; matrix products, arithmetic and copies ran while one was open for 29% -> 34% of each run, Pallas kernels for 12% -> 18%
where the time goes in v2:
time: 1720 us; the launch traced here: 1710 us
  waiting for transfers between devices  698 us (41%)
  matrix products  379 us (22%)
  Pallas kernels  305 us (18%)
  other arithmetic  132 us (8%)
  local copies, waits for them, and re-layouts  123 us (7%)
  starting transfers between devices  38.3 us (2%)
  blocking collectives  23.8 us (1%)
    dot_general x24, matrix products, dot_f32(): return jnp.einsum(spec, lhs, rhs, preferred_element_type=F32)  379 us
    all_gather x4, waiting for transfers between devices, gather_weight(): over_tp = lax.all_gather(part, 'tp', axis=0, tiled=False)  286 us
    ppermute x9, waiting for transfers between devices, exchange(): piece = lax.ppermute(piece, 'tp', [(i, i ^ k) for i in range(tp_size)])  236 us
    pallas_call x4, Pallas kernels, attn_backward(): pl.pallas_call(functools.partial(attn_back_kernel, local, scale), grid_sp...  159 us
    pallas_call x4, Pallas kernels, attn_forward(): pl.pallas_call(functools.partial(attn_kernel, local, scale), grid_spec=pl...  98 us
    ppermute x4, waiting for transfers between devices, swap(): return lax.ppermute(val, 'tp', [(i, i ^ 1) for i in range(tp_size)])  93.7 us
    reduce_scatter x1, waiting for transfers between devices, body(): grad_wo_a = lax.psum_scatter(part_o, 'tp', scatter_dimension=0, tiled=True)  69.6 us
    unnamed x83, local copies, waits for them, and re-layouts  60.6 us
  transfers between devices with their start and end apart: 42, of which 16 were waited for; matrix products, arithmetic and copies ran while one was open for 34% of the time, Pallas kernels for 18%

profile of v2, /device:TPU:0, one launch (start us, length us, event | category | flops | bytes accessed | tf_op | source)
XLA Modules:
  0.0 1713.8 jit_solution(10964326767254765163)
XLA Ops:
  18.1 96.3 %all-gather.29.cloned.1.call-done = bf16[10240,512]{1,0:T(8,128)(2,1)} async-done(((bf16[2560,512]{1,0:T(8,128)(2,1)}), bf16[10240,512]{1,0:T(8,128)(2,1)}) %all-gather.29.cloned.1.call-update) | async-done | bytes 10485776 | tf_op jit(solution)/shard_map/all_gather | solution.py:250
  117.4 55.2 %all-gather.33.cloned.1.call-done = bf16[1024,2560]{1,0:T(8,128)(2,1)} async-done(((bf16[256,2560]{1,0:T(8,128)(2,1)}), bf16[1024,2560]{1,0:T(8,128)(2,1)}) %all-gather.33.cloned.1.call-update) | async-done | bytes 5242896 | tf_op jit(solution)/shard_map/all_gather | solution.py:250
  172.6 101.7 %all-gather.37.cloned.1.call-done = bf16[10240,512]{1,0:T(8,128)(2,1)} async-done(((bf16[2560,512]{1,0:T(8,128)(2,1)}), bf16[10240,512]{1,0:T(8,128)(2,1)}) %all-gather.37.cloned.1.call-update) | async-done | bytes 10485776 | tf_op jit(solution)/shard_map/all_gather | solution.py:250
  275.7 13.9 fusion
  291.8 22.1 %fusion.2 = bf16[6,768,2560]{2,1,0:T(8,128)(2,1)} fusion(bf16[6,768,2560]{2,1,0:T(8,128)(2,1)} %param.15, f32[2560]{0:T(1024)S(1)} %convert_element_type.173, f32[6,768]{1,0:T(8,128)S(1)} %add_rsqrt_fusion), kind=kLoop, calls=%fused_computation.4 | loop fusion | flops 47185920 | bytes 47214592 | tf_op jit(solution)/shard_map/convert_element_type | solution.py:27
  313.9 19.3 %fusion.92.src = bf16[4,1152,512]{2,1,0:T(8,128)(2,1)} fusion(bf16[8,2560,512]{2,1,0:T(8,128)(2,1)} %all-gather.31.cloned.1.call-done, bf16[4608,2560]{1,0:T(8,128)(2,1)} %bitcast.176, s32[]{:T(128)S(6)} %select_n.135), kind=kOutput, calls=%fused_computation.110 | convolution fusion | flops 12081954816 | bytes 31588356 | tf_op jit(solution)/shard_map/rd,tdh->trh/dot_general | solution.py:45
  333.1 10.3 shard_map.239
  355.2 32.7 %all-gather.41.cloned.1.call-done = bf16[1024,2560]{1,0:T(8,128)(2,1)} async-done(((bf16[256,2560]{1,0:T(8,128)(2,1)}), bf16[1024,2560]{1,0:T(8,128)(2,1)}) %all-gather.41.cloned.1.call-update) | async-done | bytes 5242896 | tf_op jit(solution)/shard_map/all_gather | solution.py:250
  388.2 13.0 collective-permute-done
  401.2 5.5 fusion.108.cur
  409.7 18.3 %fusion.95.src = bf16[4,1152,512]{2,1,0:T(8,128)(2,1)} fusion(bf16[8,2560,512]{2,1,0:T(8,128)(2,1)} %all-gather.31.cloned.1.call-done, bf16[4608,2560]{1,0:T(8,128)(2,1)} %bitcast.177, s32[]{:T(128)S(6)} %select_n.135), kind=kOutput, calls=%fused_computation.111 | convolution fusion | flops 12081954816 | bytes 31588356 | tf_op jit(solution)/shard_map/rd,tdh->trh/dot_general | solution.py:45
  428.0 11.8 shard_map.238.q_ref
  439.8 32.5 %attn_fwd.4 = (bf16[2,1152,1024]{2,1,0:T(8,128)(2,1)}, f32[4,4,768]{2,1,0:T(4,128)}) custom-call(s32[4]{0:T(128)} %add_add_fusion.1.meta, bf16[4,1152,512]{2,1,0:T(8,128)(2,1)} %shard_map.238.q_ref, bf16[4,768,512]{2,1,0:T(8,128)(2,1)} %collective-permute-done.2.prev, bf16[4,768,512]{2,1,0:T(8,128)(2,1)} %constant_dynamic-slice_fusion.11.cur), custom_call_target="tpu_custom_call" | custom-call | flops 19327352832 | bytes 18874368 | tf_op jit(solution)/shard_map/attn_fwd/pallas_call | solution.py:178
  472.3 17.9 %attn_fwd.5 = (bf16[2,1152,1024]{2,1,0:T(8,128)(2,1)}, f32[4,4,384]{2,1,0:T(4,128)}) custom-call(s32[4]{0:T(128)} %add_add_fusion.meta, bf16[4,1152,512]{2,1,0:T(8,128)(2,1)} %shard_map.238.q_ref, bf16[4,768,512]{2,1,0:T(8,128)(2,1)} %collective-permute-done.1.prev, bf16[4,768,512]{2,1,0:T(8,128)(2,1)} %fusion.108.cur, ...), custom_call_target="tpu_custom_call", output_to_operand_aliasing={{0}: (4, {})} | custom-call | flops 9663676416 | bytes 9437184 | tf_op jit(solution)/shard_map/attn_fwd/pallas_call | solution.py:178
  490.1 17.9 %fusion.27 = (f32[1152]{0:T(1024)S(1)}, bf16[1152,2560]{1,0:T(8,128)(2,1)S(1)}) fusion(bf16[2,1152,1024]{2,1,0:T(8,128)(2,1)} %get-tuple-element.34, bf16[2,1024,2560]{2,1,0:T(8,128)(2,1)} %bitcast.198, bf16[4608,2560]{1,0:T(8,128)(2,1)} %bitcast.167, s32[]{:T(128)S(6)} %select_n.135), kind=kOutput, calls=%fused_computation.43 | convolution fusion | flops 12103187456 | bytes 27005444 | tf_op jit(solution)/shard_map/crh,chd->rd/dot_general | solution.py:45
  514.4 17.3 %fusion.74 = bf16[4,512,1152]{1,2,0:T(8,128)(2,1)S(1)} fusion(bf16[8,2560,512]{2,1,0:T(8,128)(2,1)} %all-gather.39.cloned.1.call-done, bf16[1152,2560]{1,0:T(8,128)(2,1)} %fusion.24), kind=kOutput, calls=%fused_computation.94 | convolution fusion | flops 12081954816 | bytes 31588352 | tf_op jit(solution)/shard_map/rd,tdh->trh/dot_general | solution.py:45
  536.1 30.0 %collective-permute-done.3 = bf16[4,384,512]{2,1,0:T(8,128)(2,1)S(1)} collective-permute-done((bf16[4,384,512]{2,1,0:T(8,128)(2,1)S(1)}, bf16[4,384,512]{2,1,0:T(8,128)(2,1)S(1)}, u32[]{:S(2)}, u32[]{:S(2)}) %collective-permute-start.3) | collective-permute-done | bytes 1572896 | tf_op jit(solution)/shard_map/ppermute | solution.py:261
  574.1 16.9 fusion.89.q_ref
  591.1 30.7 %attn_fwd.6 = (bf16[2,1152,1024]{2,1,0:T(8,128)(2,1)}, f32[4,4,768]{2,1,0:T(4,128)}) custom-call(s32[4]{0:T(128)} %add_add_fusion.1.meta, bf16[4,1152,512]{2,1,0:T(8,128)(2,1)} %fusion.89.q_ref, bf16[4,768,512]{2,1,0:T(8,128)(2,1)} %collective-permute-done.5.prev, bf16[4,768,512]{2,1,0:T(8,128)(2,1)} %copy-done.11), custom_call_target="tpu_custom_call" | custom-call | flops 19327352832 | bytes 18874368 | tf_op jit(solution)/shard_map/attn_fwd/pallas_call | solution.py:178
  621.8 17.0 attn_fwd.7
  638.7 17.4 %fusion.28 = bf16[1152,2560]{1,0:T(8,128)(2,1)S(1)} fusion(bf16[1152,2560]{1,0:T(8,128)(2,1)} %copy-done.2, bf16[2,1152,1024]{2,1,0:T(8,128)(2,1)} %get-tuple-element.36, bf16[2,1024,2560]{2,1,0:T(8,128)(2,1)} %bitcast.200), kind=kOutput, calls=%fused_computation.44 | convolution fusion | flops 12094341120 | bytes 27000832 | tf_op jit(solution)/shard_map/crh,chd->rd/dot_general | solution.py:45
  664.6 19.7 %fusion.86.g_ref = bf16[2,1152,1024]{2,1,0:T(8,128)(2,1)} fusion(bf16[2,1024,2560]{2,1,0:T(8,128)(2,1)} %bitcast.201, bf16[1152,2560]{1,0:T(8,128)(2,1)S(1)} %constant_dynamic-slice_fusion.6), kind=kOutput, calls=%fused_computation.108 | convolution fusion | flops 12081954816 | bytes 21102592 | tf_op jit(solution)/shard_map/rd,chd->crh/dot_general | solution.py:45
  684.4 26.2 %attn_bwd.4 = (bf16[4,1152,512]{2,1,0:T(8,128)(2,1)}, bf16[4,768,512]{2,1,0:T(8,128)(2,1)}, f32[4,768,512]{2,1,0:T(8,128)}) custom-call(s32[4]{0:T(128)} %add_add_fusion.meta, bf16[4,1152,512]{2,1,0:T(8,128)(2,1)} %fusion.89.q_ref, bf16[4,768,512]{2,1,0:T(8,128)(2,1)} %collective-permute-done.4.prev, bf16[4,768,512]{2,1,0:T(8,128)(2,1)} %fusion.106.cur, ...), custom_call_target="tpu_custom_call" | custom-call | flops 24159191040 | bytes 15728640 | tf_op jit(solution)/shard_map/attn_bwd/pallas_call | solution.py:198
  711.9 52.2 %attn_bwd.5 = (bf16[4,1152,512]{2,1,0:T(8,128)(2,1)}, bf16[4,768,512]{2,1,0:T(8,128)(2,1)}, f32[4,768,512]{2,1,0:T(8,128)}) custom-call(s32[4]{0:T(128)} %add_add_fusion.1.meta, bf16[4,1152,512]{2,1,0:T(8,128)(2,1)} %fusion.89.q_ref, bf16[4,768,512]{2,1,0:T(8,128)(2,1)} %collective-permute-done.5.prev, ...), custom_call_target="tpu_custom_call", output_to_operand_aliasing={{0}: (7, {})} | custom-call | flops 48318382080 | bytes 31457280 | tf_op jit(solution)/shard_map/attn_bwd/pallas_call | solution.py:198
  765.5 5.2 convert_add_fusion.3
  771.6 12.7 fusion.117
  797.0 40.3 %collective-permute-done.7 = bf16[4,384,512]{2,1,0:T(8,128)(2,1)} collective-permute-done((bf16[4,384,512]{2,1,0:T(8,128)(2,1)S(1)}, bf16[4,384,512]{2,1,0:T(8,128)(2,1)}, u32[]{:S(2)}, u32[]{:S(2)}) %collective-permute-start.7) | collective-permute-done | bytes 1572896 | tf_op jit(solution)/shard_map/ppermute | solution.py:261
  840.5 5.5 fusion.82
  848.2 18.1 %convolution_bitcast_fusion.2 = f32[1152,2560]{1,0:T(8,128)} fusion(bf16[4,1152,512]{2,1,0:T(8,128)(2,1)S(1)} %fusion.82, bf16[8,2560,512]{2,1,0:T(8,128)(2,1)} %all-gather.39.cloned.1.call-done), kind=kOutput, calls=%fused_computation.25 | convolution fusion | flops 12079595520 | bytes 27000832 | tf_op jit(solution)/shard_map/trh,tdh->rd/dot_general | solution.py:45
  866.3 24.1 %fusion.26 = (f32[2560]{0:T(1024)}, f32[1152]{0:T(1024)S(1)}, bf16[1152,2560]{1,0:T(8,128)(2,1)}) fusion(bf16[1152,2560]{1,0:T(8,128)(2,1)} %copy-done.2, f32[1152]{0:T(1024)S(1)} %copy-done.20, f32[2560]{0:T(1024)S(1)} %copy-done.18, f32[1152,2560]{1,0:T(8,128)} %convolution_bitcast_fusion.2, bf16[4,1152,512]{2,1,0:T(8,128)(2,1)} %get-tuple-element.41, ...), kind=kOutput, calls=%fused_computation.42 | convolution fusion | flops 12109083648 | bytes 38827008 | tf_op jit(solution)/shard_map/trh,tdh->rd/dot_general | solution.py:45
  890.5 11.6 fusion.19
  902.0 13.6 convolution_add_fusion.1
  915.7 18.4 %fusion.83.g_ref = bf16[2,1152,1024]{2,1,0:T(8,128)(2,1)} fusion(bf16[2,1024,2560]{2,1,0:T(8,128)(2,1)} %bitcast.199, bf16[1152,2560]{1,0:T(8,128)(2,1)} %fusion.19), kind=kOutput, calls=%fused_computation.107 | convolution fusion | flops 12081954816 | bytes 21102592 | tf_op jit(solution)/shard_map/rd,chd->crh/dot_general | solution.py:45
  934.7 27.0 %attn_bwd.6 = (bf16[4,1152,512]{2,1,0:T(8,128)(2,1)}, bf16[4,768,512]{2,1,0:T(8,128)(2,1)}, f32[4,768,512]{2,1,0:T(8,128)}) custom-call(s32[4]{0:T(128)} %add_add_fusion.meta, bf16[4,1152,512]{2,1,0:T(8,128)(2,1)} %shard_map.238.q_ref, bf16[4,768,512]{2,1,0:T(8,128)(2,1)} %collective-permute-done.1.prev, bf16[4,768,512]{2,1,0:T(8,128)(2,1)} %fusion.108.cur, ...), custom_call_target="tpu_custom_call" | custom-call | flops 24159191040 | bytes 15728640 | tf_op jit(solution)/shard_map/attn_bwd/pallas_call | solution.py:198
  963.1 53.8 %attn_bwd.7 = (bf16[4,1152,512]{2,1,0:T(8,128)(2,1)}, bf16[4,768,512]{2,1,0:T(8,128)(2,1)}, f32[4,768,512]{2,1,0:T(8,128)}) custom-call(s32[4]{0:T(128)} %add_add_fusion.1.meta, bf16[4,1152,512]{2,1,0:T(8,128)(2,1)} %shard_map.238.q_ref, bf16[4,768,512]{2,1,0:T(8,128)(2,1)} %collective-permute-done.2.prev, ...), custom_call_target="tpu_custom_call", output_to_operand_aliasing={{0}: (7, {})} | custom-call | flops 48318382080 | bytes 31457280 | tf_op jit(solution)/shard_map/attn_bwd/pallas_call | solution.py:198
  1030.5 13.3 shard_map.240
  1048.8 10.5 collective-permute-done.10
  1061.2 6.5 fusion.80.grad
  1067.7 11.9 shard_map.241
  1079.7 19.2 %convolution_bitcast_fusion = f32[1152,2560]{1,0:T(8,128)} fusion(bf16[4,1152,512]{2,1,0:T(8,128)(2,1)} %shard_map.241, bf16[8,2560,512]{2,1,0:T(8,128)(2,1)} %all-gather.31.cloned.1.call-done), kind=kOutput, calls=%fused_computation.22 | convolution fusion | flops 12079595520 | bytes 27000832 | tf_op jit(solution)/shard_map/trh,tdh->rd/dot_general | solution.py:45
  1098.8 22.4 %fusion.21 = (f32[2560]{0:T(1024)S(1)}, f32[1152]{0:T(1024)S(1)}, bf16[1152,2560]{1,0:T(8,128)(2,1)}) fusion(f32[1152]{0:T(1024)S(1)} %add_rsqrt_fusion.1, bf16[4608,2560]{1,0:T(8,128)(2,1)} %bitcast.169, s32[]{:T(128)S(6)} %select_n.135, f32[2560]{0:T(1024)S(1)} %copy-done.16, f32[1152,2560]{1,0:T(8,128)} %convolution_bitcast_fusion, ...), kind=kOutput, calls=%fused_computation.37 | convolution fusion | flops 12109083648 | bytes 38827012 | tf_op jit(solution)/shard_map/trh,tdh->rd/dot_general | solution.py:45
  1121.2 8.7 fusion.16
  1134.7 12.5 fusion.115
  1154.5 13.1 collective-permute-done.22
  1167.6 13.7 convolution_add_fusion
  1181.4 13.0 fusion.128
  1198.2 5.1 constant_dynamic-slice_fusion
  1206.8 50.9 %collective-permute-done.23 = bf16[2,1152,256]{2,1,0:T(8,128)(2,1)} collective-permute-done((bf16[2,1152,256]{2,1,0:T(8,128)(2,1)}, bf16[2,1152,256]{2,1,0:T(8,128)(2,1)}, u32[]{:S(2)}, u32[]{:S(2)}) %collective-permute-start.23) | collective-permute-done | bytes 1179680 | tf_op jit(solution)/shard_map/ppermute | solution.py:294
  1261.2 47.8 %collective-permute-done.25 = bf16[2,1152,256]{2,1,0:T(8,128)(2,1)S(1)} collective-permute-done((bf16[2,1152,256]{2,1,0:T(8,128)(2,1)}, bf16[2,1152,256]{2,1,0:T(8,128)(2,1)S(1)}, u32[]{:S(2)}, u32[]{:S(2)}) %collective-permute-start.25) | collective-permute-done | bytes 1179680 | tf_op jit(solution)/shard_map/ppermute | solution.py:294
  1315.8 12.7 fusion.125
  1330.2 27.1 %collective-permute-done.12 = bf16[1152,512]{1,0:T(8,128)(2,1)S(1)} collective-permute-done((bf16[1152,512]{1,0:T(8,128)(2,1)S(1)}, bf16[1152,512]{1,0:T(8,128)(2,1)S(1)}, u32[]{:S(2)}, u32[]{:S(2)}) %collective-permute-start.12) | collective-permute-done | bytes 1179680 | tf_op jit(solution)/shard_map/ppermute | solution.py:294
  1357.6 46.5 %collective-permute-done.14 = bf16[1152,512]{1,0:T(8,128)(2,1)S(1)} collective-permute-done((bf16[1152,512]{1,0:T(8,128)(2,1)S(1)}, bf16[1152,512]{1,0:T(8,128)(2,1)S(1)}, u32[]{:S(2)}, u32[]{:S(2)}) %collective-permute-start.14) | collective-permute-done | bytes 1179680 | tf_op jit(solution)/shard_map/ppermute | solution.py:294
  1406.5 12.5 fusion.39
  1422.6 36.1 %collective-permute-done.16 = bf16[1152,512]{1,0:T(8,128)(2,1)S(1)} collective-permute-done((bf16[1152,512]{1,0:T(8,128)(2,1)S(1)}, bf16[1152,512]{1,0:T(8,128)(2,1)S(1)}, u32[]{:S(2)}, u32[]{:S(2)}) %collective-permute-start.16) | collective-permute-done | bytes 1179680 | tf_op jit(solution)/shard_map/ppermute | solution.py:294
  1461.0 12.4 convolution_add_fusion.2
  1473.5 27.1 %collective-permute-done.18 = bf16[1152,512]{1,0:T(8,128)(2,1)} collective-permute-done((bf16[1152,512]{1,0:T(8,128)(2,1)}, bf16[1152,512]{1,0:T(8,128)(2,1)}, u32[]{:S(2)}, u32[]{:S(2)}) %collective-permute-start.18) | collective-permute-done | bytes 1179680 | tf_op jit(solution)/shard_map/ppermute | solution.py:294
  1502.9 11.7 fusion.37
  1514.7 13.4 fusion.98
  1528.2 10.7 fusion.112
  1538.9 23.8 %psum.7 = bf16[2,2560]{1,0:T(2,128)(2,1)S(1)} all-reduce(f32[2,2560]{1,0:T(2,128)S(1)} %pad_maximum_fusion), channel_id=1, replica_groups=mesh['tp'=4,'cp'=2] {'tp','cp'}, use_global_device_ids=true, to_apply=%region_7.8 | all-reduce | flops 5120 | bytes 30720 | tf_op jit(solution)/shard_map/psum | solution.py:407
  1563.4 11.1 fusion.109
  1584.2 7.3 slice_dynamic-update-slice_fusion.1
  1612.3 7.0 slice_dynamic-update-slice_fusion
  1634.5 69.6 %reduce-scatter.4.cloned.1.call-done = f32[256,2560]{1,0:T(8,128)} async-done(((f32[1024,2560]{1,0:T(8,128)}), f32[256,2560]{1,0:T(8,128)}) %reduce-scatter.4.cloned.1.call-update) | async-done | bytes 2621456 | tf_op jit(solution)/shard_map/reduce_scatter | solution.py:394
  (238 shorter events, 194.7 us)
Async XLA Ops:
  7.2 107.2 %all-gather.29.cloned.1.call-start = ((), (), s32[]{:S(2)}) async-start(), calls=%async_computation.10 | async-start | bytes 13107200 | tf_op jit(solution)/shard_map/all_gather | solution.py:250
  12.1 160.4 %all-gather.33.cloned.1.call-start = ((), (), s32[]{:S(2)}) async-start(), calls=%async_computation.12 | async-start | bytes 6553600 | tf_op jit(solution)/shard_map/all_gather | solution.py:250
  13.3 261.0 %all-gather.37.cloned.1.call-start = ((), (), s32[]{:S(2)}) async-start(), calls=%async_computation.14 | async-start | bytes 13107200 | tf_op jit(solution)/shard_map/all_gather | solution.py:250
  18.1 295.8 %all-gather.31.cloned.1.call-start = ((), (), s32[]{:S(2)}) async-start(), calls=%async_computation.11 | async-start | bytes 31457280 | tf_op jit(solution)/shard_map/all_gather | solution.py:251
  114.4 273.5 %all-gather.41.cloned.1.call-start = ((), (), s32[]{:S(2)}) async-start(), calls=%async_computation.16 | async-start | bytes 6553600 | tf_op jit(solution)/shard_map/all_gather | solution.py:250
  117.3 372.8 %all-gather.35.cloned.1.call-start = ((), (), s32[]{:S(2)}) async-start(), calls=%async_computation.13 | async-start | bytes 15728640 | tf_op jit(solution)/shard_map/all_gather | solution.py:251
  172.5 341.9 %all-gather.39.cloned.1.call-start = ((), (), s32[]{:S(2)}) async-start(), calls=%async_computation.15 | async-start | bytes 31457280 | tf_op jit(solution)/shard_map/all_gather | solution.py:251
  274.3 364.4 %all-gather.43.cloned.1.call-start = ((), (), s32[]{:S(2)}) async-start(), calls=%async_computation.17 | async-start | bytes 15728640 | tf_op jit(solution)/shard_map/all_gather | solution.py:251
  275.0 16.8 copy-start.15
  345.0 56.2 %collective-permute-start = (bf16[4,384,512]{2,1,0:T(8,128)(2,1)S(1)}, bf16[4,384,512]{2,1,0:T(8,128)(2,1)}, u32[]{:S(2)}, u32[]{:S(2)}) collective-permute-start(bf16[4,384,512]{2,1,0:T(8,128)(2,1)S(1)} %constant_dynamic-slice_fusion.12), channel_id=1, source_target_pairs={{0,2},{2,0},{4,6},{6,4},{1,3},{3,1},{5,7},{7,5}} | collective-permute-start | bytes 4718600 | tf_op jit(solution)/shard_map/ppermute | solution.py:261
  350.0 89.8 %collective-permute-start.2 = (bf16[4,768,512]{2,1,0:T(8,128)(2,1)}, bf16[4,768,512]{2,1,0:T(8,128)(2,1)}, u32[]{:S(2)}, u32[]{:S(2)}) collective-permute-start(bf16[4,768,512]{2,1,0:T(8,128)(2,1)} %constant_dynamic-slice_fusion.11.cur), channel_id=1, source_target_pairs={{0,1},{2,3},{4,5},{6,7}} | collective-permute-start | bytes 9437192 | tf_op jit(solution)/shard_map/ppermute | solution.py:267
  353.4 154.7 %copy-start.17 = (f32[2560]{0:T(1024)}, f32[2560]{0:T(1024)S(1)}, u32[]{:S(2)}) copy-start(f32[2560]{0:T(1024)S(1)} %convert_element_type.183) | copy-start | bytes 30724
  388.0 1187.6 %all-gather.21.cloned.1.call-start = ((), (), s32[]{:S(2)}) async-start(), calls=%async_computation.3 | async-start | bytes 19660800 | tf_op jit(solution)/shard_map/all_gather | solution.py:312
  406.7 65.6 %collective-permute-start.1 = (bf16[4,768,512]{2,1,0:T(8,128)(2,1)}, bf16[4,768,512]{2,1,0:T(8,128)(2,1)}, u32[]{:S(2)}, u32[]{:S(2)}) collective-permute-start(bf16[4,768,512]{2,1,0:T(8,128)(2,1)} %fusion.108.cur), channel_id=1, source_target_pairs={{0,1},{2,3},{4,5},{6,7}} | collective-permute-start | bytes 9437192 | tf_op jit(solution)/shard_map/ppermute | solution.py:271
  531.8 42.4 %slice-start.4 = ((s8[5898240]{0:T(1024)(128)(4,1)}), s8[4194304]{0:T(1024)(128)(4,1)S(1)}, s32[]{:S(2)}) async-start(s8[5898240]{0:T(1024)(128)(4,1)} %bitcast.188), calls=%async_computation.22 | async-start | bytes 8388608
  531.9 42.2 %slice-start.5 = ((s8[5898240]{0:T(1024)(128)(4,1)}), s8[1703936]{0:T(1024)(128)(4,1)S(1)}, s32[]{:S(2)}) async-start(s8[5898240]{0:T(1024)(128)(4,1)} %bitcast.188), calls=%async_computation.23 | async-start | bytes 3407872
  531.9 34.2 %collective-permute-start.3 = (bf16[4,384,512]{2,1,0:T(8,128)(2,1)S(1)}, bf16[4,384,512]{2,1,0:T(8,128)(2,1)S(1)}, u32[]{:S(2)}, u32[]{:S(2)}) collective-permute-start(bf16[4,384,512]{2,1,0:T(8,128)(2,1)S(1)} %dynamic-slice_bitcast_fusion.1), channel_id=1, source_target_pairs={{0,2},{2,0},{4,6},{6,4},{1,3},{3,1},{5,7},{7,5}} | collective-permute-start | bytes 4718600 | tf_op jit(solution)/shard_map/ppermute | solution.py:261
  532.8 58.3 %copy-start.11 = (bf16[4,768,512]{2,1,0:T(8,128)(2,1)}, bf16[4,768,512]{2,1,0:T(8,128)(2,1)S(1)}, u32[]{:S(2)}) copy-start(bf16[4,768,512]{2,1,0:T(8,128)(2,1)S(1)} %dynamic-slice_bitcast_fusion.cur) | copy-start | bytes 9437188
  532.8 58.3 %collective-permute-start.5 = (bf16[4,768,512]{2,1,0:T(8,128)(2,1)S(1)}, bf16[4,768,512]{2,1,0:T(8,128)(2,1)}, u32[]{:S(2)}, u32[]{:S(2)}) collective-permute-start(bf16[4,768,512]{2,1,0:T(8,128)(2,1)S(1)} %dynamic-slice_bitcast_fusion.cur), channel_id=1, source_target_pairs={{0,1},{2,3},{4,5},{6,7}} | collective-permute-start | bytes 9437192 | tf_op jit(solution)/shard_map/ppermute | solution.py:267
  571.1 50.6 %collective-permute-start.4 = (bf16[4,768,512]{2,1,0:T(8,128)(2,1)}, bf16[4,768,512]{2,1,0:T(8,128)(2,1)}, u32[]{:S(2)}, u32[]{:S(2)}) collective-permute-start(bf16[4,768,512]{2,1,0:T(8,128)(2,1)} %fusion.106.cur), channel_id=1, source_target_pairs={{0,1},{2,3},{4,5},{6,7}} | collective-permute-start | bytes 9437192 | tf_op jit(solution)/shard_map/ppermute | solution.py:271
  660.9 919.0 %all-gather.23.cloned.1.call-start = ((), (), s32[]{:S(2)}) async-start(), calls=%async_computation.4 | async-start | bytes 9830400 | tf_op jit(solution)/shard_map/all_gather | solution.py:311
  664.6 19.7 %copy-start.3 = (bf16[1152,2560]{1,0:T(8,128)(2,1)}, bf16[1152,2560]{1,0:T(8,128)(2,1)S(1)}, u32[]{:S(2)}) copy-start(bf16[1152,2560]{1,0:T(8,128)(2,1)S(1)} %constant_dynamic-slice_fusion.6) | copy-start | bytes 17694724
  710.6 54.8 %collective-permute-start.6 = (bf16[4,768,512]{2,1,0:T(8,128)(2,1)}, bf16[4,768,512]{2,1,0:T(8,128)(2,1)}, u32[]{:S(2)}, u32[]{:S(2)}) collective-permute-start(bf16[4,768,512]{2,1,0:T(8,128)(2,1)} %get-tuple-element.43), channel_id=1, source_target_pairs={{1,0},{3,2},{5,4},{7,6}} | collective-permute-start | bytes 9437192 | tf_op jit(solution)/shard_map/ppermute | solution.py:278
  764.1 27.9 %collective-permute-start.8 = (bf16[4,768,512]{2,1,0:T(8,128)(2,1)}, bf16[4,768,512]{2,1,0:T(8,128)(2,1)}, u32[]{:S(2)}, u32[]{:S(2)}) collective-permute-start(bf16[4,768,512]{2,1,0:T(8,128)(2,1)} %get-tuple-element.45), channel_id=1, source_target_pairs={{1,0},{3,2},{5,4},{7,6}} | collective-permute-start | bytes 9437192 | tf_op jit(solution)/shard_map/ppermute | solution.py:285
  770.7 13.7 copy-start.5
  770.9 66.4 %collective-permute-start.7 = (bf16[4,384,512]{2,1,0:T(8,128)(2,1)S(1)}, bf16[4,384,512]{2,1,0:T(8,128)(2,1)}, u32[]{:S(2)}, u32[]{:S(2)}) collective-permute-start(bf16[4,384,512]{2,1,0:T(8,128)(2,1)S(1)} %dynamic-slice_convert_fusion.1), channel_id=1, source_target_pairs={{0,2},{2,0},{4,6},{6,4},{1,3},{3,1},{5,7},{7,5}} | collective-permute-start | bytes 4718600 | tf_op jit(solution)/shard_map/ppermute | solution.py:261
  784.4 117.7 %collective-permute-start.21 = (f32[4,512,1280]{2,1,0:T(8,128)}, f32[4,512,1280]{2,1,0:T(8,128)}, u32[]{:S(2)}, u32[]{:S(2)}) collective-permute-start(f32[4,512,1280]{2,1,0:T(8,128)} %fusion.117), channel_id=1, source_target_pairs={{0,1},{1,0},{2,3},{3,2},{4,5},{5,4},{6,7},{7,6}} | collective-permute-start | bytes 31457288 | tf_op jit(solution)/shard_map/ppermute | solution.py:320
  791.9 808.3 %reduce-scatter.6.cloned.1.call-start = ((), (), s32[]{:S(2)}) async-start(), calls=%async_computation.8 | async-start | bytes 13107200 | tf_op jit(solution)/shard_map/reduce_scatter | solution.py:382
  848.2 18.1 %copy-start.18 = (f32[2560]{0:T(1024)S(1)}, f32[2560]{0:T(1024)}, u32[]{:S(2)}) copy-start(f32[2560]{0:T(1024)} %copy-done.17) | copy-start | bytes 30724
  848.2 18.1 %copy-start.20 = (f32[1152]{0:T(1024)S(1)}, f32[1152]{0:T(1024)}, u32[]{:S(2)}) copy-start(f32[1152]{0:T(1024)} %copy-done.19) | copy-start | bytes 13828
  915.7 687.9 %all-gather.25.cloned.1.call-start = ((), (), s32[]{:S(2)}) async-start(), calls=%async_computation.5 | async-start | bytes 19660800 | tf_op jit(solution)/shard_map/all_gather | solution.py:312
  961.8 56.4 %collective-permute-start.9 = (bf16[4,768,512]{2,1,0:T(8,128)(2,1)}, bf16[4,768,512]{2,1,0:T(8,128)(2,1)}, u32[]{:S(2)}, u32[]{:S(2)}) collective-permute-start(bf16[4,768,512]{2,1,0:T(8,128)(2,1)} %get-tuple-element.51), channel_id=1, source_target_pairs={{1,0},{3,2},{5,4},{7,6}} | collective-permute-start | bytes 9437192 | tf_op jit(solution)/shard_map/ppermute | solution.py:278
  1016.9 26.9 %collective-permute-start.11 = (bf16[4,768,512]{2,1,0:T(8,128)(2,1)}, bf16[4,768,512]{2,1,0:T(8,128)(2,1)}, u32[]{:S(2)}, u32[]{:S(2)}) collective-permute-start(bf16[4,768,512]{2,1,0:T(8,128)(2,1)} %get-tuple-element.53), channel_id=1, source_target_pairs={{1,0},{3,2},{5,4},{7,6}} | collective-permute-start | bytes 9437192 | tf_op jit(solution)/shard_map/ppermute | solution.py:285
  1026.2 33.1 %collective-permute-start.10 = (bf16[4,384,512]{2,1,0:T(8,128)(2,1)S(1)}, bf16[4,384,512]{2,1,0:T(8,128)(2,1)}, u32[]{:S(2)}, u32[]{:S(2)}) collective-permute-start(bf16[4,384,512]{2,1,0:T(8,128)(2,1)S(1)} %dynamic-slice_convert_fusion), channel_id=1, source_target_pairs={{0,2},{2,0},{4,6},{6,4},{1,3},{3,1},{5,7},{7,5}} | collective-permute-start | bytes 4718600 | tf_op jit(solution)/shard_map/ppermute | solution.py:261
  1043.8 15.5 copy-start.7
  1079.7 19.2 %copy-start.16 = (f32[2560]{0:T(1024)S(1)}, f32[2560]{0:T(1024)}, u32[]{:S(2)}) copy-start(f32[2560]{0:T(1024)} %copy-done.15) | copy-start | bytes 30724
  1134.6 473.2 %all-gather.27.cloned.1.call-start = ((), (), s32[]{:S(2)}) async-start(), calls=%async_computation.6 | async-start | bytes 9830400 | tf_op jit(solution)/shard_map/all_gather | solution.py:311
  1147.1 20.5 %collective-permute-start.22 = (f32[4,512,1280]{2,1,0:T(8,128)}, f32[4,512,1280]{2,1,0:T(8,128)}, u32[]{:S(2)}, u32[]{:S(2)}) collective-permute-start(f32[4,512,1280]{2,1,0:T(8,128)} %fusion.115), channel_id=1, source_target_pairs={{0,1},{1,0},{2,3},{3,2},{4,5},{5,4},{6,7},{7,6}} | collective-permute-start | bytes 31457288 | tf_op jit(solution)/shard_map/ppermute | solution.py:320
  1154.5 473.8 %reduce-scatter.8.cloned.1.call-start = ((), (), s32[]{:S(2)}) async-start(), calls=%async_computation.9 | async-start | bytes 13107200 | tf_op jit(solution)/shard_map/reduce_scatter | solution.py:382
  1181.3 522.8 %reduce-scatter.4.cloned.1.call-start = ((), (), s32[]{:S(2)}) async-start(), calls=%async_computation.7 | async-start | bytes 13107200 | tf_op jit(solution)/shard_map/reduce_scatter | solution.py:394
  1194.4 266.6 %collective-permute-start.20 = (f32[1024,2560]{1,0:T(8,128)}, f32[1024,2560]{1,0:T(8,128)}, u32[]{:S(2)}, u32[]{:S(2)}) collective-permute-start(f32[1024,2560]{1,0:T(8,128)} %fusion.128), channel_id=1, source_target_pairs={{0,1},{1,0},{2,3},{3,2},{4,5},{5,4},{6,7},{7,6}} | collective-permute-start | bytes 31457288 | tf_op jit(solution)/shard_map/ppermute | solution.py:320
  1203.3 54.4 %collective-permute-start.23 = (bf16[2,1152,256]{2,1,0:T(8,128)(2,1)}, bf16[2,1152,256]{2,1,0:T(8,128)(2,1)}, u32[]{:S(2)}, u32[]{:S(2)}) collective-permute-start(bf16[2,1152,256]{2,1,0:T(8,128)(2,1)} %get-tuple-element.98), channel_id=1, source_target_pairs={{0,2},{2,0},{4,6},{6,4},{1,3},{3,1},{5,7},{7,5}} | collective-permute-start | bytes 3538952 | tf_op jit(solution)/shard_map/ppermute | solution.py:294
  1204.2 55.9 %collective-permute-start.24 = (bf16[2,1152,256]{2,1,0:T(8,128)(2,1)}, bf16[2,1152,256]{2,1,0:T(8,128)(2,1)S(1)}, u32[]{:S(2)}, u32[]{:S(2)}) collective-permute-start(bf16[2,1152,256]{2,1,0:T(8,128)(2,1)} %get-tuple-element.97), channel_id=1, source_target_pairs={{0,4},{2,6},{4,0},{6,2},{1,5},{3,7},{5,1},{7,3}} | collective-permute-start | bytes 3538952 | tf_op jit(solution)/shard_map/ppermute | solution.py:294
  1205.4 103.6 %collective-permute-start.25 = (bf16[2,1152,256]{2,1,0:T(8,128)(2,1)}, bf16[2,1152,256]{2,1,0:T(8,128)(2,1)S(1)}, u32[]{:S(2)}, u32[]{:S(2)}) collective-permute-start(bf16[2,1152,256]{2,1,0:T(8,128)(2,1)} %get-tuple-element.96), channel_id=1, source_target_pairs={{0,6},{2,4},{4,2},{6,0},{1,7},{3,5},{5,3},{7,1}} | collective-permute-start | bytes 3538952 | tf_op jit(solution)/shard_map/ppermute | solution.py:294
  1312.3 45.0 %collective-permute-start.12 = (bf16[1152,512]{1,0:T(8,128)(2,1)S(1)}, bf16[1152,512]{1,0:T(8,128)(2,1)S(1)}, u32[]{:S(2)}, u32[]{:S(2)}) collective-permute-start(bf16[1152,512]{1,0:T(8,128)(2,1)S(1)} %get-tuple-element.105), channel_id=1, source_target_pairs={{0,2},{2,0},{4,6},{6,4},{1,3},{3,1},{5,7},{7,5}} | collective-permute-start | bytes 3538952 | tf_op jit(solution)/shard_map/ppermute | solution.py:294
  1312.9 44.6 %collective-permute-start.13 = (bf16[1152,512]{1,0:T(8,128)(2,1)S(1)}, bf16[1152,512]{1,0:T(8,128)(2,1)S(1)}, u32[]{:S(2)}, u32[]{:S(2)}) collective-permute-start(bf16[1152,512]{1,0:T(8,128)(2,1)S(1)} %get-tuple-element.104), channel_id=1, source_target_pairs={{0,4},{2,6},{4,0},{6,2},{1,5},{3,7},{5,1},{7,3}} | collective-permute-start | bytes 3538952 | tf_op jit(solution)/shard_map/ppermute | solution.py:294
  1313.7 90.5 %slice-start.2 = ((s8[4718592]{0:T(1024)(128)(4,1)}), s8[4194304]{0:T(1024)(128)(4,1)S(1)}, s32[]{:S(2)}) async-start(s8[4718592]{0:T(1024)(128)(4,1)} %bitcast.182), calls=%async_computation.20 | async-start | bytes 8388608
  1313.7 90.5 %slice-start.3 = ((s8[4718592]{0:T(1024)(128)(4,1)}), s8[524288]{0:T(1024)(128)(4,1)S(1)}, s32[]{:S(2)}) async-start(s8[4718592]{0:T(1024)(128)(4,1)} %bitcast.182), calls=%async_computation.21 | async-start | bytes 1048576
  1313.7 90.4 %collective-permute-start.14 = (bf16[1152,512]{1,0:T(8,128)(2,1)S(1)}, bf16[1152,512]{1,0:T(8,128)(2,1)S(1)}, u32[]{:S(2)}, u32[]{:S(2)}) collective-permute-start(bf16[1152,512]{1,0:T(8,128)(2,1)S(1)} %get-tuple-element.103), channel_id=1, source_target_pairs={{0,6},{2,4},{4,2},{6,0},{1,7},{3,5},{5,3},{7,1}} | collective-permute-start | bytes 3538952 | tf_op jit(solution)/shard_map/ppermute | solution.py:294
  1328.5 186.1 %collective-permute-start.26 = (f32[256,2560]{1,0:T(8,128)}, f32[256,2560]{1,0:T(8,128)S(1)}, u32[]{:S(2)}, u32[]{:S(2)}) collective-permute-start(f32[256,2560]{1,0:T(8,128)} %fusion.125), channel_id=1, source_target_pairs={{0,1},{1,0},{2,3},{3,2},{4,5},{5,4},{6,7},{7,6}} | collective-permute-start | bytes 7864328 | tf_op jit(solution)/shard_map/ppermute | solution.py:320
  1404.3 14.7 copy-start.10
  1404.3 56.7 %slice-start.8 = ((s8[4718592]{0:T(1024)(128)(4,1)}), s8[4194304]{0:T(1024)(128)(4,1)S(1)}, s32[]{:S(2)}) async-start(s8[4718592]{0:T(1024)(128)(4,1)} %bitcast.194), calls=%async_computation.26 | async-start | bytes 8388608
  1405.5 53.2 %collective-permute-start.16 = (bf16[1152,512]{1,0:T(8,128)(2,1)S(1)}, bf16[1152,512]{1,0:T(8,128)(2,1)S(1)}, u32[]{:S(2)}, u32[]{:S(2)}) collective-permute-start(bf16[1152,512]{1,0:T(8,128)(2,1)S(1)} %get-tuple-element.102), channel_id=1, source_target_pairs={{0,2},{2,0},{4,6},{6,4},{1,3},{3,1},{5,7},{7,5}} | collective-permute-start | bytes 3538952 | tf_op jit(solution)/shard_map/ppermute | solution.py:294
  1406.1 54.9 %slice-start = ((s8[5898240]{0:T(1024)(128)(4,1)}), s8[4194304]{0:T(1024)(128)(4,1)S(1)}, s32[]{:S(2)}) async-start(s8[5898240]{0:T(1024)(128)(4,1)} %bitcast.174), calls=%async_computation.18 | async-start | bytes 8388608
  1406.1 54.9 %slice-start.1 = ((s8[5898240]{0:T(1024)(128)(4,1)}), s8[1703936]{0:T(1024)(128)(4,1)S(1)}, s32[]{:S(2)}) async-start(s8[5898240]{0:T(1024)(128)(4,1)} %bitcast.174), calls=%async_computation.19 | async-start | bytes 3407872
  1406.1 54.9 %slice-start.9 = ((s8[4718592]{0:T(1024)(128)(4,1)}), s8[524288]{0:T(1024)(128)(4,1)S(1)}, s32[]{:S(2)}) async-start(s8[4718592]{0:T(1024)(128)(4,1)} %bitcast.194), calls=%async_computation.27 | async-start | bytes 1048576
  1406.1 53.8 %collective-permute-start.17 = (bf16[1152,512]{1,0:T(8,128)(2,1)S(1)}, bf16[1152,512]{1,0:T(8,128)(2,1)S(1)}, u32[]{:S(2)}, u32[]{:S(2)}) collective-permute-start(bf16[1152,512]{1,0:T(8,128)(2,1)S(1)} %get-tuple-element.101), channel_id=1, source_target_pairs={{0,4},{2,6},{4,0},{6,2},{1,5},{3,7},{5,1},{7,3}} | collective-permute-start | bytes 3538952 | tf_op jit(solution)/shard_map/ppermute | solution.py:294
  1419.0 109.2 %collective-permute-start.15 = (f32[1280,512]{1,0:T(8,128)}, f32[1280,512]{1,0:T(8,128)}, u32[]{:S(2)}, u32[]{:S(2)}) collective-permute-start(f32[1280,512]{1,0:T(8,128)} %fusion.39), channel_id=1, source_target_pairs={{0,1},{1,0},{2,3},{3,2},{4,5},{5,4},{6,7},{7,6}} | collective-permute-start | bytes 7864328 | tf_op jit(solution)/shard_map/ppermute | solution.py:320
  1458.7 41.8 %collective-permute-start.18 = (bf16[1152,512]{1,0:T(8,128)(2,1)}, bf16[1152,512]{1,0:T(8,128)(2,1)}, u32[]{:S(2)}, u32[]{:S(2)}) collective-permute-start(bf16[1152,512]{1,0:T(8,128)(2,1)} %get-tuple-element.100), channel_id=1, source_target_pairs={{0,6},{2,4},{4,2},{6,0},{1,7},{3,5},{5,3},{7,1}} | collective-permute-start | bytes 3538952 | tf_op jit(solution)/shard_map/ppermute | solution.py:294
  1502.9 25.2 %slice-start.6 = ((s8[4718592]{0:T(1024)(128)(4,1)}), s8[4194304]{0:T(1024)(128)(4,1)S(1)}, s32[]{:S(2)}) async-start(s8[4718592]{0:T(1024)(128)(4,1)} %bitcast.192), calls=%async_computation.24 | async-start | bytes 8388608
  1514.7 13.4 copy-start.21
  1514.7 13.5 slice-start.7
  1514.7 48.7 %collective-permute-start.19 = (f32[1280,512]{1,0:T(8,128)}, f32[1280,512]{1,0:T(8,128)}, u32[]{:S(2)}, u32[]{:S(2)}) collective-permute-start(f32[1280,512]{1,0:T(8,128)} %fusion.37), channel_id=1, source_target_pairs={{0,1},{1,0},{2,3},{3,2},{4,5},{5,4},{6,7},{7,6}} | collective-permute-start | bytes 7864328 | tf_op jit(solution)/shard_map/ppermute | solution.py:320
  1628.3 78.8 %copy-start.1 = (bf16[512,2560]{1,0:T(8,128)(2,1)S(1)}, bf16[512,2560]{1,0:T(8,128)(2,1)}, u32[]{:S(2)}) copy-start(bf16[512,2560]{1,0:T(8,128)(2,1)} %param.23) | copy-start | bytes 7864324
  (14 other events, 54.4 us)
Sparse Core Ops, SparseCore 0:
  12.2 102.1 all-gather.28
  116.8 55.7 all-gather.32
  174.9 99.3 all-gather.36
  275.7 32.8 all-gather.30
  310.8 77.1 all-gather.40
  389.3 20.2 all-gather.34
  411.2 35.1 all-gather.38
  447.9 21.0 all-gather.42
  661.0 172.9 all-gather.20
  835.7 77.3 all-gather.22
  916.1 98.3 reduce-scatter.5
  1134.8 214.0 all-gather.24
  1350.6 150.3 all-gather.26
  1503.9 99.3 reduce-scatter.7
  1606.2 97.8 reduce-scatter.3

commit v3 on v2

--- a/solution.py
+++ b/solution.py
@@ -248,14 +248,15 @@
 
         def gather_weight(part):
             over_tp = lax.all_gather(part, 'tp', axis=0, tiled=False)
-            return lax.all_gather(over_tp, 'cp', axis=0, tiled=False)
+            other = lax.ppermute(over_tp, 'cp', [(0, 1), (1, 0)])
+            return jnp.where(cp_rank == 0, over_tp, other), jnp.where(cp_rank == 0, other, over_tp)
 
         def gather_qkv(w_q, w_k, w_v):
             return gather_weight(jnp.where(cp_rank == 0, w_q, jnp.concatenate([w_k, w_v], axis=1)))
 
         def gather_out(w_o):
             part = lax.dynamic_slice_in_dim(w_o, cp_rank * head_dim, head_dim, 0)
-            return gather_weight(part).reshape(2, tp_size * head_dim, d_model)
+            return jnp.stack(gather_weight(part)).reshape(2, tp_size * head_dim, d_model)
 
         def swap(val):
             return lax.ppermute(val, 'tp', [(i, i ^ 1) for i in range(tp_size)])
@@ -306,15 +307,13 @@
                             jnp.zeros((2, batch * block, head_dim), val.dtype))
 
         def to_all(rows):
-            own = lax.dynamic_slice_in_dim(rows, own_at, block, 0)
-            shared = lax.dynamic_slice_in_dim(rows, shared_at, half, 0)
-            shared = lax.all_gather(shared, 'tp', axis=0, tiled=True)
-            own = lax.all_gather(own, 'tp', axis=0, tiled=True)
-            pieces = []
-            for chip in range(tp_size):
-                pair = [own[block * chip:block * (chip + 1)], shared[half * chip:half * (chip + 1)]]
-                pieces += pair[::-1] if chip % 2 else pair
-            return jnp.concatenate(pieces, axis=0).reshape(batch, block, d_model)
+            return lax.all_gather(rows, 'tp', axis=0, tiled=True).reshape(batch, block, d_model)
+
+        def to_all_early(rows):
+            parts = jnp.stack([cols(rows, 0), cols(rows, 1)])
+            parts = lax.all_gather(parts, 'tp', axis=0, tiled=False)
+            pieces = [parts[:, side].reshape(batch, block, d_model // 2) for side in range(2)]
+            return jnp.concatenate(pieces, axis=2)
 
         def cp_sum(part_of):
             sent = lax.ppermute(part_of(1 - cp_rank), 'cp', [(0, 1), (1, 0)])
@@ -367,7 +366,7 @@
         out_b, saved_b = attention(False, kv_b, query_b)
         attn_b = dot_f32('crh,chd->rd', out_b, w_out_b).astype(BF16)
         y_rows = (h_rows.astype(F32) + attn_b.astype(F32)).astype(BF16)
-        out_y = to_all(y_rows)
+        out_y = to_all_early(y_rows)
         gy_rows, _ = lax.optimization_barrier((gy_rows, y_rows))
 
         grad_ob = dot_f32('rd,chd->crh', gy_rows, w_out_b).astype(BF16)

time: 1720 us -> 1720 us (level)
  other arithmetic: 132 us -> 154 us
  waiting for transfers between devices: 698 us -> 677 us
  local copies, waits for them, and re-layouts: 123 us -> 105 us
    reduce_scatter x1, waiting for transfers between devices: 69.6 us -> 0.01 us  [body(): grad_wo_a = lax.psum_scatter(part_o, 'tp', scatter_dimension=0, tiled=True)]
    all_gather x8 -> x2, waiting for transfers between devices: 0.01 us -> 50.3 us  [the longest x1 50.3 us: to_all(): lax.all_gather(rows, 'tp', axis=0, tiled=True)]
    all_gather x4, waiting for transfers between devices: 286 us -> 246 us  [gather_weight(): over_tp = lax.all_gather(part, 'tp', axis=0, tiled=False)]
    unnamed x83 -> x78, local copies, waits for them, and re-layouts: 60.6 us -> 28 us
    ppermute x4, waiting for transfers between devices: 93.7 us -> 117 us  [swap(): return lax.ppermute(val, 'tp', [(i, i ^ 1) for i in range(tp_size)])]
    ppermute x6, waiting for transfers between devices: 13.1 us -> 32.6 us  [cp_sum(): sent = lax.ppermute(part_of(1 - cp_rank), 'cp', [(0, 1), (1, 0)])]
    select_n x0 -> x2, other arithmetic: none -> 18.6 us  [gather_weight(): jnp.where(cp_rank == 0, over_tp, other)]
  transfers between devices with their start and end apart: 42 -> 40, of which waited for: 16 -> 17; matrix products, arithmetic and copies ran while one was open for 34% -> 32% of each run, Pallas kernels for 18% -> 12%
where the time goes in v3:
time: 1720 us; the launch traced here: 1710 us
  waiting for transfers between devices  677 us (39%)
  matrix products  386 us (22%)
  Pallas kernels  304 us (18%)
  other arithmetic  154 us (9%)
  local copies, waits for them, and re-layouts  105 us (6%)
  starting transfers between devices  38 us (2%)
  blocking collectives  24.6 us (1%)
    dot_general x24, matrix products, dot_f32(): return jnp.einsum(spec, lhs, rhs, preferred_element_type=F32)  386 us
    all_gather x4, waiting for transfers between devices, gather_weight(): over_tp = lax.all_gather(part, 'tp', axis=0, tiled=False)  246 us
    ppermute x9, waiting for transfers between devices, exchange(): piece = lax.ppermute(piece, 'tp', [(i, i ^ k) for i in range(tp_size)])  226 us
    pallas_call x4, Pallas kernels, attn_backward(): pl.pallas_call(functools.partial(attn_back_kernel, local, scale), grid_sp...  159 us
    ppermute x4, waiting for transfers between devices, swap(): return lax.ppermute(val, 'tp', [(i, i ^ 1) for i in range(tp_size)])  117 us
    pallas_call x4, Pallas kernels, attn_forward(): pl.pallas_call(functools.partial(attn_kernel, local, scale), grid_spec=pl...  98.3 us
    all_gather x1, waiting for transfers between devices, to_all(): lax.all_gather(rows, 'tp', axis=0, tiled=True)  50.3 us
    pallas_call x4, Pallas kernels, prep_call(): pl.pallas_call(functools.partial(kernel, heads), grid=(rows // TILE, grou...  46.7 us
  transfers between devices with their start and end apart: 40, of which 17 were waited for; matrix products, arithmetic and copies ran while one was open for 32% of the time, Pallas kernels for 12%

profile of v3, /device:TPU:0, one launch (start us, length us, event | category | flops | bytes accessed | tf_op | source)
XLA Modules:
  0.0 1705.9 jit_solution(8805882889699592075)
XLA Ops:
  16.1 98.4 %all-gather.14.cloned.1.call-done = bf16[10240,512]{1,0:T(8,128)(2,1)} async-done(((bf16[2560,512]{1,0:T(8,128)(2,1)}), bf16[10240,512]{1,0:T(8,128)(2,1)}) %all-gather.14.cloned.1.call-update) | async-done | bytes 10485776 | tf_op jit(solution)/shard_map/all_gather | solution.py:250
  119.6 10.8 fusion
  132.6 21.6 %fusion.2 = bf16[6,768,2560]{2,1,0:T(8,128)(2,1)} fusion(bf16[6,768,2560]{2,1,0:T(8,128)(2,1)} %param.15, f32[2560]{0:T(1024)S(1)} %convert_element_type.173, f32[6,768]{1,0:T(8,128)S(1)} %add_rsqrt_fusion), kind=kLoop, calls=%fused_computation.4 | loop fusion | flops 47185920 | bytes 47214592 | tf_op jit(solution)/shard_map/convert_element_type | solution.py:27
  154.2 18.3 %all-gather.16.cloned.1.call-done = bf16[1024,2560]{1,0:T(8,128)(2,1)} async-done(((bf16[256,2560]{1,0:T(8,128)(2,1)}), bf16[1024,2560]{1,0:T(8,128)(2,1)}) %all-gather.16.cloned.1.call-update) | async-done | bytes 5242896 | tf_op jit(solution)/shard_map/all_gather | solution.py:250
  175.7 5.8 constant_dynamic-slice_fusion.4
  181.5 18.5 %fusion.88.src = bf16[4,1152,512]{2,1,0:T(8,128)(2,1)} fusion(bf16[4608,2560]{1,0:T(8,128)(2,1)} %bitcast.176, s32[]{:T(128)S(6)} %select_n.171, bf16[4,2560,512]{2,1,0:T(8,128)(2,1)} %collective-permute-done, bf16[4,2560,512]{2,1,0:T(8,128)(2,1)} %bitcast.205, pred[]{:T(512)S(6)} %eq.4), kind=kOutput, calls=%fused_computation.116 | convolution fusion | flops 12087197696 | bytes 31588356 | tf_op jit(solution)/shard_map/rd,tdh->trh/dot_general | solution.py:45
  200.0 10.3 shard_map.239
  214.0 32.2 %all-gather.20.cloned.1.call-done = bf16[1024,2560]{1,0:T(8,128)(2,1)} async-done(((bf16[256,2560]{1,0:T(8,128)(2,1)}), bf16[1024,2560]{1,0:T(8,128)(2,1)}) %all-gather.20.cloned.1.call-update) | async-done | bytes 5242896 | tf_op jit(solution)/shard_map/all_gather | solution.py:250
  246.2 9.8 broadcast_select_fusion.7
  256.0 97.5 %all-gather.18.cloned.1.call-done = bf16[10240,512]{1,0:T(8,128)(2,1)} async-done(((bf16[2560,512]{1,0:T(8,128)(2,1)}), bf16[10240,512]{1,0:T(8,128)(2,1)}) %all-gather.18.cloned.1.call-update) | async-done | bytes 10485776 | tf_op jit(solution)/shard_map/all_gather | solution.py:250
  370.1 18.4 %fusion.85.src = bf16[4,1152,512]{2,1,0:T(8,128)(2,1)} fusion(bf16[4608,2560]{1,0:T(8,128)(2,1)} %bitcast.177, s32[]{:T(128)S(6)} %select_n.171, bf16[4,2560,512]{2,1,0:T(8,128)(2,1)} %bitcast.206, bf16[4,2560,512]{2,1,0:T(8,128)(2,1)} %collective-permute-done, pred[]{:T(512)S(6)} %eq.4), kind=kOutput, calls=%fused_computation.115 | convolution fusion | flops 12087197696 | bytes 31588356 | tf_op jit(solution)/shard_map/rd,tdh->trh/dot_general | solution.py:45
  388.5 10.5 shard_map.238.q_ref
  399.0 32.5 %attn_fwd.4 = (bf16[2,1152,1024]{2,1,0:T(8,128)(2,1)}, f32[4,4,768]{2,1,0:T(4,128)}) custom-call(s32[4]{0:T(128)} %add_add_fusion.1.meta, bf16[4,1152,512]{2,1,0:T(8,128)(2,1)} %shard_map.238.q_ref, bf16[4,768,512]{2,1,0:T(8,128)(2,1)} %collective-permute-done.3.prev, bf16[4,768,512]{2,1,0:T(8,128)(2,1)} %constant_dynamic-slice_fusion.7.cur), custom_call_target="tpu_custom_call" | custom-call | flops 19327352832 | bytes 18874368 | tf_op jit(solution)/shard_map/attn_fwd/pallas_call | solution.py:178
  431.5 17.8 %attn_fwd.5 = (bf16[2,1152,1024]{2,1,0:T(8,128)(2,1)}, f32[4,4,384]{2,1,0:T(4,128)}) custom-call(s32[4]{0:T(128)} %add_add_fusion.meta, bf16[4,1152,512]{2,1,0:T(8,128)(2,1)} %shard_map.238.q_ref, bf16[4,768,512]{2,1,0:T(8,128)(2,1)} %collective-permute-done.2.prev, bf16[4,768,512]{2,1,0:T(8,128)(2,1)} %fusion.104.cur, ...), custom_call_target="tpu_custom_call", output_to_operand_aliasing={{0}: (4, {})} | custom-call | flops 9663676416 | bytes 9437184 | tf_op jit(solution)/shard_map/attn_fwd/pallas_call | solution.py:178
  449.3 18.8 %fusion.27 = (f32[1152]{0:T(1024)S(1)}, bf16[1152,2560]{1,0:T(8,128)(2,1)S(1)}) fusion(bf16[2,1152,1024]{2,1,0:T(8,128)(2,1)} %get-tuple-element.34, bf16[1,1024,2560]{2,1,0:T(8,128)(2,1)} %bitcast.194, bf16[1,1024,2560]{2,1,0:T(8,128)(2,1)} %bitcast.192, bf16[4608,2560]{1,0:T(8,128)(2,1)} %bitcast.167, s32[]{:T(128)S(6)} %select_n.171), kind=kOutput, calls=%fused_computation.44 | convolution fusion | flops 12108430336 | bytes 27005444 | tf_op jit(solution)/shard_map/crh,chd->rd/dot_general | solution.py:45
  470.7 19.1 %fusion.59 = bf16[4,512,1152]{1,2,0:T(8,128)(2,1)} fusion(bf16[1152,2560]{1,0:T(8,128)(2,1)S(1)} %fusion.24, bf16[4,2560,512]{2,1,0:T(8,128)(2,1)} %collective-permute-done.5, bf16[4,2560,512]{2,1,0:T(8,128)(2,1)} %bitcast.210, pred[]{:T(512)S(6)} %eq.4), kind=kOutput, calls=%fused_computation.93 | convolution fusion | flops 12087197696 | bytes 31588352 | tf_op jit(solution)/shard_map/rd,tdh->trh/dot_general | solution.py:45
  493.3 8.8 broadcast_select_fusion.5
  507.6 16.2 collective-permute-done.6
  532.1 16.9 fusion.91.q_ref
  549.0 30.7 %attn_fwd.6 = (bf16[2,1152,1024]{2,1,0:T(8,128)(2,1)}, f32[4,4,768]{2,1,0:T(4,128)}) custom-call(s32[4]{0:T(128)} %add_add_fusion.1.meta, bf16[4,1152,512]{2,1,0:T(8,128)(2,1)} %fusion.91.q_ref, bf16[4,768,512]{2,1,0:T(8,128)(2,1)} %collective-permute-done.8.prev, bf16[4,768,512]{2,1,0:T(8,128)(2,1)} %copy-done.10), custom_call_target="tpu_custom_call" | custom-call | flops 19327352832 | bytes 18874368 | tf_op jit(solution)/shard_map/attn_fwd/pallas_call | solution.py:178
  579.7 17.4 %attn_fwd.7 = (bf16[2,1152,1024]{2,1,0:T(8,128)(2,1)}, f32[4,4,384]{2,1,0:T(4,128)}) custom-call(s32[4]{0:T(128)} %add_add_fusion.meta, bf16[4,1152,512]{2,1,0:T(8,128)(2,1)} %fusion.91.q_ref, bf16[4,768,512]{2,1,0:T(8,128)(2,1)} %collective-permute-done.7.prev, bf16[4,768,512]{2,1,0:T(8,128)(2,1)} %fusion.102.cur, ...), custom_call_target="tpu_custom_call", output_to_operand_aliasing={{0}: (4, {})} | custom-call | flops 9663676416 | bytes 9437184 | tf_op jit(solution)/shard_map/attn_fwd/pallas_call | solution.py:178
  597.1 20.0 %fusion.28 = bf16[1152,2560]{1,0:T(8,128)(2,1)} fusion(bf16[1152,2560]{1,0:T(8,128)(2,1)} %copy-done.3, bf16[2,1152,1024]{2,1,0:T(8,128)(2,1)} %get-tuple-element.36, bf16[1,1024,2560]{2,1,0:T(8,128)(2,1)} %bitcast.202, bf16[1,1024,2560]{2,1,0:T(8,128)(2,1)} %bitcast.200), kind=kOutput, calls=%fused_computation.45 | convolution fusion | flops 12099584000 | bytes 27000832 | tf_op jit(solution)/shard_map/crh,chd->rd/dot_general | solution.py:45
  617.1 16.8 fusion.79.g_ref
  633.9 26.3 %attn_bwd.4 = (bf16[4,1152,512]{2,1,0:T(8,128)(2,1)}, bf16[4,768,512]{2,1,0:T(8,128)(2,1)}, f32[4,768,512]{2,1,0:T(8,128)}) custom-call(s32[4]{0:T(128)} %add_add_fusion.meta, bf16[4,1152,512]{2,1,0:T(8,128)(2,1)} %fusion.91.q_ref, bf16[4,768,512]{2,1,0:T(8,128)(2,1)} %collective-permute-done.7.prev, bf16[4,768,512]{2,1,0:T(8,128)(2,1)} %fusion.102.cur, ...), custom_call_target="tpu_custom_call" | custom-call | flops 24159191040 | bytes 15728640 | tf_op jit(solution)/shard_map/attn_bwd/pallas_call | solution.py:198
  660.2 52.2 %attn_bwd.5 = (bf16[4,1152,512]{2,1,0:T(8,128)(2,1)}, bf16[4,768,512]{2,1,0:T(8,128)(2,1)}, f32[4,768,512]{2,1,0:T(8,128)}) custom-call(s32[4]{0:T(128)} %add_add_fusion.1.meta, bf16[4,1152,512]{2,1,0:T(8,128)(2,1)} %fusion.91.q_ref, bf16[4,768,512]{2,1,0:T(8,128)(2,1)} %collective-permute-done.8.prev, ...), custom_call_target="tpu_custom_call", output_to_operand_aliasing={{0}: (7, {})} | custom-call | flops 48318382080 | bytes 31457280 | tf_op jit(solution)/shard_map/attn_bwd/pallas_call | solution.py:198
  712.4 12.2 fusion.113
  724.6 16.5 collective-permute-done.25
  741.1 14.0 convolution_add_fusion.1
  781.4 64.1 %collective-permute-done.11 = bf16[4,384,512]{2,1,0:T(8,128)(2,1)S(1)} collective-permute-done((bf16[4,384,512]{2,1,0:T(8,128)(2,1)S(1)}, bf16[4,384,512]{2,1,0:T(8,128)(2,1)S(1)}, u32[]{:S(2)}, u32[]{:S(2)}) %collective-permute-start.11) | collective-permute-done | bytes 1572896 | tf_op jit(solution)/shard_map/ppermute | solution.py:262
  851.4 9.6 fusion.111
  861.0 19.6 %convolution_bitcast_fusion.2 = f32[1152,2560]{1,0:T(8,128)} fusion(bf16[4,1152,512]{2,1,0:T(8,128)(2,1)} %copy-done.8, bf16[4,2560,512]{2,1,0:T(8,128)(2,1)} %collective-permute-done.5, bf16[4,2560,512]{2,1,0:T(8,128)(2,1)} %bitcast.212, pred[]{:T(512)S(6)} %eq.4), kind=kOutput, calls=%fused_computation.26 | convolution fusion | flops 12084838400 | bytes 37486592 | tf_op jit(solution)/shard_map/trh,tdh->rd/dot_general | solution.py:45
  880.7 14.7 convolution_add_fusion
  896.2 27.4 %fusion.26 = (f32[2560]{0:T(1024)}, f32[1152]{0:T(1024)S(1)}, bf16[1152,2560]{1,0:T(8,128)(2,1)}) fusion(bf16[1152,2560]{1,0:T(8,128)(2,1)} %copy-done.3, f32[1152]{0:T(1024)S(1)} %copy-done.19, f32[2560]{0:T(1024)S(1)} %copy-done.17, f32[1152,2560]{1,0:T(8,128)} %convolution_bitcast_fusion.2, bf16[4,1152,512]{2,1,0:T(8,128)(2,1)} %get-tuple-element.41, ...), kind=kOutput, calls=%fused_computation.43 | convolution fusion | flops 12114326528 | bytes 49312768 | tf_op jit(solution)/shard_map/trh,tdh->rd/dot_general | solution.py:45
  923.6 8.7 fusion.19
  932.3 11.9 fusion.124
  945.5 16.1 collective-permute-done.24
  961.6 14.9 convolution_add_fusion.2
  976.6 18.4 %fusion.82.g_ref = bf16[2,1152,1024]{2,1,0:T(8,128)(2,1)} fusion(bf16[1152,2560]{1,0:T(8,128)(2,1)} %copy-done.2, bf16[1,1024,2560]{2,1,0:T(8,128)(2,1)} %bitcast.195, bf16[1,1024,2560]{2,1,0:T(8,128)(2,1)} %bitcast.193), kind=kOutput, calls=%fused_computation.114 | convolution fusion | flops 12087197696 | bytes 21102592 | tf_op jit(solution)/shard_map/rd,chd->crh/dot_general | solution.py:45
  995.6 27.0 %attn_bwd.6 = (bf16[4,1152,512]{2,1,0:T(8,128)(2,1)}, bf16[4,768,512]{2,1,0:T(8,128)(2,1)}, f32[4,768,512]{2,1,0:T(8,128)}) custom-call(s32[4]{0:T(128)} %add_add_fusion.meta, bf16[4,1152,512]{2,1,0:T(8,128)(2,1)} %shard_map.238.q_ref, bf16[4,768,512]{2,1,0:T(8,128)(2,1)} %collective-permute-done.2.prev, bf16[4,768,512]{2,1,0:T(8,128)(2,1)} %fusion.104.cur, ...), custom_call_target="tpu_custom_call" | custom-call | flops 24159191040 | bytes 15728640 | tf_op jit(solution)/shard_map/attn_bwd/pallas_call | solution.py:198
  1023.9 53.8 %attn_bwd.7 = (bf16[4,1152,512]{2,1,0:T(8,128)(2,1)}, bf16[4,768,512]{2,1,0:T(8,128)(2,1)}, f32[4,768,512]{2,1,0:T(8,128)}) custom-call(s32[4]{0:T(128)} %add_add_fusion.1.meta, bf16[4,1152,512]{2,1,0:T(8,128)(2,1)} %shard_map.238.q_ref, bf16[4,768,512]{2,1,0:T(8,128)(2,1)} %collective-permute-done.3.prev, ...), custom_call_target="tpu_custom_call", output_to_operand_aliasing={{0}: (7, {})} | custom-call | flops 48318382080 | bytes 31457280 | tf_op jit(solution)/shard_map/attn_bwd/pallas_call | solution.py:198
  1092.8 13.3 shard_map.240
  1111.2 36.7 %collective-permute-done.14 = bf16[4,384,512]{2,1,0:T(8,128)(2,1)} collective-permute-done((bf16[4,384,512]{2,1,0:T(8,128)(2,1)S(1)}, bf16[4,384,512]{2,1,0:T(8,128)(2,1)}, u32[]{:S(2)}, u32[]{:S(2)}) %collective-permute-start.14) | collective-permute-done | bytes 1572896 | tf_op jit(solution)/shard_map/ppermute | solution.py:262
  1150.0 6.5 fusion.76.grad
  1156.5 12.5 shard_map.241
  1169.0 19.5 %convolution_bitcast_fusion = f32[1152,2560]{1,0:T(8,128)} fusion(bf16[4,1152,512]{2,1,0:T(8,128)(2,1)} %shard_map.241, bf16[4,2560,512]{2,1,0:T(8,128)(2,1)} %collective-permute-done, bf16[4,2560,512]{2,1,0:T(8,128)(2,1)} %bitcast.207, pred[]{:T(512)S(6)} %eq.4), kind=kOutput, calls=%fused_computation.23 | convolution fusion | flops 12084838400 | bytes 37486592 | tf_op jit(solution)/shard_map/trh,tdh->rd/dot_general | solution.py:45
  1188.5 25.0 %fusion.21 = (f32[2560]{0:T(1024)S(1)}, f32[1152]{0:T(1024)S(1)}, bf16[1152,2560]{1,0:T(8,128)(2,1)}) fusion(f32[1152]{0:T(1024)S(1)} %add_rsqrt_fusion.1, bf16[4608,2560]{1,0:T(8,128)(2,1)} %bitcast.169, s32[]{:T(128)S(6)} %select_n.171, f32[2560]{0:T(1024)S(1)} %copy-done.15, f32[1152,2560]{1,0:T(8,128)} %convolution_bitcast_fusion, ...), kind=kOutput, calls=%fused_computation.38 | convolution fusion | flops 12114326528 | bytes 49312772 | tf_op jit(solution)/shard_map/trh,tdh->rd/dot_general | solution.py:45
  1213.5 11.6 fusion.16
  1235.9 50.5 %collective-permute-done.27 = bf16[2,1152,256]{2,1,0:T(8,128)(2,1)} collective-permute-done((bf16[2,1152,256]{2,1,0:T(8,128)(2,1)}, bf16[2,1152,256]{2,1,0:T(8,128)(2,1)}, u32[]{:S(2)}, u32[]{:S(2)}) %collective-permute-start.27) | collective-permute-done | bytes 1179680 | tf_op jit(solution)/shard_map/ppermute | solution.py:295
  1290.0 47.7 %collective-permute-done.29 = bf16[2,1152,256]{2,1,0:T(8,128)(2,1)S(1)} collective-permute-done((bf16[2,1152,256]{2,1,0:T(8,128)(2,1)}, bf16[2,1152,256]{2,1,0:T(8,128)(2,1)S(1)}, u32[]{:S(2)}, u32[]{:S(2)}) %collective-permute-start.29) | collective-permute-done | bytes 1179680 | tf_op jit(solution)/shard_map/ppermute | solution.py:295
  1346.3 12.4 fusion.121
  1364.4 32.7 %collective-permute-done.16 = bf16[1152,512]{1,0:T(8,128)(2,1)} collective-permute-done((bf16[1152,512]{1,0:T(8,128)(2,1)}, bf16[1152,512]{1,0:T(8,128)(2,1)}, u32[]{:S(2)}, u32[]{:S(2)}) %collective-permute-start.16) | collective-permute-done | bytes 1179680 | tf_op jit(solution)/shard_map/ppermute | solution.py:295
  1401.8 22.5 %collective-permute-done.18 = bf16[1152,512]{1,0:T(8,128)(2,1)S(1)} collective-permute-done((bf16[1152,512]{1,0:T(8,128)(2,1)}, bf16[1152,512]{1,0:T(8,128)(2,1)S(1)}, u32[]{:S(2)}, u32[]{:S(2)}) %collective-permute-start.18) | collective-permute-done | bytes 1179680 | tf_op jit(solution)/shard_map/ppermute | solution.py:295
  1432.8 10.2 fusion.35
  1447.9 28.1 %collective-permute-done.20 = bf16[1152,512]{1,0:T(8,128)(2,1)} collective-permute-done((bf16[1152,512]{1,0:T(8,128)(2,1)}, bf16[1152,512]{1,0:T(8,128)(2,1)}, u32[]{:S(2)}, u32[]{:S(2)}) %collective-permute-start.20) | collective-permute-done | bytes 1179680 | tf_op jit(solution)/shard_map/ppermute | solution.py:295
  1480.8 43.9 %collective-permute-done.22 = bf16[1152,512]{1,0:T(8,128)(2,1)S(1)} collective-permute-done((bf16[1152,512]{1,0:T(8,128)(2,1)}, bf16[1152,512]{1,0:T(8,128)(2,1)S(1)}, u32[]{:S(2)}, u32[]{:S(2)}) %collective-permute-start.22) | collective-permute-done | bytes 1179680 | tf_op jit(solution)/shard_map/ppermute | solution.py:295
  1525.8 9.3 fusion.33
  1535.2 12.5 fusion.94
  1547.7 15.3 fusion.108
  1563.1 24.6 %psum.7 = bf16[2,2560]{1,0:T(2,128)(2,1)S(1)} all-reduce(f32[2,2560]{1,0:T(2,128)S(1)} %pad_maximum_fusion.16), channel_id=1, replica_groups=mesh['tp'=4,'cp'=2] {'tp','cp'}, use_global_device_ids=true, to_apply=%region_7.8 | all-reduce | flops 5120 | bytes 30720 | tf_op jit(solution)/shard_map/psum | solution.py:406
  1588.3 10.9 fusion.105
  1603.8 8.9 fusion.161
  1612.6 9.1 pad_maximum_fusion
  1628.8 50.3 %all-gather.12.cloned.1.call-done = bf16[4608,2560]{1,0:T(8,128)(2,1)} async-done(((bf16[1152,2560]{1,0:T(8,128)(2,1)}), bf16[4608,2560]{1,0:T(8,128)(2,1)}) %all-gather.12.cloned.1.call-update) | async-done | bytes 23592976 | tf_op jit(solution)/shard_map/all_gather | solution.py:310
  1679.1 19.8 %copy.96 = bf16[6,768,2560]{2,1,0:T(8,128)(2,1)} copy(bf16[6,768,2560]{2,1,0:T(8,128)(2,1)} %bitcast.185) | data formatting | bytes 47185920
  (221 shorter events, 181.5 us)
Async XLA Ops:
  7.2 107.2 %all-gather.14.cloned.1.call-start = ((), (), s32[]{:S(2)}) async-start(), calls=%async_computation.7 | async-start | bytes 13107200 | tf_op jit(solution)/shard_map/all_gather | solution.py:250
  12.1 160.4 %all-gather.16.cloned.1.call-start = ((), (), s32[]{:S(2)}) async-start(), calls=%async_computation.8 | async-start | bytes 6553600 | tf_op jit(solution)/shard_map/all_gather | solution.py:250
  13.3 101.1 %copy-start.11 = (bf16[2560,512]{1,0:T(8,128)(2,1)S(1)}, bf16[2560,512]{1,0:T(8,128)(2,1)}, u32[]{:S(2)}) copy-start(bf16[2560,512]{1,0:T(8,128)(2,1)} %param.25) | copy-start | bytes 7864324
  13.3 232.8 %all-gather.20.cloned.1.call-start = ((), (), s32[]{:S(2)}) async-start(), calls=%async_computation.10 | async-start | bytes 6553600 | tf_op jit(solution)/shard_map/all_gather | solution.py:250
  16.0 337.4 %all-gather.18.cloned.1.call-start = ((), (), s32[]{:S(2)}) async-start(), calls=%async_computation.9 | async-start | bytes 13107200 | tf_op jit(solution)/shard_map/all_gather | solution.py:250
  114.4 67.1 %collective-permute-start = (bf16[4,2560,512]{2,1,0:T(8,128)(2,1)}, bf16[4,2560,512]{2,1,0:T(8,128)(2,1)}, u32[]{:S(2)}, u32[]{:S(2)}) collective-permute-start(bf16[4,2560,512]{2,1,0:T(8,128)(2,1)} %bitcast.204), channel_id=1, source_target_pairs={{0,1},{1,0},{2,3},{3,2},{4,5},{5,4},{6,7},{7,6}} | collective-permute-start | bytes 31457288 | tf_op jit(solution)/shard_map/ppermute | solution.py:251
  118.4 1482.0 %reduce-scatter.6.cloned.1.call-start = ((), (), s32[]{:S(2)}) async-start(), calls=%async_computation.5 | async-start | bytes 13107200 | tf_op jit(solution)/shard_map/reduce_scatter | solution.py:381
  118.5 14.0 copy-start.14
  132.5 40.0 %copy-start.26 = (s32[768]{0:T(1024)S(1)}, s32[768]{0:T(1024)}, u32[]{:S(2)}) copy-start(s32[768]{0:T(1024)} %param.16) | copy-start | bytes 9220
  132.5 40.5 %copy-start.25 = (bf16[2560]{0:T(1024)(128)(2,1)S(1)}, bf16[2560]{0:T(1024)(128)(2,1)}, u32[]{:S(2)}) copy-start(bf16[2560]{0:T(1024)(128)(2,1)} %param.24) | copy-start | bytes 15364
  172.5 73.6 %collective-permute-start.4 = (bf16[4,256,2560]{2,1,0:T(8,128)(2,1)}, bf16[4,256,2560]{2,1,0:T(8,128)(2,1)}, u32[]{:S(2)}, u32[]{:S(2)}) collective-permute-start(bf16[4,256,2560]{2,1,0:T(8,128)(2,1)} %bitcast.198), channel_id=1, source_target_pairs={{0,1},{1,0},{2,3},{3,2},{4,5},{5,4},{6,7},{7,6}} | collective-permute-start | bytes 15728648 | tf_op jit(solution)/shard_map/ppermute | solution.py:251
  211.8 150.0 %collective-permute-start.1 = (bf16[4,384,512]{2,1,0:T(8,128)(2,1)S(1)}, bf16[4,384,512]{2,1,0:T(8,128)(2,1)}, u32[]{:S(2)}, u32[]{:S(2)}) collective-permute-start(bf16[4,384,512]{2,1,0:T(8,128)(2,1)S(1)} %constant_dynamic-slice_fusion.8), channel_id=1, source_target_pairs={{0,2},{2,0},{4,6},{6,4},{1,3},{3,1},{5,7},{7,5}} | collective-permute-start | bytes 4718600 | tf_op jit(solution)/shard_map/ppermute | solution.py:262
  246.2 247.1 %collective-permute-start.9 = (bf16[4,256,2560]{2,1,0:T(8,128)(2,1)}, bf16[4,256,2560]{2,1,0:T(8,128)(2,1)}, u32[]{:S(2)}, u32[]{:S(2)}) collective-permute-start(bf16[4,256,2560]{2,1,0:T(8,128)(2,1)} %bitcast.196), channel_id=1, source_target_pairs={{0,1},{1,0},{2,3},{3,2},{4,5},{5,4},{6,7},{7,6}} | collective-permute-start | bytes 15728648 | tf_op jit(solution)/shard_map/ppermute | solution.py:251
  353.5 117.2 %collective-permute-start.5 = (bf16[4,2560,512]{2,1,0:T(8,128)(2,1)}, bf16[4,2560,512]{2,1,0:T(8,128)(2,1)}, u32[]{:S(2)}, u32[]{:S(2)}) collective-permute-start(bf16[4,2560,512]{2,1,0:T(8,128)(2,1)} %bitcast.209), channel_id=1, source_target_pairs={{0,1},{1,0},{2,3},{3,2},{4,5},{5,4},{6,7},{7,6}} | collective-permute-start | bytes 31457288 | tf_op jit(solution)/shard_map/ppermute | solution.py:251
  357.3 41.7 %collective-permute-start.3 = (bf16[4,768,512]{2,1,0:T(8,128)(2,1)}, bf16[4,768,512]{2,1,0:T(8,128)(2,1)}, u32[]{:S(2)}, u32[]{:S(2)}) collective-permute-start(bf16[4,768,512]{2,1,0:T(8,128)(2,1)} %constant_dynamic-slice_fusion.7.cur), channel_id=1, source_target_pairs={{0,1},{2,3},{4,5},{6,7}} | collective-permute-start | bytes 9437192 | tf_op jit(solution)/shard_map/ppermute | solution.py:268
  367.1 64.3 %collective-permute-start.2 = (bf16[4,768,512]{2,1,0:T(8,128)(2,1)}, bf16[4,768,512]{2,1,0:T(8,128)(2,1)}, u32[]{:S(2)}, u32[]{:S(2)}) collective-permute-start(bf16[4,768,512]{2,1,0:T(8,128)(2,1)} %fusion.104.cur), channel_id=1, source_target_pairs={{0,1},{2,3},{4,5},{6,7}} | collective-permute-start | bytes 9437192 | tf_op jit(solution)/shard_map/ppermute | solution.py:272
  449.3 18.9 %copy-start.16 = (f32[2560]{0:T(1024)S(1)}, f32[2560]{0:T(1024)}, u32[]{:S(2)}) copy-start(f32[2560]{0:T(1024)} %convert_element_type.183) | copy-start | bytes 30724
  470.7 19.1 %copy-start.6 = (bf16[1152,2560]{1,0:T(8,128)(2,1)}, bf16[1152,2560]{1,0:T(8,128)(2,1)S(1)}, u32[]{:S(2)}) copy-start(bf16[1152,2560]{1,0:T(8,128)(2,1)S(1)} %fusion.24) | copy-start | bytes 17694724
  470.7 21.9 %copy-start.21 = (f32[768]{0:T(1024)S(1)}, f32[768]{0:T(1024)}, u32[]{:S(2)}) copy-start(f32[768]{0:T(1024)} %copy-done.20) | copy-start | bytes 9220
  470.7 21.9 %copy-start.23 = (f32[384]{0:T(512)S(1)}, f32[384]{0:T(512)}, u32[]{:S(2)}) copy-start(f32[384]{0:T(512)} %dynamic_slice.155) | copy-start | bytes 4612
  491.3 32.5 %collective-permute-start.6 = (bf16[4,384,512]{2,1,0:T(8,128)(2,1)S(1)}, bf16[4,384,512]{2,1,0:T(8,128)(2,1)}, u32[]{:S(2)}, u32[]{:S(2)}) collective-permute-start(bf16[4,384,512]{2,1,0:T(8,128)(2,1)S(1)} %dynamic-slice_bitcast_fusion.1), channel_id=1, source_target_pairs={{0,2},{2,0},{4,6},{6,4},{1,3},{3,1},{5,7},{7,5}} | collective-permute-start | bytes 4718600 | tf_op jit(solution)/shard_map/ppermute | solution.py:262
  502.1 30.0 %copy-start.7 = (bf16[1152,2560]{1,0:T(8,128)(2,1)S(1)}, bf16[1152,2560]{1,0:T(8,128)(2,1)}, u32[]{:S(2)}) copy-start(bf16[1152,2560]{1,0:T(8,128)(2,1)} %copy-done.6) | copy-start | bytes 17694724
  504.4 44.6 %copy-start.10 = (bf16[4,768,512]{2,1,0:T(8,128)(2,1)}, bf16[4,768,512]{2,1,0:T(8,128)(2,1)S(1)}, u32[]{:S(2)}) copy-start(bf16[4,768,512]{2,1,0:T(8,128)(2,1)S(1)} %dynamic-slice_bitcast_fusion.cur) | copy-start | bytes 9437188
  504.4 44.6 %collective-permute-start.8 = (bf16[4,768,512]{2,1,0:T(8,128)(2,1)S(1)}, bf16[4,768,512]{2,1,0:T(8,128)(2,1)}, u32[]{:S(2)}, u32[]{:S(2)}) collective-permute-start(bf16[4,768,512]{2,1,0:T(8,128)(2,1)S(1)} %dynamic-slice_bitcast_fusion.cur), channel_id=1, source_target_pairs={{0,1},{2,3},{4,5},{6,7}} | collective-permute-start | bytes 9437192 | tf_op jit(solution)/shard_map/ppermute | solution.py:268
  529.2 50.5 %collective-permute-start.7 = (bf16[4,768,512]{2,1,0:T(8,128)(2,1)}, bf16[4,768,512]{2,1,0:T(8,128)(2,1)}, u32[]{:S(2)}, u32[]{:S(2)}) collective-permute-start(bf16[4,768,512]{2,1,0:T(8,128)(2,1)} %fusion.102.cur), channel_id=1, source_target_pairs={{0,1},{2,3},{4,5},{6,7}} | collective-permute-start | bytes 9437192 | tf_op jit(solution)/shard_map/ppermute | solution.py:272
  579.7 37.4 %slice-start.6 = ((s8[5898240]{0:T(1024)(128)(4,1)}), s8[1703936]{0:T(1024)(128)(4,1)S(1)}, s32[]{:S(2)}) async-start(s8[5898240]{0:T(1024)(128)(4,1)} %bitcast.186), calls=%async_computation.18 | async-start | bytes 3407872
  597.1 20.0 %slice-start.7 = ((s8[5898240]{0:T(1024)(128)(4,1)}), s8[4194304]{0:T(1024)(128)(4,1)S(1)}, s32[]{:S(2)}) async-start(s8[5898240]{0:T(1024)(128)(4,1)} %bitcast.186), calls=%async_computation.19 | async-start | bytes 8388608
  724.6 16.5 collective-permute-start.25
  755.1 848.7 %all-gather.22.cloned.1.call-start = ((), (), s32[]{:S(2)}) async-start(), calls=%async_computation.11 | async-start | bytes 29491200 | tf_op jit(solution)/shard_map/all_gather | solution.py:314
  761.3 860.4 %reduce-scatter.8.cloned.1.call-start = ((), (), s32[]{:S(2)}) async-start(), calls=%async_computation.6 | async-start | bytes 13107200 | tf_op jit(solution)/shard_map/reduce_scatter | solution.py:381
  761.4 7.9 collective-permute-start.10
  762.7 13.6 collective-permute-start.12
  774.8 70.7 %collective-permute-start.11 = (bf16[4,384,512]{2,1,0:T(8,128)(2,1)S(1)}, bf16[4,384,512]{2,1,0:T(8,128)(2,1)S(1)}, u32[]{:S(2)}, u32[]{:S(2)}) collective-permute-start(bf16[4,384,512]{2,1,0:T(8,128)(2,1)S(1)} %dynamic-slice_convert_fusion.1), channel_id=1, source_target_pairs={{0,2},{2,0},{4,6},{6,4},{1,3},{3,1},{5,7},{7,5}} | collective-permute-start | bytes 4718600 | tf_op jit(solution)/shard_map/ppermute | solution.py:262
  861.0 19.7 %collective-permute-start.26 = (f32[4,512,1280]{2,1,0:T(8,128)}, f32[4,512,1280]{2,1,0:T(8,128)}, u32[]{:S(2)}, u32[]{:S(2)}) collective-permute-start(f32[4,512,1280]{2,1,0:T(8,128)} %fusion.111), channel_id=1, source_target_pairs={{0,1},{1,0},{2,3},{3,2},{4,5},{5,4},{6,7},{7,6}} | collective-permute-start | bytes 31457288 | tf_op jit(solution)/shard_map/ppermute | solution.py:319
  861.0 19.7 %copy-start.9 = (bf16[4,1152,512]{2,1,0:T(8,128)(2,1)S(1)}, bf16[4,1152,512]{2,1,0:T(8,128)(2,1)}, u32[]{:S(2)}) copy-start(bf16[4,1152,512]{2,1,0:T(8,128)(2,1)} %copy-done.8) | copy-start | bytes 14155780
  895.5 730.4 %reduce-scatter.4.cloned.1.call-start = ((), (), s32[]{:S(2)}) async-start(), calls=%async_computation.4 | async-start | bytes 13107200 | tf_op jit(solution)/shard_map/reduce_scatter | solution.py:393
  932.3 12.0 copy-start.2
  944.2 17.4 %collective-permute-start.24 = (f32[1024,2560]{1,0:T(8,128)}, f32[1024,2560]{1,0:T(8,128)}, u32[]{:S(2)}, u32[]{:S(2)}) collective-permute-start(f32[1024,2560]{1,0:T(8,128)} %fusion.124), channel_id=1, source_target_pairs={{0,1},{1,0},{2,3},{3,2},{4,5},{5,4},{6,7},{7,6}} | collective-permute-start | bytes 31457288 | tf_op jit(solution)/shard_map/ppermute | solution.py:319
  976.5 702.6 %all-gather.12.cloned.1.call-start = ((), (), s32[]{:S(2)}) async-start(), calls=%async_computation.3 | async-start | bytes 29491200 | tf_op jit(solution)/shard_map/all_gather | solution.py:310
  1022.6 56.4 %collective-permute-start.13 = (bf16[4,768,512]{2,1,0:T(8,128)(2,1)}, bf16[4,768,512]{2,1,0:T(8,128)(2,1)}, u32[]{:S(2)}, u32[]{:S(2)}) collective-permute-start(bf16[4,768,512]{2,1,0:T(8,128)(2,1)} %get-tuple-element.51), channel_id=1, source_target_pairs={{1,0},{3,2},{5,4},{7,6}} | collective-permute-start | bytes 9437192 | tf_op jit(solution)/shard_map/ppermute | solution.py:279
  1077.8 28.3 %collective-permute-start.15 = (bf16[4,768,512]{2,1,0:T(8,128)(2,1)}, bf16[4,768,512]{2,1,0:T(8,128)(2,1)}, u32[]{:S(2)}, u32[]{:S(2)}) collective-permute-start(bf16[4,768,512]{2,1,0:T(8,128)(2,1)} %get-tuple-element.53), channel_id=1, source_target_pairs={{1,0},{3,2},{5,4},{7,6}} | collective-permute-start | bytes 9437192 | tf_op jit(solution)/shard_map/ppermute | solution.py:286
  1087.0 60.8 %collective-permute-start.14 = (bf16[4,384,512]{2,1,0:T(8,128)(2,1)S(1)}, bf16[4,384,512]{2,1,0:T(8,128)(2,1)}, u32[]{:S(2)}, u32[]{:S(2)}) collective-permute-start(bf16[4,384,512]{2,1,0:T(8,128)(2,1)S(1)} %dynamic-slice_convert_fusion), channel_id=1, source_target_pairs={{0,2},{2,0},{4,6},{6,4},{1,3},{3,1},{5,7},{7,5}} | collective-permute-start | bytes 4718600 | tf_op jit(solution)/shard_map/ppermute | solution.py:262
  1106.1 41.8 %copy-start.5 = (f32[4,768,512]{2,1,0:T(8,128)S(1)}, f32[4,768,512]{2,1,0:T(8,128)}, u32[]{:S(2)}) copy-start(f32[4,768,512]{2,1,0:T(8,128)} %copy-done.4) | copy-start | bytes 18874372
  1169.0 19.5 %copy-start.15 = (f32[2560]{0:T(1024)S(1)}, f32[2560]{0:T(1024)}, u32[]{:S(2)}) copy-start(f32[2560]{0:T(1024)} %copy-done.14) | copy-start | bytes 30724
  1232.5 54.0 %collective-permute-start.27 = (bf16[2,1152,256]{2,1,0:T(8,128)(2,1)}, bf16[2,1152,256]{2,1,0:T(8,128)(2,1)}, u32[]{:S(2)}, u32[]{:S(2)}) collective-permute-start(bf16[2,1152,256]{2,1,0:T(8,128)(2,1)} %get-tuple-element.94), channel_id=1, source_target_pairs={{0,2},{2,0},{4,6},{6,4},{1,3},{3,1},{5,7},{7,5}} | collective-permute-start | bytes 3538952 | tf_op jit(solution)/shard_map/ppermute | solution.py:295
  1232.9 56.0 %collective-permute-start.28 = (bf16[2,1152,256]{2,1,0:T(8,128)(2,1)}, bf16[2,1152,256]{2,1,0:T(8,128)(2,1)S(1)}, u32[]{:S(2)}, u32[]{:S(2)}) collective-permute-start(bf16[2,1152,256]{2,1,0:T(8,128)(2,1)} %get-tuple-element.93), channel_id=1, source_target_pairs={{0,4},{2,6},{4,0},{6,2},{1,5},{3,7},{5,1},{7,3}} | collective-permute-start | bytes 3538952 | tf_op jit(solution)/shard_map/ppermute | solution.py:295
  1234.6 103.1 %collective-permute-start.29 = (bf16[2,1152,256]{2,1,0:T(8,128)(2,1)}, bf16[2,1152,256]{2,1,0:T(8,128)(2,1)S(1)}, u32[]{:S(2)}, u32[]{:S(2)}) collective-permute-start(bf16[2,1152,256]{2,1,0:T(8,128)(2,1)} %get-tuple-element.92), channel_id=1, source_target_pairs={{0,6},{2,4},{4,2},{6,0},{1,7},{3,5},{5,3},{7,1}} | collective-permute-start | bytes 3538952 | tf_op jit(solution)/shard_map/ppermute | solution.py:295
  1342.8 54.3 %collective-permute-start.16 = (bf16[1152,512]{1,0:T(8,128)(2,1)}, bf16[1152,512]{1,0:T(8,128)(2,1)}, u32[]{:S(2)}, u32[]{:S(2)}) collective-permute-start(bf16[1152,512]{1,0:T(8,128)(2,1)} %get-tuple-element.101), channel_id=1, source_target_pairs={{0,2},{2,0},{4,6},{6,4},{1,3},{3,1},{5,7},{7,5}} | collective-permute-start | bytes 3538952 | tf_op jit(solution)/shard_map/ppermute | solution.py:295
  1343.3 56.2 %collective-permute-start.17 = (bf16[1152,512]{1,0:T(8,128)(2,1)}, bf16[1152,512]{1,0:T(8,128)(2,1)}, u32[]{:S(2)}, u32[]{:S(2)}) collective-permute-start(bf16[1152,512]{1,0:T(8,128)(2,1)} %get-tuple-element.100), channel_id=1, source_target_pairs={{0,4},{2,6},{4,0},{6,2},{1,5},{3,7},{5,1},{7,3}} | collective-permute-start | bytes 3538952 | tf_op jit(solution)/shard_map/ppermute | solution.py:295
  1343.5 80.9 %collective-permute-start.18 = (bf16[1152,512]{1,0:T(8,128)(2,1)}, bf16[1152,512]{1,0:T(8,128)(2,1)S(1)}, u32[]{:S(2)}, u32[]{:S(2)}) collective-permute-start(bf16[1152,512]{1,0:T(8,128)(2,1)} %get-tuple-element.99), channel_id=1, source_target_pairs={{0,6},{2,4},{4,2},{6,0},{1,7},{3,5},{5,3},{7,1}} | collective-permute-start | bytes 3538952 | tf_op jit(solution)/shard_map/ppermute | solution.py:295
  1346.3 86.4 %slice-start = ((s8[23592960]{0:T(1024)(128)(4,1)}), s8[2621440]{0:T(1024)(128)(4,1)S(1)}, s32[]{:S(2)}) async-start(s8[23592960]{0:T(1024)(128)(4,1)} %bitcast.180), calls=%async_computation.12 | async-start | bytes 5242880
  1346.3 86.4 %slice-start.1 = ((s8[23592960]{0:T(1024)(128)(4,1)}), s8[4194304]{0:T(1024)(128)(4,1)S(1)}, s32[]{:S(2)}) async-start(s8[23592960]{0:T(1024)(128)(4,1)} %bitcast.180), calls=%async_computation.13 | async-start | bytes 8388608
  1346.3 86.4 %slice-start.2 = ((s8[23592960]{0:T(1024)(128)(4,1)}), s8[4194304]{0:T(1024)(128)(4,1)S(1)}, s32[]{:S(2)}) async-start(s8[23592960]{0:T(1024)(128)(4,1)} %bitcast.180), calls=%async_computation.14 | async-start | bytes 8388608
  1346.3 86.4 %slice-start.3 = ((s8[23592960]{0:T(1024)(128)(4,1)}), s8[4194304]{0:T(1024)(128)(4,1)S(1)}, s32[]{:S(2)}) async-start(s8[23592960]{0:T(1024)(128)(4,1)} %bitcast.180), calls=%async_computation.15 | async-start | bytes 8388608
  1358.7 74.1 %slice-start.4 = ((s8[23592960]{0:T(1024)(128)(4,1)}), s8[4194304]{0:T(1024)(128)(4,1)S(1)}, s32[]{:S(2)}) async-start(s8[23592960]{0:T(1024)(128)(4,1)} %bitcast.180), calls=%async_computation.16 | async-start | bytes 8388608
  1358.7 176.5 %collective-permute-start.30 = (f32[256,2560]{1,0:T(8,128)S(1)}, f32[256,2560]{1,0:T(8,128)S(1)}, u32[]{:S(2)}, u32[]{:S(2)}) collective-permute-start(f32[256,2560]{1,0:T(8,128)S(1)} %fusion.121), channel_id=1, source_target_pairs={{0,1},{1,0},{2,3},{3,2},{4,5},{5,4},{6,7},{7,6}} | collective-permute-start | bytes 7864328 | tf_op jit(solution)/shard_map/ppermute | solution.py:319
  1401.8 31.0 %slice-start.5 = ((s8[23592960]{0:T(1024)(128)(4,1)}), s8[4194304]{0:T(1024)(128)(4,1)S(1)}, s32[]{:S(2)}) async-start(s8[23592960]{0:T(1024)(128)(4,1)} %bitcast.180), calls=%async_computation.17 | async-start | bytes 8388608
  1429.3 46.8 %collective-permute-start.20 = (bf16[1152,512]{1,0:T(8,128)(2,1)}, bf16[1152,512]{1,0:T(8,128)(2,1)}, u32[]{:S(2)}, u32[]{:S(2)}) collective-permute-start(bf16[1152,512]{1,0:T(8,128)(2,1)} %get-tuple-element.98), channel_id=1, source_target_pairs={{0,2},{2,0},{4,6},{6,4},{1,3},{3,1},{5,7},{7,5}} | collective-permute-start | bytes 3538952 | tf_op jit(solution)/shard_map/ppermute | solution.py:295
  1429.7 48.7 %collective-permute-start.21 = (bf16[1152,512]{1,0:T(8,128)(2,1)}, bf16[1152,512]{1,0:T(8,128)(2,1)}, u32[]{:S(2)}, u32[]{:S(2)}) collective-permute-start(bf16[1152,512]{1,0:T(8,128)(2,1)} %get-tuple-element.97), channel_id=1, source_target_pairs={{0,4},{2,6},{4,0},{6,2},{1,5},{3,7},{5,1},{7,3}} | collective-permute-start | bytes 3538952 | tf_op jit(solution)/shard_map/ppermute | solution.py:295
  1430.2 94.5 %collective-permute-start.22 = (bf16[1152,512]{1,0:T(8,128)(2,1)}, bf16[1152,512]{1,0:T(8,128)(2,1)S(1)}, u32[]{:S(2)}, u32[]{:S(2)}) collective-permute-start(bf16[1152,512]{1,0:T(8,128)(2,1)} %get-tuple-element.96), channel_id=1, source_target_pairs={{0,6},{2,4},{4,2},{6,0},{1,7},{3,5},{5,3},{7,1}} | collective-permute-start | bytes 3538952 | tf_op jit(solution)/shard_map/ppermute | solution.py:295
  1443.0 104.7 %collective-permute-start.19 = (f32[1280,512]{1,0:T(8,128)}, f32[1280,512]{1,0:T(8,128)}, u32[]{:S(2)}, u32[]{:S(2)}) collective-permute-start(f32[1280,512]{1,0:T(8,128)} %fusion.35), channel_id=1, source_target_pairs={{0,1},{1,0},{2,3},{3,2},{4,5},{5,4},{6,7},{7,6}} | collective-permute-start | bytes 7864328 | tf_op jit(solution)/shard_map/ppermute | solution.py:319
  1535.2 12.5 copy-start.22
  1535.2 53.1 %collective-permute-start.23 = (f32[1280,512]{1,0:T(8,128)}, f32[1280,512]{1,0:T(8,128)}, u32[]{:S(2)}, u32[]{:S(2)}) collective-permute-start(f32[1280,512]{1,0:T(8,128)} %fusion.33), channel_id=1, source_target_pairs={{0,1},{1,0},{2,3},{3,2},{4,5},{5,4},{6,7},{7,6}} | collective-permute-start | bytes 7864328 | tf_op jit(solution)/shard_map/ppermute | solution.py:319
  1679.1 19.8 %copy-start.1 = (bf16[512,2560]{1,0:T(8,128)(2,1)S(1)}, bf16[512,2560]{1,0:T(8,128)(2,1)}, u32[]{:S(2)}) copy-start(bf16[512,2560]{1,0:T(8,128)(2,1)} %param.23) | copy-start | bytes 7864324
  (13 other events, 63.9 us)
Sparse Core Ops, SparseCore 0:
  12.2 102.1 all-gather.13
  116.8 55.7 all-gather.15
  174.9 71.2 all-gather.19
  247.8 105.6 all-gather.17
  755.2 131.6 reduce-scatter.5
  888.5 214.8 all-gather.21
  1106.4 116.7 reduce-scatter.7
  1226.2 174.9 reduce-scatter.3
  1403.1 275.9 all-gather.11
